TPU v7x, 8 devices: a whole 2x2x1 slice. The times are simulated.
8 devices in a mesh: dp: 1 (over z), tp: 2 (over y), sp: 4 (over x, core).
Axes of the slice: x: 2, y: 2, z: 1, core: 2. Of those that a mesh axis runs over, the one named last changes fastest.
Arguments:
- x_in: bfloat16 [65536, 1536], P(('dp', 'sp'))
- grad_y: bfloat16 [65536, 1536], P(('dp', 'sp'))
- w_qkv: bfloat16 [1536, 3, 1536], P(None, None, 'tp')
- w_out: bfloat16 [1536, 1536], P('tp')
- ln_gamma: float32 [1536], replicated
- ln_beta: float32 [1536], replicated
- temperature: float32 [48], replicated
Outputs:
- output 1: bfloat16 [65536, 1536], P(('dp', 'sp'))
- output 2: bfloat16 [65536, 1536], P(('dp', 'sp'))
- output 3: float32 [1536, 3, 1536], P(('dp', 'sp'), None, 'tp')
- output 4: float32 [1536, 1536], P(('dp', 'tp', 'sp'))
- output 5: float32 [1536], P('dp')
- output 6: float32 [1536], P('dp')
- output 7: float32 [48], P('dp')
All inputs are finite; a program needn't handle non-finite values.
Results may differ from a plain program's by a relative error of at most 0.001.
Values are sent between devices in bfloat16 or wider.
A program may use at most 1 GiB of HBM per device.

v0:
```python
import jax
import jax.numpy as jnp
from jax import lax
from jax.sharding import PartitionSpec as P

LN_EPS = 1e-6


def layer_norm_fwd(x_rows, ln_gamma, ln_beta):
    x_float = x_rows.astype(jnp.float32)
    centered = x_float - jnp.mean(x_float, axis=-1, keepdims=True)
    inv_std = lax.rsqrt(jnp.mean(centered * centered, axis=-1, keepdims=True) + LN_EPS)
    x_hat = centered * inv_std
    return x_hat, inv_std, (x_hat * ln_gamma + ln_beta).astype(jnp.bfloat16)


def layer_norm_bwd(grad_u, x_hat, inv_std, ln_gamma):
    value_a9 = grad_u * ln_gamma
    return inv_std * (value_a9 - jnp.mean(value_a9, axis=-1, keepdims=True) - x_hat * jnp.mean(value_a9 * x_hat, axis=-1, keepdims=True))


def state_forward(gram_mat, q_sq, k_sq, temp_heads):
    norm_prod = jnp.sqrt(q_sq)[:, :, None] * jnp.sqrt(k_sq)[:, None, :]
    gram_n = gram_mat / norm_prod
    attn_prob = jax.nn.softmax(temp_heads[:, None, None] * gram_n, axis=-1)
    return gram_n, norm_prod, attn_prob


def state_backward(d_attn, attn_prob, gram_n, norm_prod, q_sq, k_sq, temp_heads):
    d_logit = attn_prob * (d_attn - jnp.sum(attn_prob * d_attn, axis=-1, keepdims=True))
    temp_grad = jnp.sum(d_logit * gram_n, axis=(1, 2))
    grad_sn = temp_heads[:, None, None] * d_logit
    d_gram = (grad_sn / norm_prod).astype(jnp.bfloat16)
    prod_sn = grad_sn * gram_n
    q_coef = -jnp.sum(prod_sn, axis=2) / q_sq
    k_coef = -jnp.sum(prod_sn, axis=1) / k_sq
    return d_gram, q_coef, k_coef, temp_grad


def solution(mesh):
    tp_size = mesh.shape["tp"]
    row_spec = P(("dp", "sp"), None)

    def local_step(x_blk, grad_blk, w_qkv, w_out, ln_gamma, ln_beta, value_a11):
        tokens, model_width = x_blk.shape
        local_cols = w_qkv.shape[2]
        heads_loc = value_a11.shape[0] // tp_size
        head_dim = local_cols // heads_loc
        temp_heads = lax.dynamic_slice_in_dim(value_a11, lax.axis_index("tp") * heads_loc, heads_loc)
        x_hat, inv_std, u_act = layer_norm_fwd(x_blk, ln_gamma, ln_beta)
        qkv_act = jnp.einsum("nd,dec->nec", u_act, w_qkv, preferred_element_type=jnp.float32).astype(jnp.bfloat16)
        qkv_heads = qkv_act.reshape(tokens, 3, heads_loc, head_dim)
        q_act = qkv_heads[:, 0]
        k_act = qkv_heads[:, 1]
        v_act = qkv_heads[:, 2]
        gram_part = jnp.einsum("nhi,nhj->hij", q_act, k_act, preferred_element_type=jnp.float32)
        q_part = jnp.einsum("nhi,nhi->hi", q_act, q_act, preferred_element_type=jnp.float32)
        k_part = jnp.einsum("nhj,nhj->hj", k_act, k_act, preferred_element_type=jnp.float32)
        gram_mat, q_sq, k_sq = lax.psum((gram_part, q_part, k_part), "sp")
        gram_n, norm_prod, attn_prob = state_forward(gram_mat, q_sq, k_sq, temp_heads)
        attn_bf = attn_prob.astype(jnp.bfloat16)
        out_act = jnp.einsum("hij,nhj->nhi", attn_bf, v_act, preferred_element_type=jnp.float32).astype(jnp.bfloat16)
        w_out_heads = w_out.reshape(heads_loc, head_dim, model_width)
        y_part = jnp.einsum("nhi,hid->nd", out_act, w_out_heads, preferred_element_type=jnp.float32)
        y_out = (x_blk.astype(jnp.float32) + lax.psum(y_part, "tp")).astype(jnp.bfloat16)
        wout_part = jnp.einsum("nhi,nd->hid", out_act, grad_blk, preferred_element_type=jnp.float32).reshape(local_cols, model_width)
        grad_wout = lax.psum_scatter(wout_part, "sp", scatter_dimension=0, tiled=True)
        dout_act = jnp.einsum("nd,hid->nhi", grad_blk, w_out_heads, preferred_element_type=jnp.float32).astype(jnp.bfloat16)
        d_attn = lax.psum(jnp.einsum("nhi,nhj->hij", dout_act, v_act, preferred_element_type=jnp.float32), "sp")
        dv_act = jnp.einsum("hij,nhi->nhj", attn_bf, dout_act, preferred_element_type=jnp.float32).astype(jnp.bfloat16)
        d_gram, q_coef, k_coef, temp_grad = state_backward(d_attn, attn_prob, gram_n, norm_prod, q_sq, k_sq, temp_heads)
        dq_act = (jnp.einsum("hij,nhj->nhi", d_gram, k_act, preferred_element_type=jnp.float32) + q_act * q_coef).astype(jnp.bfloat16)
        dk_act = (jnp.einsum("hij,nhi->nhj", d_gram, q_act, preferred_element_type=jnp.float32) + k_act * k_coef).astype(jnp.bfloat16)
        dqkv_act = jnp.stack([dq_act, dk_act, dv_act], axis=1).reshape(tokens, 3, local_cols)
        wqkv_part = jnp.einsum("nd,nec->dec", u_act, dqkv_act, preferred_element_type=jnp.float32)
        grad_wqkv = lax.psum_scatter(wqkv_part, "sp", scatter_dimension=0, tiled=True)
        grad_u = lax.psum(jnp.einsum("nec,dec->nd", dqkv_act, w_qkv, preferred_element_type=jnp.float32), "tp")
        grad_gamma, grad_beta = lax.psum((jnp.sum(grad_u * x_hat, axis=0), jnp.sum(grad_u, axis=0)), "sp")
        grad_x = (grad_blk.astype(jnp.float32) + layer_norm_bwd(grad_u, x_hat, inv_std, ln_gamma)).astype(jnp.bfloat16)
        grad_temp = lax.all_gather(temp_grad, "tp", tiled=True)
        return y_out, grad_x, grad_wqkv, grad_wout, grad_gamma, grad_beta, grad_temp

    in_specs = (row_spec, row_spec, P(None, None, "tp"), P("tp", None), P(None), P(None), P(None))
    out_specs = (row_spec, row_spec, P(("dp", "sp"), None, "tp"), P(("dp", "tp", "sp"), None), P("dp"), P("dp"), P("dp"))
    return jax.shard_map(local_step, mesh=mesh, in_specs=in_specs, out_specs=out_specs, check_vma=False)
```

profile of v0, /device:TPU:0, one launch (start us, length us, event | category | flops | bytes accessed | tf_op | source)
XLA Modules:
  0.0 5131.7 jit_solution(11564960795523213179)
XLA Ops:
  7.2 0.0 copy-start
  7.2 0.0 copy-start.15
  7.2 0.0 copy-start.20
  7.2 0.0 all-reduce.12.cloned.1.call-start
  7.3 16.5 convert_reduce_fusion
  23.8 0.0 copy-start.2
  23.8 23.3 fusion.16
  47.1 136.0 %convolution_convert_fusion = bf16[16384,3,768]{0,2,1:T(8,128)(2,1)} fusion(bf16[1536,3,768]{2,0,1:T(8,128)(2,1)} %param.9, bf16[16384,1536]{1,0:T(8,128)(2,1)} %param.7, f32[1536]{0:T(1024)S(1)} %copy-done.20, f32[1536]{0:T(1024)S(1)} %copy-done.15, f32[16384]{0:T(1024)S(1)} %add_rsqrt_fusion, f32[16384]{0:T(1024)S(1)} %broadcast_multiply_fusion.2), kind=kOutput, calls=%fused_computation.38 | convolution fusion | flops 116152860672 | bytes 133050368 | tf_op jit(solution)/shard_map/nd,dec->nec/dot_general | solution.py:51
  183.2 0.0 copy-done.2
  183.2 18.7 fusion.34
  201.9 47.2 fusion.28
  249.1 18.7 fusion.38
  267.8 0.0 all-reduce.12.cloned.1.call-update
  267.8 0.0 all-reduce.10.cloned.1.call-start
  267.9 21.2 fusion.26
  289.1 14.0 all-reduce.2
  303.0 0.0 copy-start.8
  303.1 0.1 dynamic_slice.3
  303.2 5.0 fusion.69
  308.1 22.6 convolution_convert_fusion.2
  330.7 32.6 copy.19
  363.3 0.0 copy-done.12
  363.4 6.8 fusion.56
  370.2 26.2 fusion.20
  396.4 0.0 copy-done.8
  396.4 0.0 copy-done.18
  396.4 31.0 fusion.19
  427.4 32.6 copy.18
  460.0 32.6 copy.17
  492.5 129.0 %convolution_bitcast_fusion = f32[16384,1536]{1,0:T(8,128)} fusion(bf16[1536,3,768]{2,0,1:T(8,128)(2,1)} %param.9, bf16[16384,1,768]{2,0,1:T(8,128)(2,1)} %copy.19, bf16[16384,1,768]{2,0,1:T(8,128)(2,1)} %copy.18, bf16[16384,1,768]{2,0,1:T(8,128)(2,1)} %copy.17), kind=kOutput, calls=%fused_computation.23 | convolution fusion | flops 116039614464 | bytes 183238656 | tf_op jit(solution)/shard_map/nec,dec->nd/dot_general | solution.py:77
  621.5 0.0 copy-start.19
  621.5 0.0 all-reduce.10.cloned.1.call-update
  621.5 0.0 all-reduce.8.cloned.1.call-start
  621.6 0.6 copy-done.9
  622.2 0.0 copy-done.11
  622.2 0.0 copy-done.13
  622.2 0.0 copy-done.19
  622.2 23.6 convolution_convert_fusion.1
  645.9 50.8 convolution_bitcast_fusion.1
  696.7 0.0 copy-start.21
  696.7 0.0 all-reduce.8.cloned.1.call-update
  696.7 0.0 reduce-scatter.5.cloned.1.call-start
  696.8 0.5 copy-done.24
  697.3 0.6 dynamic-slice
  698.6 0.0 copy-start.25
  698.6 33.5 fusion.83
  732.1 0.2 dynamic-update-slice
  732.3 5.5 all-reduce
  737.8 46.5 fusion.21
  784.3 0.0 reduce-scatter.5.cloned.1.call-update
  784.3 0.0 copy-start.4
  784.3 0.0 copy-start.7
  784.3 0.0 copy-start.17
  784.3 0.0 reduce-scatter.3.cloned.1.call-start
  784.4 130.2 %fusion.27 = f32[1536,3,768]{2,0,1:T(8,128)} fusion(bf16[16384,1,768]{2,0,1:T(8,128)(2,1)} %copy.19, bf16[16384,1,768]{2,0,1:T(8,128)(2,1)} %copy.18, bf16[16384,1,768]{2,0,1:T(8,128)(2,1)} %copy.17, bf16[16384,1536,1]{1,0,2:T(8,128)(2,1)} %fusion.83), kind=kOutput, calls=%fused_computation.39 | convolution fusion | flops 116190609408 | bytes 139984896 | tf_op jit(solution)/shard_map/nd,nec->dec/dot_general | solution.py:75
  914.6 0.0 reduce-scatter.3.cloned.1.call-update
  914.6 1881.5 %all-reduce.10.cloned.1.call-done = f32[16384,1536]{1,0:T(8,128)} async-done(((f32[16384,1536]{1,0:T(8,128)}), f32[16384,1536]{1,0:T(8,128)}) %all-reduce.10.cloned.1.call-update) | async-done | bytes 100663312 | tf_op jit(solution)/shard_map/psum | solution.py:77
  2796.1 0.0 copy-done.7
  2796.1 47.1 fusion.15
  2843.2 12.3 all-reduce.1
  2855.5 2119.4 %all-reduce.8.cloned.1.call-done = f32[16384,1536]{1,0:T(8,128)} async-done(((f32[16384,1536]{1,0:T(8,128)}), f32[16384,1536]{1,0:T(8,128)}) %all-reduce.8.cloned.1.call-update) | async-done | bytes 100663312 | tf_op jit(solution)/shard_map/psum | solution.py:65
  4974.9 125.6 %fusion.14 = (bf16[16384,1536]{1,0:T(8,128)(2,1)}, bf16[16384,1536]{1,0:T(8,128)(2,1)}) fusion(bf16[16384,1536]{1,0:T(8,128)(2,1)} %param.7, bf16[16384,1536]{1,0:T(8,128)(2,1)} %param.8, f32[16384,1536]{1,0:T(8,128)} %all-reduce.10.cloned.1.call-done, f32[16384]{0:T(1024)S(1)} %broadcast_multiply_fusion, f32[16384]{0:T(1024)S(1)} %broadcast_multiply_fusion.1, ...), kind=kLoop, calls=%fused_computation.17 | loop fusion | flops 327155712 | bytes 402921472 | tf_op jit(solution)/shard_map/convert_element_type | solution.py:79
  5100.5 24.3 reduce-scatter.3.cloned.1.call-done
  5124.8 0.0 copy-done.1
  (42 shorter events, 0.1 us)
Async XLA Ops:
  7.2 194.7 %copy-start = (bf16[768,1536]{1,0:T(8,128)(2,1)S(1)}, bf16[768,1536]{1,0:T(8,128)(2,1)}, u32[]{:S(2)}) copy-start(bf16[768,1536]{1,0:T(8,128)(2,1)} %param.10) | copy-start | bytes 7077892
  7.2 39.9 copy-start.15
  7.2 39.9 copy-start.20
  7.2 296.0 %all-reduce.12.cloned.1.call-start = ((), (), s32[]{:S(2)}) async-start(), calls=%async_computation.6 | async-start | bytes 1572864 | tf_op jit(solution)/shard_map/psum | solution.py:59
  23.8 159.4 %copy-start.2 = (f32[16384]{0:T(1024)}, f32[16384]{0:T(1024)S(1)}, u32[]{:S(2)}) copy-start(f32[16384]{0:T(1024)S(1)} %broadcast_multiply_fusion.2) | copy-start | bytes 196612
  47.1 136.0 %copy-start.5 = (f32[16384]{0:T(1024)}, f32[16384]{0:T(1024)S(1)}, u32[]{:S(2)}) copy-start(f32[16384]{0:T(1024)S(1)} %add_rsqrt_fusion) | copy-start | bytes 196612
  249.1 54.0 %copy-start.23 = (f32[48]{0:T(128)S(1)}, f32[48]{0:T(128)}, u32[]{:S(2)}) copy-start(f32[48]{0:T(128)} %param.13) | copy-start | bytes 580
  267.8 2528.3 %all-reduce.10.cloned.1.call-start = ((), (), s32[]{:S(2)}) async-start(), calls=%async_computation.3 | async-start | bytes 201326592 | tf_op jit(solution)/shard_map/psum | solution.py:77
  303.0 93.4 %copy-start.8 = (f32[24,32]{1,0:T(8,128)}, f32[24,32]{1,0:T(8,128)S(1)}, u32[]{:S(2)}) copy-start(f32[24,32]{1,0:T(8,128)S(1)} %sqrt.7) | copy-start | bytes 9220
  303.1 93.4 %copy-start.10 = (f32[24,32]{1,0:T(8,128)}, f32[24,32]{1,0:T(8,128)S(1)}, u32[]{:S(2)}) copy-start(f32[24,32]{1,0:T(8,128)S(1)} %sqrt.6) | copy-start | bytes 9220
  303.2 93.3 %copy-start.18 = (f32[24]{0:T(128)}, f32[24]{0:T(128)S(1)}, u32[]{:S(2)}) copy-start(f32[24]{0:T(128)S(1)} %dynamic_slice.3) | copy-start | bytes 292
  308.1 55.2 %copy-start.12 = (f32[24,32]{1,0:T(8,128)}, f32[24,32]{1,0:T(8,128)S(1)}, u32[]{:S(2)}) copy-start(f32[24,32]{1,0:T(8,128)S(1)} %get-tuple-element.24) | copy-start | bytes 9220
  308.1 55.2 %copy-start.14 = (f32[24,32,32]{2,1,0:T(8,128)S(1)}, f32[24,32,32]{2,1,0:T(8,128)}, u32[]{:S(2)}) copy-start(f32[24,32,32]{2,1,0:T(8,128)} %get-tuple-element.20) | copy-start | bytes 294916
  308.1 55.2 %copy-start.22 = (f32[24,32,32]{2,1,0:T(8,128)S(1)}, f32[24,32,32]{2,1,0:T(8,128)}, u32[]{:S(2)}) copy-start(f32[24,32,32]{2,1,0:T(8,128)} %get-tuple-element.21) | copy-start | bytes 294916
  370.2 26.3 copy-start.26
  621.5 0.7 copy-start.9
  621.5 0.7 copy-start.11
  621.5 0.7 copy-start.13
  621.5 0.7 copy-start.19
  621.5 4353.4 %all-reduce.8.cloned.1.call-start = ((), (), s32[]{:S(2)}) async-start(), calls=%async_computation.2 | async-start | bytes 201326592 | tf_op jit(solution)/shard_map/psum | solution.py:65
  696.7 0.7 copy-start.24
  696.7 1.9 copy-start.3
  696.7 1.9 copy-start.6
  696.7 1.9 copy-start.16
  696.7 1.9 copy-start.21
  696.7 4403.8 %reduce-scatter.5.cloned.1.call-start = ((), (), s32[]{:S(2)}) async-start(), calls=%async_computation.5 | async-start | bytes 5898240 | tf_op jit(solution)/shard_map/reduce_scatter | solution.py:67
  698.6 33.5 copy-start.25
  784.3 2011.8 %copy-start.4 = (f32[16384]{0:T(1024)S(1)}, f32[16384]{0:T(1024)}, u32[]{:S(2)}) copy-start(f32[16384]{0:T(1024)} %copy-done.2) | copy-start | bytes 196612
  784.3 2011.8 %copy-start.7 = (f32[16384]{0:T(1024)S(1)}, f32[16384]{0:T(1024)}, u32[]{:S(2)}) copy-start(f32[16384]{0:T(1024)} %copy-done.5) | copy-start | bytes 196612
  784.3 2011.8 %copy-start.17 = (f32[1536]{0:T(1024)S(1)}, f32[1536]{0:T(1024)}, u32[]{:S(2)}) copy-start(f32[1536]{0:T(1024)} %param.11) | copy-start | bytes 18436
  784.3 4340.4 %reduce-scatter.3.cloned.1.call-start = ((), (), s32[]{:S(2)}) async-start(), calls=%async_computation.4 | async-start | bytes 17694720 | tf_op jit(solution)/shard_map/reduce_scatter | solution.py:76
  4974.9 149.9 %copy-start.1 = (bf16[768,1536]{1,0:T(8,128)(2,1)S(1)}, bf16[768,1536]{1,0:T(8,128)(2,1)}, u32[]{:S(2)}) copy-start(bf16[768,1536]{1,0:T(8,128)(2,1)} %param.10) | copy-start | bytes 7077892
Sparse Core Ops, SparseCore 0:
  267.9 32.3 all-reduce.11
  621.7 2174.3 all-reduce.9
  2798.6 2176.3 all-reduce.7
  4977.8 43.7 reduce-scatter.4
  5024.7 100.0 reduce-scatter.2
where the time goes:
time: 5140 us; the launch traced here: 5130 us
  waiting for transfers between devices  4030 us (78%)
  matrix products  680 us (13%)
  other arithmetic  279 us (5%)
  local copies, waits for them, and re-layouts  100 us (2%)
    psum x1, waiting for transfers between devices, local_step(): lax.psum(y_part, 'tp')  2120 us
    psum x1, waiting for transfers between devices, local_step(): lax.psum(jnp.einsum('nec,dec->nd', dqkv_act, w_qkv, preferred_element_typ...  1880 us
    dot_general x1, matrix products, local_step(): jnp.einsum('nd,dec->nec', u_act, w_qkv, preferred_element_type=jnp.float32)  136 us
    dot_general x1, matrix products, local_step(): jnp.einsum('nd,nec->dec', u_act, dqkv_act, preferred_element_type=jnp.flo...  130 us
    dot_general x1, matrix products, local_step(): jnp.einsum('nec,dec->nd', dqkv_act, w_qkv, preferred_element_type=jnp.flo...  129 us
    convert_element_type x1, other arithmetic, local_step(): (grad_blk.astype(jnp.float32) + layer_norm_bwd(grad_u, x_hat, inv_std, ln...  126 us
  transfers between devices with their start and end apart: 5, of which 3 were waited for; matrix products, arithmetic and copies ran while one was open for 9% of the time, Pallas kernels for 0%

commit v1 on v0

v1 whole, which is shorter than its diff:
```python
import jax
import jax.numpy as jnp
from jax import lax
from jax.sharding import PartitionSpec as P

LN_EPS = 1e-6
GROUP = 256
F32 = jnp.float32
BF16 = jnp.bfloat16


def layer_norm_fwd(x_rows, ln_gamma, ln_beta):
    x_float = x_rows.astype(F32)
    centered = x_float - jnp.mean(x_float, axis=-1, keepdims=True)
    inv_std = lax.rsqrt(jnp.mean(centered * centered, axis=-1, keepdims=True) + LN_EPS)
    x_hat = centered * inv_std
    return x_hat, inv_std, (x_hat * ln_gamma + ln_beta).astype(BF16)


def layer_norm_bwd(grad_u, x_hat, inv_std, ln_gamma):
    gh = grad_u * ln_gamma
    return inv_std * (gh - jnp.mean(gh, axis=-1, keepdims=True) - x_hat * jnp.mean(gh * x_hat, axis=-1, keepdims=True))


def state_forward(gram_mat, q_sq, k_sq, temp_heads):
    norm_prod = jnp.sqrt(q_sq)[:, :, None] * jnp.sqrt(k_sq)[:, None, :]
    gram_n = gram_mat / norm_prod
    attn_prob = jax.nn.softmax(temp_heads[:, None, None] * gram_n, axis=-1)
    return gram_n, norm_prod, attn_prob


def state_backward(d_attn, attn_prob, gram_n, norm_prod, q_sq, k_sq, temp_heads):
    d_logit = attn_prob * (d_attn - jnp.sum(attn_prob * d_attn, axis=-1, keepdims=True))
    temp_grad = jnp.sum(d_logit * gram_n, axis=(1, 2))
    grad_sn = temp_heads[:, None, None] * d_logit
    d_gram = (grad_sn / norm_prod).astype(BF16)
    prod_sn = grad_sn * gram_n
    q_coef = -jnp.sum(prod_sn, axis=2) / q_sq
    k_coef = -jnp.sum(prod_sn, axis=1) / k_sq
    return d_gram, q_coef, k_coef, temp_grad


def block_diag(mat):
    heads, dim, _ = mat.shape
    per = GROUP // dim
    m = mat.reshape(heads // per, per, dim, dim)
    eye = jnp.eye(per, dtype=mat.dtype)
    out = m[:, :, :, None, :] * eye[None, :, None, :, None]
    return out.reshape(heads // per, GROUP, GROUP)


def diag_blocks(mat, dim):
    groups = mat.shape[0]
    per = GROUP // dim
    m = mat.reshape(groups, per, dim, per, dim)
    return jnp.stack([m[:, i, :, i, :] for i in range(per)], axis=1).reshape(groups * per, dim, dim)


def mix(act, bd):
    n, cols = act.shape
    out = [jnp.dot(act[:, g * GROUP:(g + 1) * GROUP], bd[g], preferred_element_type=F32) for g in range(cols // GROUP)]
    return jnp.concatenate(out, axis=1)


def gram(lhs, rhs):
    cols = lhs.shape[1]
    sl = lambda t, g: t[:, g * GROUP:(g + 1) * GROUP]
    return jnp.stack([lax.dot_general(sl(lhs, g), sl(rhs, g), (((0,), (0,)), ((), ())), preferred_element_type=F32) for g in range(cols // GROUP)])


def solution(mesh):
    tp_size = mesh.shape["tp"]
    row_spec = P(("dp", "sp"), None)
    swap = [(0, 1), (1, 0)]

    def local_step(x_blk, grad_blk, w_qkv, w_out, ln_gamma, ln_beta, temps):
        tokens, model_width = x_blk.shape
        local_cols = w_qkv.shape[2]
        heads_loc = temps.shape[0] // tp_size
        head_dim = local_cols // heads_loc
        temp_heads = lax.dynamic_slice_in_dim(temps, lax.axis_index("tp") * heads_loc, heads_loc)
        w_far = lax.ppermute(w_qkv, "tp", swap)
        wo_far = lax.ppermute(w_out, "tp", swap)
        x_hat, inv_std, u_act = layer_norm_fwd(x_blk, ln_gamma, ln_beta)

        def project(w3, wo):
            q, k, v = [jnp.dot(u_act, w3[:, e], preferred_element_type=F32).astype(BF16) for e in range(3)]
            do = lax.dot_general(grad_blk, wo, (((1,), (1,)), ((), ())), preferred_element_type=F32).astype(BF16)
            return q, k, v, do

        near = project(w_qkv, w_out)
        q, k, v, do = near
        sq = lambda t: jnp.sum(jnp.square(t.astype(F32)), axis=0).reshape(heads_loc, head_dim)
        gram_mat, d_attn, q_sq, k_sq = lax.psum(
            (diag_blocks(gram(q, k), head_dim), diag_blocks(gram(do, v), head_dim), sq(q), sq(k)), "sp")
        gram_n, norm_prod, attn_prob = state_forward(gram_mat, q_sq, k_sq, temp_heads)
        d_gram, q_coef, k_coef, temp_grad = state_backward(d_attn, attn_prob, gram_n, norm_prod, q_sq, k_sq, temp_heads)
        state = (attn_prob.astype(BF16), d_gram, q_coef, k_coef)
        far_state = lax.ppermute(state, "tp", swap)
        far = project(w_far, wo_far)

        def backward(acts, st):
            q, k, v, do = acts
            attn_bf, d_gram, q_coef, k_coef = st
            tr = lambda m: jnp.swapaxes(m, 1, 2)
            o = mix(v, block_diag(tr(attn_bf))).astype(BF16)
            dv = mix(do, block_diag(attn_bf)).astype(BF16)
            dq = (mix(k, block_diag(tr(d_gram))) + q.astype(F32) * q_coef.reshape(1, -1)).astype(BF16)
            dk = (mix(q, block_diag(d_gram)) + k.astype(F32) * k_coef.reshape(1, -1)).astype(BF16)
            return o, jnp.concatenate([dq, dk, dv], axis=1)

        o_n, r_n = backward(near, state)
        wout_part = lax.dot_general(o_n, grad_blk, (((0,), (0,)), ((), ())), preferred_element_type=F32)
        grad_wout = lax.psum_scatter(wout_part, "sp", scatter_dimension=0, tiled=True)
        wqkv_part = lax.dot_general(u_act, r_n, (((0,), (0,)), ((), ())), preferred_element_type=F32).reshape(model_width, 3, local_cols)
        grad_wqkv = lax.psum_scatter(wqkv_part, "sp", scatter_dimension=0, tiled=True)
        o_f, r_f = backward(far, far_state)
        y_out = (x_blk.astype(F32) + jnp.dot(jnp.concatenate([o_n, o_f], axis=1), jnp.concatenate([w_out, wo_far], axis=0), preferred_element_type=F32)).astype(BF16)
        w_all = jnp.concatenate([w_qkv.reshape(model_width, -1), w_far.reshape(model_width, -1)], axis=1)
        grad_u = lax.dot_general(jnp.concatenate([r_n, r_f], axis=1), w_all, (((1,), (1,)), ((), ())), preferred_element_type=F32)
        grad_gamma, grad_beta = lax.psum((jnp.sum(grad_u * x_hat, axis=0), jnp.sum(grad_u, axis=0)), "sp")
        grad_x = (grad_blk.astype(F32) + layer_norm_bwd(grad_u, x_hat, inv_std, ln_gamma)).astype(BF16)
        grad_temp = lax.all_gather(temp_grad, "tp", tiled=True)
        return y_out, grad_x, grad_wqkv, grad_wout, grad_gamma, grad_beta, grad_temp

    in_specs = (row_spec, row_spec, P(None, None, "tp"), P("tp", None), P(None), P(None), P(None))
    out_specs = (row_spec, row_spec, P(("dp", "sp"), None, "tp"), P(("dp", "tp", "sp"), None), P("dp"), P("dp"), P("dp"))
    return jax.shard_map(local_step, mesh=mesh, in_specs=in_specs, out_specs=out_specs, check_vma=False)
```

time: 5140 us -> 1960 us (0.38)
  waiting for transfers between devices: 4030 us -> 23.2 us
  matrix products: 680 us -> 1270 us
  blocking collectives: 31.8 us -> 214 us
    psum x3 -> x1, waiting for transfers between devices: 4000 us -> 18.2 us  [local_step(): lax.psum((diag_blocks(gram(q, k), head_dim), diag_blocks(gram(do, v), hea...]
    dot_general x12 -> x42, matrix products: 680 us -> 1270 us  [the longest x6 303 us: project(): jnp.dot(u_act, w3[:, e], preferred_element_type=F32).astype(BF16)]
    unnamed x1, blocking collectives: 5.5 us -> 189 us
    unnamed x0 -> x3, other arithmetic: none -> 118 us
    another operation x3 -> x10, local copies, waits for them, and re-layouts: 97.8 us -> 5.52 us  [the longest x8 3.91 us: gram(): jnp.stack([lax.dot_general(sl(lhs, g), sl(rhs, g), (((0,), (0,)), ((), ()...]
    unnamed x57 -> x107, local copies, waits for them, and re-layouts: 2.13 us -> 73.9 us
    dot_general x2 -> x0, other arithmetic: 54.7 us -> none  [the longest x1 33.5 us: local_step(): jnp.einsum('nd,nec->dec', u_act, dqkv_act, preferred_element_type=jnp.flo...]
    convert_element_type x1 -> x3, other arithmetic: 126 us -> 112 us  [the longest x1 78.5 us: local_step(): (grad_blk.astype(F32) + layer_norm_bwd(grad_u, x_hat, inv_std, ln_gamma))...]
  transfers between devices with their start and end apart: 5 -> 9, of which waited for: 3 -> 3; matrix products, arithmetic and copies ran while one was open for 9% -> 49% of each run, Pallas kernels for 0% -> 0%
where the time goes in v1:
time: 1960 us; the launch traced here: 1950 us
  matrix products  1270 us (65%)
  other arithmetic  282 us (14%)
  blocking collectives  214 us (11%)
  local copies, waits for them, and re-layouts  133 us (7%)
  waiting for transfers between devices  23.2 us (1%)
    dot_general x6, matrix products, project(): jnp.dot(u_act, w3[:, e], preferred_element_type=F32).astype(BF16)  303 us
    dot_general x1, matrix products, local_step(): lax.dot_general(jnp.concatenate([r_n, r_f], axis=1), w_all, (((1,), (1,))...  289 us
    dot_general x24, matrix products, mix(): jnp.dot(act[:, g * GROUP:(g + 1) * GROUP], bd[g], preferred_element_type=...  268 us
    unnamed x1, blocking collectives  189 us
    dot_general x1, matrix products, local_step(): lax.dot_general(u_act, r_n, (((0,), (0,)), ((), ())), preferred_element_t...  130 us
    unnamed x3, other arithmetic  118 us
    dot_general x2, matrix products, project(): lax.dot_general(grad_blk, wo, (((1,), (1,)), ((), ())), preferred_element...  95.9 us
    dot_general x1, matrix products, local_step(): jnp.dot(jnp.concatenate([o_n, o_f], axis=1), jnp.concatenate([w_out, wo_f...  89.1 us
  transfers between devices with their start and end apart: 9, of which 3 were waited for; matrix products, arithmetic and copies ran while one was open for 49% of the time, Pallas kernels for 0%

profile of v1, /device:TPU:0, one launch (start us, length us, event | category | flops | bytes accessed | tf_op | source)
XLA Modules:
  0.0 1948.3 jit_solution(4995384215006939480)
XLA Ops:
  7.2 16.4 convert_reduce_fusion
  23.6 23.3 %fusion.17 = f32[16384]{0:T(1024)S(1)} fusion(bf16[16384,1536]{1,0:T(8,128)(2,1)} %param.7, f32[16384]{0:T(1024)S(1)} %broadcast_multiply_fusion.10), kind=kLoop, calls=%fused_computation.20 | loop fusion | flops 100646912 | bytes 50462720 | tf_op jit(solution)/shard_map/reduce_sum | solution.py:15
  47.0 33.5 %fusion.10 = bf16[16384,1536]{1,0:T(8,128)(2,1)} fusion(bf16[16384,1536]{1,0:T(8,128)(2,1)} %param.7, f32[1536]{0:T(1024)S(1)} %copy-done.34, f32[1536]{0:T(1024)S(1)} %copy-done.31, f32[16384]{0:T(1024)S(1)} %add_rsqrt_fusion, f32[16384]{0:T(1024)S(1)} %broadcast_multiply_fusion.10), kind=kLoop, calls=%fused_computation.13 | loop fusion | flops 150994944 | bytes 100806656 | tf_op jit(solution)/shard_map/convert_element_type | solution.py:17
  80.5 48.0 %convolution_convert_fusion.7 = bf16[16384,768]{1,0:T(8,128)(2,1)} fusion(bf16[16384,1536]{1,0:T(8,128)(2,1)} %fusion.10, bf16[1536,3,768]{2,0,1:T(8,128)(2,1)} %param.9), kind=kOutput, calls=%fused_computation.44 | convolution fusion | flops 38667288576 | bytes 77856768 | tf_op jit(solution)/shard_map/dot_general | solution.py:87
  128.5 47.9 %convolution_convert_fusion.3 = bf16[16384,768]{1,0:T(8,128)(2,1)} fusion(bf16[16384,1536]{1,0:T(8,128)(2,1)} %param.8, bf16[768,1536]{1,0:T(8,128)(2,1)S(1)} %copy-done.36), kind=kOutput, calls=%fused_computation.40 | convolution fusion | flops 38667288576 | bytes 77856768 | tf_op jit(solution)/shard_map/dot_general | solution.py:88
  176.4 9.1 fusion.70
  185.6 8.8 fusion.67
  194.4 9.3 fusion.64
  203.7 48.9 %fusion.22 = (f32[768]{0:T(1024)S(1)}, bf16[16384,768]{0,1:T(8,128)(2,1)}) fusion(bf16[16384,1536]{1,0:T(8,128)(2,1)} %fusion.10, bf16[1536,3,768]{2,0,1:T(8,128)(2,1)} %param.9), kind=kOutput, calls=%fused_computation.30 | convolution fusion | flops 38705037312 | bytes 77859840 | tf_op jit(solution)/shard_map/dot_general | solution.py:87
  252.6 49.3 %fusion.19 = (f32[768]{0:T(1024)S(1)}, bf16[16384,768]{0,1:T(8,128)(2,1)}) fusion(bf16[16384,1536]{1,0:T(8,128)(2,1)} %fusion.10, bf16[1536,3,768]{2,0,1:T(8,128)(2,1)} %param.9), kind=kOutput, calls=%fused_computation.27 | convolution fusion | flops 38705037312 | bytes 77859840 | tf_op jit(solution)/shard_map/dot_general | solution.py:87
  302.0 8.1 fusion.85
  310.2 8.2 fusion.92
  318.4 8.1 fusion.78
  348.9 13.8 all-reduce.2
  362.9 18.2 all-reduce.6.cloned.1.call-done
  381.1 4.3 fusion.136
  385.4 2.9 fusion.117
  392.1 3.7 collective-permute-done.3
  398.7 4.9 broadcast_multiply_fusion
  406.7 11.5 fusion.76
  419.7 11.5 fusion.83
  432.6 11.5 fusion.90
  445.6 11.5 fusion.80
  458.5 11.9 fusion.87
  471.9 11.6 fusion.94
  483.5 42.3 %constant_dynamic-update-slice_fusion.28 = (bf16[16384,2304]{0,1:T(8,128)(2,1)}, bf16[16384,768]{0,1:T(8,128)(2,1)}) fusion(f32[768]{0:T(1024)S(1)} %mul.272, bf16[16384,768]{0,1:T(8,128)(2,1)} %get-tuple-element.73, f32[16384,256]{0,1:T(8,128)} %fusion.76, f32[16384,256]{0,1:T(8,128)} %fusion.83, f32[16384,256]{0,1:T(8,128)} %fusion.90), kind=kLoop, calls=%fused_computation.198 | loop fusion | flops 75497472 | bytes 125832192
  525.8 20.4 %constant_dynamic-update-slice_fusion.23 = bf16[16384,4608]{0,1:T(8,128)(2,1)} fusion(bf16[16384,768]{0,1:T(8,128)(2,1)} %get-tuple-element.30), kind=kLoop, calls=%fused_computation.193 | loop fusion | bytes 50331648
  552.3 42.3 %constant_dynamic-update-slice_fusion.27 = (bf16[16384,2304]{0,1:T(8,128)(2,1)}, bf16[16384,768]{0,1:T(8,128)(2,1)}) fusion(bf16[16384,2304]{0,1:T(8,128)(2,1)} %get-tuple-element.29, f32[768]{0:T(1024)S(1)} %mul.278, bf16[16384,768]{0,1:T(8,128)(2,1)} %get-tuple-element.71, f32[16384,256]{0,1:T(8,128)} %fusion.80, f32[16384,256]{0,1:T(8,128)} %fusion.87, ...), kind=kLoop, calls=%fused_computation.197 | loop fusion | flops 75497472 | bytes 125832192
  594.6 20.4 %constant_dynamic-update-slice_fusion.22 = bf16[16384,4608]{0,1:T(8,128)(2,1)} fusion(bf16[16384,4608]{0,1:T(8,128)(2,1)} %constant_dynamic-update-slice_fusion.23, bf16[16384,768]{0,1:T(8,128)(2,1)} %get-tuple-element.28), kind=kLoop, calls=%fused_computation.192 | loop fusion | bytes 50331648
  615.0 12.4 constant_dynamic-update-slice_fusion.26
  627.3 12.6 constant_dynamic-update-slice_fusion.25
  639.9 12.7 constant_dynamic-update-slice_fusion.24
  652.6 129.9 %fusion.139 = f32[1536,2304]{0,1:T(8,128)} fusion(bf16[16384,2304]{0,1:T(8,128)(2,1)} %get-tuple-element.31, bf16[16384,1536]{1,0:T(8,128)(2,1)} %fusion.10), kind=kOutput, calls=%fused_computation.238 | convolution fusion | flops 115964116992 | bytes 139984896 | tf_op jit(solution)/shard_map/dot_general | solution.py:115
  786.5 10.3 copy.44
  798.5 189.5 %all-reduce = f32[48]{0:T(128)} all-reduce(f32[48]{0:T(128)S(1)} %dynamic-update-slice), channel_id=1, replica_groups=mesh['dp'=1,'tp'=2,'sp'=4] {'tp'}, use_global_device_ids=true, to_apply=%add | all-reduce | flops 48 | bytes 384
  995.4 12.6 constant_dynamic-update-slice_fusion.10
  1007.9 12.4 constant_dynamic-update-slice_fusion.9
  1020.3 12.3 constant_dynamic-update-slice_fusion.8
  1032.6 46.8 %fusion.29 = f32[768,1536]{1,0:T(8,128)} fusion(bf16[16384,1536]{1,0:T(8,128)(2,1)} %param.8, bf16[16384,256]{0,1:T(8,128)(2,1)} %get-tuple-element.81, bf16[16384,256]{0,1:T(8,128)(2,1)} %get-tuple-element.79, bf16[16384,256]{0,1:T(8,128)(2,1)} %get-tuple-element.77), kind=kOutput, calls=%fused_computation.47 | convolution fusion | flops 38730203136 | bytes 80216064 | tf_op jit(solution)/shard_map/dot_general | solution.py:113
  1081.5 2.1 squeeze.111
  1093.7 2.1 squeeze.117
  1099.9 2.1 squeeze.97
  1106.2 48.0 %convolution_convert_fusion = bf16[16384,768]{1,0:T(8,128)(2,1)} fusion(bf16[16384,1536]{1,0:T(8,128)(2,1)} %param.8, bf16[768,1536]{1,0:T(8,128)(2,1)} %collective-permute-done.2), kind=kOutput, calls=%fused_computation.37 | convolution fusion | flops 38667288576 | bytes 77856768 | tf_op jit(solution)/shard_map/dot_general | solution.py:88
  1154.2 48.1 %convolution_convert_fusion.2 = bf16[16384,768]{0,1:T(8,128)(2,1)} fusion(bf16[16384,1536]{1,0:T(8,128)(2,1)} %fusion.10, bf16[1536,3,768]{0,2,1:T(8,128)(2,1)} %collective-permute-done), kind=kOutput, calls=%fused_computation.39 | convolution fusion | flops 38667288576 | bytes 77856768 | tf_op jit(solution)/shard_map/dot_general | solution.py:87
  1202.3 11.6 fusion.54
  1214.0 11.6 fusion.56
  1225.6 11.5 fusion.58
  1237.1 60.2 %fusion.28 = (bf16[16384,4608]{0,1:T(8,128)(2,1)}, bf16[16384,768]{0,1:T(8,128)(2,1)}) fusion(bf16[16384,4608]{0,1:T(8,128)(2,1)} %get-tuple-element.32, f32[16384,256]{0,1:T(8,128)} %fusion.54, f32[16384,256]{0,1:T(8,128)} %fusion.56, f32[16384,256]{0,1:T(8,128)} %fusion.58, f32[768]{0:T(1024)S(1)} %copy-done.35, bf16[16384,1536]{1,0:T(8,128)(2,1)} %fusion.10, ...), kind=kOutput, calls=%fused_computation.46 | convolution fusion | flops 38742786048 | bytes 153357312 | tf_op jit(solution)/shard_map/dot_general | solution.py:87
  1297.3 11.6 fusion.52
  1309.0 11.6 fusion.50
  1320.6 11.5 fusion.48
  1332.1 33.5 %fusion.27 = bf16[16384,4608]{0,1:T(8,128)(2,1)} fusion(bf16[16384,4608]{0,1:T(8,128)(2,1)} %get-tuple-element.82, bf16[16384,768]{0,1:T(8,128)(2,1)} %convolution_convert_fusion.2, f32[16384,256]{0,1:T(8,128)} %fusion.48, f32[16384,256]{0,1:T(8,128)} %fusion.50, f32[16384,256]{0,1:T(8,128)} %fusion.52, f32[768]{0:T(1024)S(1)} %copy-done.33), kind=kLoop, calls=%fused_computation.45 | loop fusion | flops 75497472 | bytes 100666368
  1365.6 9.2 fusion.38
  1374.8 9.0 fusion.39
  1383.9 9.1 fusion.40
  1393.0 289.0 %fusion.16 = (f32[1536]{0:T(1024)S(1)}, f32[16384]{0:T(1024)S(1)}, f32[16384]{0:T(1024)S(1)}, f32[1536]{0:T(1024)S(1)}, f32[16384,1536]{1,0:T(8,128)}) fusion(bf16[16384,1536]{1,0:T(8,128)(2,1)} %param.7, f32[16384]{0:T(1024)S(1)} %copy-done.9, f32[16384]{0:T(1024)S(1)} %copy-done.5, f32[1536]{0:T(1024)S(1)} %copy-done.32, bf16[16384,4608]{0,1:T(8,128)(2,1)} %fusion.40, ...), kind=kOutput, calls=%fused_computation.19 | convolution fusion | flops 232208171008 | bytes 316426240 | tf_op jit(solution)/shard_map/dot_general | solution.py:120
  1682.0 11.0 all-reduce.1
  1693.0 48.3 %convolution_convert_fusion.4 = bf16[16384,768]{1,0:T(8,128)(2,1)} fusion(bf16[16384,1536]{1,0:T(8,128)(2,1)} %fusion.10, bf16[1536,3,768]{0,2,1:T(8,128)(2,1)} %collective-permute-done), kind=kOutput, calls=%fused_computation.41 | convolution fusion | flops 38667288576 | bytes 77856768 | tf_op jit(solution)/shard_map/dot_general | solution.py:87
  1741.4 9.0 fusion.35
  1750.4 9.1 fusion.36
  1759.5 9.0 fusion.37
  1768.5 78.5 %fusion.15 = bf16[16384,1536]{1,0:T(8,128)(2,1)} fusion(bf16[16384,1536]{1,0:T(8,128)(2,1)} %param.7, bf16[16384,1536]{1,0:T(8,128)(2,1)} %param.8, f32[16384,1536]{1,0:T(8,128)} %get-tuple-element.84, f32[16384]{0:T(1024)S(1)} %broadcast_multiply_fusion.8, f32[16384]{0:T(1024)S(1)} %broadcast_multiply_fusion.9, f32[1536]{0:T(1024)S(1)} %copy-done.32, ...), kind=kLoop, calls=%fused_computation.18 | loop fusion | flops 276824064 | bytes 251926528 | tf_op jit(solution)/shard_map/convert_element_type | solution.py:122
  1847.1 89.1 %fusion.18 = bf16[16384,1536]{1,0:T(8,128)(2,1)} fusion(bf16[16384,1536]{1,0:T(8,128)(2,1)} %param.7, bf16[16384,1536]{0,1:T(8,128)(2,1)} %fusion.37, bf16[768,1536]{1,0:T(8,128)(2,1)} %collective-permute-done.2, bf16[768,1536]{1,0:T(8,128)(2,1)S(1)} %copy-done.37), kind=kOutput, calls=%fused_computation.21 | convolution fusion | flops 77394345984 | bytes 155713536 | tf_op jit(solution)/shard_map/dot_general | solution.py:118
  1936.2 5.2 copy.60
  (177 shorter events, 78.6 us)
Async XLA Ops:
  7.2 373.9 %all-reduce.6.cloned.1.call-start = ((), (), s32[]{:S(2)}) async-start(), calls=%async_computation.4 | async-start | bytes 1572864 | tf_op jit(solution)/shard_map/psum | solution.py:94
  23.6 23.3 %copy-start.4 = (f32[16384]{0:T(1024)}, f32[16384]{0:T(1024)S(1)}, u32[]{:S(2)}) copy-start(f32[16384]{0:T(1024)S(1)} %broadcast_multiply_fusion.10) | copy-start | bytes 196612
  23.6 23.3 %copy-start.31 = (f32[1536]{0:T(1024)S(1)}, f32[1536]{0:T(1024)}, u32[]{:S(2)}) copy-start(f32[1536]{0:T(1024)} %param.11) | copy-start | bytes 18436
  23.6 23.3 %copy-start.34 = (f32[1536]{0:T(1024)S(1)}, f32[1536]{0:T(1024)}, u32[]{:S(2)}) copy-start(f32[1536]{0:T(1024)} %param.12) | copy-start | bytes 18436
  47.0 33.5 %copy-start.8 = (f32[16384]{0:T(1024)}, f32[16384]{0:T(1024)S(1)}, u32[]{:S(2)}) copy-start(f32[16384]{0:T(1024)S(1)} %add_rsqrt_fusion) | copy-start | bytes 196612
  80.5 48.0 %copy-start.36 = (bf16[768,1536]{1,0:T(8,128)(2,1)S(1)}, bf16[768,1536]{1,0:T(8,128)(2,1)}, u32[]{:S(2)}) copy-start(bf16[768,1536]{1,0:T(8,128)(2,1)} %param.10) | copy-start | bytes 7077892
  310.1 16.4 copy-start.20
  310.1 17.8 copy-start.19
  310.1 18.1 copy-start.18
  318.4 44.4 %copy-start.38 = (f32[48]{0:T(128)S(1)}, f32[48]{0:T(128)}, u32[]{:S(2)}) copy-start(f32[48]{0:T(128)} %param.13) | copy-start | bytes 580
  337.2 10.7 copy-start.16
  347.9 0.7 copy-start.17
  348.7 1587.4 %reduce-scatter.3.cloned.1.call-start = ((), (), s32[]{:S(2)}) async-start(), calls=%async_computation.2 | async-start | bytes 17694720 | tf_op jit(solution)/shard_map/reduce_scatter | solution.py:116
  388.3 7.5 collective-permute-start.3
  389.8 8.1 collective-permute-start.1
  390.3 8.4 copy-start.29
  390.3 8.3 copy-start.27
  395.8 2.9 copy-start.6
  397.9 0.8 copy-start.7
  652.6 130.1 %copy-start.30 = (f32[24,32]{1,0:T(8,128)S(1)}, f32[24,32]{1,0:T(8,128)}, u32[]{:S(2)}) copy-start(f32[24,32]{1,0:T(8,128)} %copy-done.29) | copy-start | bytes 9220
  652.6 131.9 %copy-start.28 = (f32[24,32]{1,0:T(8,128)S(1)}, f32[24,32]{1,0:T(8,128)}, u32[]{:S(2)}) copy-start(f32[24,32]{1,0:T(8,128)} %copy-done.27) | copy-start | bytes 9220
  782.5 14.5 copy-start.39
  782.6 15.7 copy-start.40
  782.6 206.8 %copy-start.2 = (bf16[3,8,32,8,32]{4,3,2,1,0:T(8,128)(2,1)S(1)}, bf16[3,8,32,8,32]{4,3,2,1,0:T(8,128)(2,1)}, u32[]{:S(2)}) copy-start(bf16[3,8,32,8,32]{4,3,2,1,0:T(8,128)(2,1)} %get-tuple-element.63) | copy-start | bytes 1179652
  782.6 206.7 %copy-start.3 = (bf16[3,8,32,8,32]{4,3,2,1,0:T(8,128)(2,1)S(1)}, bf16[3,8,32,8,32]{4,3,2,1,0:T(8,128)(2,1)}, u32[]{:S(2)}) copy-start(bf16[3,8,32,8,32]{4,3,2,1,0:T(8,128)(2,1)} %get-tuple-element.69) | copy-start | bytes 1179652
  782.6 1158.7 %reduce-scatter.5.cloned.1.call-start = ((), (), s32[]{:S(2)}) async-start(), calls=%async_computation.3 | async-start | bytes 5898240 | tf_op jit(solution)/shard_map/reduce_scatter | solution.py:114
  782.7 205.3 %collective-permute-start.4 = (f32[24,32]{1,0:T(8,128)S(1)}, f32[24,32]{1,0:T(8,128)S(1)}, u32[]{:S(2)}, u32[]{:S(2)}) collective-permute-start(f32[24,32]{1,0:T(8,128)S(1)} %copy-done.30), channel_id=1, source_target_pairs={{0,4},{4,0},{1,5},{5,1},{2,6},{6,2},{3,7},{7,3}} | collective-permute-start | bytes 9224 | tf_op jit(solution)/shard_map/ppermute | solution.py:99
  784.4 204.2 %collective-permute-start.5 = (f32[24,32]{1,0:T(8,128)S(1)}, f32[24,32]{1,0:T(8,128)S(1)}, u32[]{:S(2)}, u32[]{:S(2)}) collective-permute-start(f32[24,32]{1,0:T(8,128)S(1)} %copy-done.28), channel_id=1, source_target_pairs={{0,4},{4,0},{1,5},{5,1},{2,6},{6,2},{3,7},{7,3}} | collective-permute-start | bytes 9224 | tf_op jit(solution)/shard_map/ppermute | solution.py:99
  784.7 321.5 %collective-permute-start.2 = (bf16[768,1536]{1,0:T(8,128)(2,1)}, bf16[768,1536]{1,0:T(8,128)(2,1)}, u32[]{:S(2)}, u32[]{:S(2)}) collective-permute-start(bf16[768,1536]{1,0:T(8,128)(2,1)} %param.10), channel_id=1, source_target_pairs={{0,4},{4,0},{1,5},{5,1},{2,6},{6,2},{3,7},{7,3}} | collective-permute-start | bytes 7077896 | tf_op jit(solution)/shard_map/ppermute | solution.py:83
  796.8 357.5 %collective-permute-start = (bf16[1536,3,768]{0,2,1:T(8,128)(2,1)}, bf16[1536,3,768]{0,2,1:T(8,128)(2,1)}, u32[]{:S(2)}, u32[]{:S(2)}) collective-permute-start(bf16[1536,3,768]{0,2,1:T(8,128)(2,1)} %copy.44), channel_id=1, source_target_pairs={{0,4},{4,0},{1,5},{5,1},{2,6},{6,2},{3,7},{7,3}} | collective-permute-start | bytes 21233672 | tf_op jit(solution)/shard_map/ppermute | solution.py:82
  1032.6 53.1 %copy-start = (bf16[3,8,32,8,32]{4,3,2,1,0:T(8,128)(2,1)S(1)}, bf16[3,8,32,8,32]{4,3,2,1,0:T(8,128)(2,1)}, u32[]{:S(2)}) copy-start(bf16[3,8,32,8,32]{4,3,2,1,0:T(8,128)(2,1)} %get-tuple-element.62) | copy-start | bytes 1179652
  1032.6 53.1 %copy-start.1 = (bf16[3,8,32,8,32]{4,3,2,1,0:T(8,128)(2,1)S(1)}, bf16[3,8,32,8,32]{4,3,2,1,0:T(8,128)(2,1)}, u32[]{:S(2)}) copy-start(bf16[3,8,32,8,32]{4,3,2,1,0:T(8,128)(2,1)} %get-tuple-element.68) | copy-start | bytes 1179652
  1154.2 48.1 %copy-start.10 = (bf16[256,256]{1,0:T(8,128)(2,1)S(1)}, bf16[256,256]{1,0:T(8,128)(2,1)}, u32[]{:S(2)}) copy-start(bf16[256,256]{1,0:T(8,128)(2,1)} %squeeze.112) | copy-start | bytes 393220
  1202.3 11.7 copy-start.11
  1202.3 23.3 %copy-start.12 = (bf16[256,256]{1,0:T(8,128)(2,1)S(1)}, bf16[256,256]{1,0:T(8,128)(2,1)}, u32[]{:S(2)}) copy-start(bf16[256,256]{1,0:T(8,128)(2,1)} %squeeze.110) | copy-start | bytes 393220
  1214.0 23.1 %copy-start.35 = (f32[768]{0:T(1024)S(1)}, f32[768]{0:T(1024)}, u32[]{:S(2)}) copy-start(f32[768]{0:T(1024)} %mul.287) | copy-start | bytes 9220
  1237.1 60.2 %copy-start.13 = (bf16[256,256]{1,0:T(8,128)(2,1)S(1)}, bf16[256,256]{1,0:T(8,128)(2,1)}, u32[]{:S(2)}) copy-start(bf16[256,256]{1,0:T(8,128)(2,1)} %squeeze.114) | copy-start | bytes 393220
  1297.3 11.7 copy-start.14
  1297.3 23.3 %copy-start.15 = (bf16[256,256]{1,0:T(8,128)(2,1)S(1)}, bf16[256,256]{1,0:T(8,128)(2,1)}, u32[]{:S(2)}) copy-start(bf16[256,256]{1,0:T(8,128)(2,1)} %squeeze.116) | copy-start | bytes 393220
  1309.0 23.1 %copy-start.33 = (f32[768]{0:T(1024)S(1)}, f32[768]{0:T(1024)}, u32[]{:S(2)}) copy-start(f32[768]{0:T(1024)} %mul.293) | copy-start | bytes 9220
  1332.1 33.5 %copy-start.26 = (bf16[256,256]{1,0:T(8,128)(2,1)S(1)}, bf16[256,256]{1,0:T(8,128)(2,1)}, u32[]{:S(2)}) copy-start(bf16[256,256]{1,0:T(8,128)(2,1)} %squeeze.117) | copy-start | bytes 393220
  1332.1 42.7 %copy-start.24 = (bf16[256,256]{1,0:T(8,128)(2,1)S(1)}, bf16[256,256]{1,0:T(8,128)(2,1)}, u32[]{:S(2)}) copy-start(bf16[256,256]{1,0:T(8,128)(2,1)} %squeeze.118) | copy-start | bytes 393220
  1365.6 18.3 copy-start.25
  1374.8 18.2 copy-start.5
  1374.8 18.2 copy-start.9
  1374.8 18.2 copy-start.32
  1693.0 48.4 %copy-start.21 = (bf16[256,256]{1,0:T(8,128)(2,1)S(1)}, bf16[256,256]{1,0:T(8,128)(2,1)}, u32[]{:S(2)}) copy-start(bf16[256,256]{1,0:T(8,128)(2,1)} %squeeze.97) | copy-start | bytes 393220
  1693.0 57.4 %copy-start.22 = (bf16[256,256]{1,0:T(8,128)(2,1)S(1)}, bf16[256,256]{1,0:T(8,128)(2,1)}, u32[]{:S(2)}) copy-start(bf16[256,256]{1,0:T(8,128)(2,1)} %squeeze.98) | copy-start | bytes 393220
  1741.3 18.1 copy-start.23
  1768.5 78.6 %copy-start.37 = (bf16[768,1536]{1,0:T(8,128)(2,1)S(1)}, bf16[768,1536]{1,0:T(8,128)(2,1)}, u32[]{:S(2)}) copy-start(bf16[768,1536]{1,0:T(8,128)(2,1)} %param.10) | copy-start | bytes 7077892
Sparse Core Ops, SparseCore 0:
  348.8 32.2 all-reduce.5
  782.7 100.7 reduce-scatter.2
  1106.4 42.3 reduce-scatter.4

commit v2 on v0

v2 whole, which is shorter than its diff:
```python
import functools

import jax
import jax.numpy as jnp
from jax import lax
from jax.experimental import pallas as pl
from jax.experimental.pallas import tpu as pltpu
from jax.sharding import PartitionSpec as P


LN_EPS = 1e-6
GROUP = 256
HEAD = 32
F32 = jnp.float32
BF16 = jnp.bfloat16
NN = (((1,), (0,)), ((), ()))
NT = (((1,), (1,)), ((), ()))
TN = (((0,), (0,)), ((), ()))
PROJ_ROWS = 512
ROWS = 256
OWN_CHUNKS = (4, 6, 8, 6)


def dot(a, b, dims=NN):
    return lax.dot_general(a, b, dims, preferred_element_type=F32)


def normalize(x):
    cen = x - jnp.mean(x, axis=-1, keepdims=True)
    inv = lax.rsqrt(jnp.mean(cen * cen, axis=-1, keepdims=True) + LN_EPS)
    return cen * inv, inv


def row_spec(rows, cols, index):
    return pl.BlockSpec((rows, cols), lambda *a: (index(*a), 0))


def whole(shape):
    return pl.BlockSpec(shape, lambda *a: (0,) * len(shape), pipeline_mode=pl.Buffered(1))


def sds(shape, dtype):
    return jax.ShapeDtypeStruct(shape, dtype)


def params(**kw):
    return pltpu.CompilerParams(vmem_limit_bytes=64_000_000, **kw)


def cost(flops, nbytes):
    return pl.CostEstimate(flops=int(flops), bytes_accessed=int(nbytes), transcendentals=0)


def project_body(x_ref, g_ref, w_ref, wo_ref, gm_ref, bt_ref, u_ref, q_ref, k_ref, v_ref, do_ref, part_ref, gr, da, qs, ks):
    i = pl.program_id(0)
    rows, cols = q_ref.shape
    groups = cols // GROUP
    do_ref[...] = dot(g_ref[...], wo_ref[...], NT).astype(BF16)
    xh, _ = normalize(x_ref[...].astype(F32))
    u_ref[...] = (xh * gm_ref[...] + bt_ref[...]).astype(BF16)
    u = u_ref[...]
    for e, out in enumerate((q_ref, k_ref, v_ref)):
        out[...] = dot(u, w_ref[e]).astype(BF16)

    def add(acc, s, val):
        acc[s] = jnp.where(i == 0, val, acc[s] + val)

    for s in range(groups):
        c = slice(s * GROUP, (s + 1) * GROUP)
        add(gr, s, dot(q_ref[:, c], k_ref[:, c], TN))
        add(da, s, dot(do_ref[:, c], v_ref[:, c], TN))
    for acc, t in ((qs, q_ref), (ks, k_ref)):
        f = t[...].astype(F32)
        val = jnp.sum((f * f).reshape(rows // 8, 8, cols), axis=0)
        acc[...] = jnp.where(i == 0, val, acc[...] + val)

    @pl.when(i == pl.num_programs(0) - 1)
    def _():
        col_head = lax.broadcasted_iota(jnp.int32, (HEAD, GROUP), 1) // HEAD
        for a, acc in enumerate((gr, da)):
            for s in range(groups):
                tot = jnp.zeros((HEAD, GROUP), F32)
                for h in range(GROUP // HEAD):
                    tot += jnp.where(col_head == h, acc[s, h * HEAD:(h + 1) * HEAD, :], 0.0)
                part_ref[(a * groups + s) * HEAD:(a * groups + s + 1) * HEAD, :] = tot
        base = 2 * groups * HEAD
        for a, acc in enumerate((qs, ks)):
            tot = jnp.sum(acc[...], axis=0, keepdims=True)
            for s in range(groups):
                part_ref[base + 8 * (a * groups + s):base + 8 * (a * groups + s + 1), :] = jnp.broadcast_to(
                    tot[:, s * GROUP:(s + 1) * GROUP], (8, GROUP))


def project(x, g, w3, wo, gamma, beta):
    tokens, width = x.shape
    cols = wo.shape[0]
    groups = cols // GROUP
    part_rows = 2 * groups * (HEAD + 8)
    row = lambda c: row_spec(PROJ_ROWS, c, lambda i: i)
    return pl.pallas_call(
        project_body,
        grid=(tokens // PROJ_ROWS,),
        in_specs=[row(width), row(width), whole(w3.shape), whole(wo.shape), whole((1, width)), whole((1, width))],
        out_specs=[row(width)] + [row(cols)] * 4 + [pl.BlockSpec((part_rows, GROUP), lambda i: (0, 0))],
        out_shape=[sds((tokens, width), BF16)] + [sds((tokens, cols), BF16)] * 4 + [sds((part_rows, GROUP), F32)],
        scratch_shapes=[pltpu.VMEM((groups, GROUP, GROUP), F32)] * 2 + [pltpu.VMEM((8, cols), F32)] * 2,
        name="project",
        compiler_params=params(),
        cost_estimate=cost(2 * tokens * width * cols * 4.4, 2 * tokens * (3 * width + 4 * cols)),
    )(x, g, w3, wo, gamma, beta)


def far_v_body(off_ref, u_ref, w_ref, v_ref):
    v_ref[...] = dot(u_ref[...], w_ref[...]).astype(BF16)


def far_v(off, u, w, blocks):
    width, cols = w.shape
    rows = 2 * ROWS
    return pl.pallas_call(
        far_v_body,
        grid_spec=pltpu.PrefetchScalarGridSpec(
            num_scalar_prefetch=1,
            grid=(blocks // 2,),
            in_specs=[row_spec(rows, width, lambda j, off: off[1] // 2 + j), whole(w.shape)],
            out_specs=row_spec(rows, cols, lambda j, off: j),
        ),
        out_shape=sds((blocks * ROWS, cols), BF16),
        name="far_v",
        compiler_params=params(),
        cost_estimate=cost(2 * blocks * ROWS * width * cols, 2 * blocks * ROWS * (width + cols)),
    )(off, u, w)


def state_body(near_ref, far_ref, tau_ref, attn_ref, dgram_ref, coef_ref, dtau_ref, *, groups):
    r_head = lax.broadcasted_iota(jnp.int32, (GROUP, GROUP), 0)
    c_head = lax.broadcasted_iota(jnp.int32, (GROUP, GROUP), 1)
    eye = r_head == c_head
    mask = (r_head // HEAD) == (c_head // HEAD)
    spread = lambda t: jnp.concatenate([t] * (GROUP // HEAD), axis=0)
    to_col = lambda t: jnp.sum(jnp.where(eye, t, 0.0), axis=1, keepdims=True)
    to_row = lambda t: jnp.sum(jnp.where(eye, t, 0.0), axis=0, keepdims=True)
    base = 2 * groups * HEAD
    coef_ref[...] = jnp.zeros_like(coef_ref)
    dtau_ref[...] = jnp.zeros_like(dtau_ref)
    for side, ref in enumerate((near_ref, far_ref)):
        for s in range(groups):
            gram_mat = spread(ref[s * HEAD:(s + 1) * HEAD, :])
            d_attn = spread(ref[(groups + s) * HEAD:(groups + s + 1) * HEAD, :])
            b_row = ref[base + 8 * (groups + s):base + 8 * (groups + s) + 1, :]
            a_col = to_col(ref[base + 8 * s:base + 8 * s + 1, :])
            g = side * groups + s
            tau = to_col(tau_ref[g:g + 1, :])
            norm_prod = jnp.sqrt(a_col) * jnp.sqrt(b_row)
            gram_n = gram_mat / norm_prod
            logit = jnp.where(mask, tau * gram_n, -jnp.inf)
            e = jnp.exp(logit - jnp.max(logit, axis=1, keepdims=True))
            attn = e / jnp.sum(e, axis=1, keepdims=True)
            d_attn = jnp.where(mask, d_attn, 0.0)
            d_logit = jnp.where(mask, attn * (d_attn - jnp.sum(attn * d_attn, axis=1, keepdims=True)), 0.0)
            gram_n = jnp.where(mask, gram_n, 0.0)
            grad_sn = tau * d_logit
            prod = grad_sn * gram_n
            attn_ref[g] = attn.astype(BF16)
            dgram_ref[g] = jnp.where(mask, grad_sn / norm_prod, 0.0).astype(BF16)
            coef_ref[2 * side:2 * side + 1, s * GROUP:(s + 1) * GROUP] = to_row(-jnp.sum(prod, axis=1, keepdims=True) / a_col)
            coef_ref[2 * side + 1:2 * side + 2, s * GROUP:(s + 1) * GROUP] = -jnp.sum(prod, axis=0, keepdims=True) / b_row
            if side == 0:
                dtau_ref[s:s + 1, :] = to_row(jnp.sum(d_logit * gram_n, axis=1, keepdims=True))


def head_state(near, far, tau_rows):
    groups = tau_rows.shape[0] // 2
    vm = pl.BlockSpec(memory_space=pltpu.VMEM)
    return pl.pallas_call(
        functools.partial(state_body, groups=groups),
        in_specs=[vm] * 3,
        out_specs=[vm] * 4,
        out_shape=[sds((2 * groups, GROUP, GROUP), BF16)] * 2 + [sds((8, groups * GROUP), F32), sds((8, GROUP), F32)],
        name="head_state",
        cost_estimate=cost(10**9, 2 * 10**6),
    )(near, far, tau_rows)


def mix_block(q, k, v, do, attn_ref, dgram_ref, coef_ref, side, s):
    groups = attn_ref.shape[0] // 2
    am, gm = attn_ref[side * groups + s], dgram_ref[side * groups + s]
    c = slice(s * GROUP, (s + 1) * GROUP)
    dq = dot(k, gm, NT) + q.astype(F32) * coef_ref[2 * side:2 * side + 1, c]
    dk = dot(q, gm, NN) + k.astype(F32) * coef_ref[2 * side + 1:2 * side + 2, c]
    return dot(v, am, NT).astype(BF16), dq.astype(BF16), dk.astype(BF16), dot(do, am, NN).astype(BF16)


def finish_rows(j, x_ref, g_ref, du, gm_ref, dx_refs, dsum_ref):
    rows, width = x_ref.shape
    xh, inv = normalize(x_ref[...].astype(F32))
    fold = lambda t: jnp.sum(t.reshape(rows // 8, 8, width), axis=0)
    for a, val in enumerate((fold(du * xh), fold(du))):
        dsum_ref[a] = jnp.where(j == 0, val, dsum_ref[a] + val)
    gh = du * gm_ref[...]
    m1 = jnp.mean(gh, axis=-1, keepdims=True)
    m2 = jnp.mean(gh * xh, axis=-1, keepdims=True)
    dx = (g_ref[...].astype(F32) + inv * (gh - m1 - xh * m2)).astype(BF16)
    for ref in dx_refs:
        ref[...] = dx


def rows_body(*refs, near_ready, n_alias, send):
    it = iter(refs)
    nxt = lambda n: [next(it) for _ in range(n)]
    _, x_ref, g_ref, u_ref = nxt(4)
    if near_ready:
        o_in, r_in = nxt(2)
    else:
        q_ref, k_ref, v_ref, do_ref = nxt(4)
    attn_ref, dgram_ref, coef_ref, wn_ref, wf_ref, won_ref, wof_ref, gm_ref = nxt(8)
    nxt(n_alias)
    y_ref, gx_ref = nxt(2)
    if not near_ready:
        o_ref, r_ref = nxt(2)
    send_ref = nxt(1) if send else []
    (dsum_ref,) = nxt(1)
    of_s, rf_s, qf_s, kf_s, vf_s, dof_s = nxt(6)
    j = pl.program_id(0)
    groups = attn_ref.shape[0] // 2
    u = u_ref[...]
    for e, t in enumerate((qf_s, kf_s, vf_s)):
        t[...] = dot(u, wf_ref[e]).astype(BF16)
    dof_s[...] = dot(g_ref[...], wof_ref[...], NT).astype(BF16)
    if near_ready:
        o_ref, r_ref = o_in, r_in
    else:
        for s in range(groups):
            c = slice(s * GROUP, (s + 1) * GROUP)
            o_ref[:, c], r_ref[0, :, c], r_ref[1, :, c], r_ref[2, :, c] = mix_block(
                q_ref[:, c], k_ref[:, c], v_ref[:, c], do_ref[:, c], attn_ref, dgram_ref, coef_ref, 0, s)
    for s in range(groups):
        c = slice(s * GROUP, (s + 1) * GROUP)
        of_s[:, c], rf_s[0, :, c], rf_s[1, :, c], rf_s[2, :, c] = mix_block(
            qf_s[:, c], kf_s[:, c], vf_s[:, c], dof_s[:, c], attn_ref, dgram_ref, coef_ref, 1, s)
    du = dot(r_ref[0], wn_ref[0], NT)
    for e in range(1, 3):
        du += dot(r_ref[e], wn_ref[e], NT)
    for e in range(3):
        du += dot(rf_s[e], wf_ref[e], NT)
    y_ref[...] = (x_ref[...].astype(F32) + (dot(o_ref[...], won_ref[...]) + dot(of_s[...], wof_ref[...]))).astype(BF16)
    finish_rows(j, x_ref, g_ref, du, gm_ref, [gx_ref] + send_ref, dsum_ref)


def rows_call(off, sel, start, blocks, acts, state, weights, prev, *, near_ready, send):
    x = acts[0]
    tokens, width = x.shape
    cols = weights[2].shape[0]
    at = lambda j, off: off[sel] + start + j
    row = lambda c: row_spec(ROWS, c, at)
    row3 = pl.BlockSpec((3, ROWS, cols), lambda j, off: (0, at(j, off), 0))
    any_ = pl.BlockSpec(memory_space=pl.ANY)
    act_specs = [row(width)] * 3 + ([row(cols), row3] if near_ready else [row(cols)] * 4)
    consts = list(state) + list(weights)
    out_specs = [row(width)] * 2
    out_shape = [sds((tokens, width), BF16)] * 2
    if not near_ready:
        out_specs += [row(cols), row3]
        out_shape += [sds((tokens, cols), BF16), sds((3, tokens, cols), BF16)]
    n_alias = 0 if prev is None else len(prev)
    first = 1 + len(acts) + len(consts)
    aliases = {first + a: a for a in range(n_alias)}
    if send:
        out_specs.append(row_spec(ROWS, width, lambda j, off: j))
        out_shape.append(sds((blocks * ROWS, width), BF16))
    out_specs.append(pl.BlockSpec((2, 8, width), lambda j, off: (0, 0, 0)))
    out_shape.append(sds((2, 8, width), F32))
    return pl.pallas_call(
        functools.partial(rows_body, near_ready=near_ready, n_alias=n_alias, send=send),
        grid_spec=pltpu.PrefetchScalarGridSpec(
            num_scalar_prefetch=1,
            grid=(blocks,),
            in_specs=act_specs + [whole(t.shape) for t in consts] + [any_] * n_alias,
            out_specs=out_specs,
            scratch_shapes=[pltpu.VMEM((ROWS, cols), BF16), pltpu.VMEM((3, ROWS, cols), BF16)] + [pltpu.VMEM((ROWS, cols), BF16)] * 4,
        ),
        out_shape=out_shape,
        input_output_aliases=aliases,
        name="rows",
        compiler_params=params(),
        cost_estimate=cost(2 * blocks * ROWS * width * cols * 13, 2 * blocks * ROWS * (5 * width + 8 * cols)),
    )(off, *acts, *consts, *(prev or ()))


def local_body(*refs, with_y):
    it = iter(refs)
    nxt = lambda n: [next(it) for _ in range(n)]
    _, q_ref, k_ref, v_ref, do_ref = nxt(5)
    if with_y:
        x_ref, vf_ref = nxt(2)
    attn_ref, dgram_ref, coef_ref = nxt(3)
    if with_y:
        won_ref, wof_ref = nxt(2)
        nxt(3)
        y_ref, o_ref, r_ref, of_s = nxt(4)
    else:
        nxt(2)
        o_ref, r_ref = nxt(2)
    groups = attn_ref.shape[0] // 2
    for s in range(groups):
        c = slice(s * GROUP, (s + 1) * GROUP)
        if with_y:
            of_s[:, c] = dot(vf_ref[:, c], attn_ref[groups + s], NT).astype(BF16)
        o_ref[:, c], r_ref[0, :, c], r_ref[1, :, c], r_ref[2, :, c] = mix_block(
            q_ref[:, c], k_ref[:, c], v_ref[:, c], do_ref[:, c], attn_ref, dgram_ref, coef_ref, 0, s)
    if with_y:
        y_ref[...] = (x_ref[...].astype(F32) + (dot(o_ref[...], won_ref[...]) + dot(of_s[...], wof_ref[...]))).astype(BF16)


def local_call(off, sel, blocks, near, state, prev, x=None, vf=None, weights=()):
    with_y = x is not None
    cols = near[0].shape[1]
    at = lambda j, off: off[sel] + j
    row = lambda c: row_spec(ROWS, c, at)
    row3 = pl.BlockSpec((3, ROWS, cols), lambda j, off: (0, at(j, off), 0))
    any_ = pl.BlockSpec(memory_space=pl.ANY)
    acts, act_specs = list(near), [row(cols)] * 4
    if with_y:
        acts += [x, vf]
        act_specs += [row(x.shape[1]), row_spec(ROWS, cols, lambda j, off: j)]
    consts = list(state) + list(weights)
    out_specs = ([row(x.shape[1])] if with_y else []) + [row(cols), row3]
    first = 1 + len(acts) + len(consts)
    return pl.pallas_call(
        functools.partial(local_body, with_y=with_y),
        grid_spec=pltpu.PrefetchScalarGridSpec(
            num_scalar_prefetch=1,
            grid=(blocks,),
            in_specs=act_specs + [whole(t.shape) for t in consts] + [any_] * len(prev),
            out_specs=out_specs,
            scratch_shapes=[pltpu.VMEM((ROWS, cols), BF16)] if with_y else [],
        ),
        out_shape=[sds(t.shape, t.dtype) for t in prev],
        input_output_aliases={first + a: a for a in range(len(prev))},
        name="local_y" if with_y else "local",
        compiler_params=params(),
        cost_estimate=cost(2 * blocks * ROWS * cols * (1536 * 2.8 if with_y else 1024), 2 * blocks * ROWS * cols * (13 if with_y else 8)),
    )(off, *acts, *consts, *prev)


def solution(mesh):
    tp_size = mesh.shape["tp"]
    sp_size = mesh.shape["sp"]
    in_rows = P(("dp", "sp"), None)
    swap = [(0, 1), (1, 0)]

    def exchange(t):
        return lax.ppermute(t, "tp", swap)

    def step(x, g, w_qkv, w_out, ln_gamma, ln_beta, temps):
        tokens, width = x.shape
        cols = w_qkv.shape[2]
        groups = cols // GROUP
        me = lax.axis_index("tp")
        w_near = jnp.transpose(w_qkv, (1, 0, 2))
        w_far = exchange(w_near)
        wo_far = exchange(w_out)
        gamma, beta = ln_gamma.reshape(1, width), ln_beta.reshape(1, width)
        own = sum(OWN_CHUNKS)
        rest = tokens // ROWS - 2 * own
        off = jnp.stack([me * own, (1 - me) * own, jnp.full_like(me, 2 * own)]).astype(jnp.int32)

        u, q, k, v, do, part = project(x, g, w_near, w_out, gamma, beta)
        near = (q, k, v, do)
        peers = [lax.ppermute(part, "sp", [(s, s ^ d) for s in range(sp_size)]) for d in (1, 2, 3)]
        part = (part + peers[0]) + (peers[1] + peers[2])
        part_far = exchange(part)
        vf = far_v(off, u, w_far[2], own)
        tau = jnp.repeat(temps, HEAD).reshape(tp_size, groups, GROUP)
        tau = jnp.where(me == 0, tau, tau[::-1]).reshape(2 * groups, GROUP)
        attn, dgram, coef, dtau = head_state(part, part_far, tau)
        state = (attn, dgram, coef)
        weights = (w_near, w_far, w_out, wo_far, gamma)

        prev, dsum, recv, start = None, None, [], 0
        for blocks in OWN_CHUNKS:
            *prev, sent, ds = rows_call(off, 0, start, blocks, (x, g, u) + near, state, weights, prev, near_ready=False, send=True)
            recv.append((start, exchange(sent)))
            dsum = ds if dsum is None else dsum + ds
            start += blocks
        y, gx, o, r = prev
        y, o, r = local_call(off, 1, own, near, state, (y, o, r), x, vf, (w_out, wo_far))
        o, r = local_call(off, 2, rest, near, state, (o, r))
        wqkv_part = lax.dot_general(u, r, (((0,), (1,)), ((), ())), preferred_element_type=F32)
        o, wqkv_part = lax.optimization_barrier((o, wqkv_part))
        grad_wqkv = lax.psum_scatter(wqkv_part, "sp", scatter_dimension=0, tiled=True)
        wout_part = dot(o, g, TN)
        gx, wout_part = lax.optimization_barrier((gx, wout_part))
        grad_wout = lax.psum_scatter(wout_part, "sp", scatter_dimension=0, tiled=True)
        y, gx, ds = rows_call(off, 2, 0, rest, (x, g, u, o, r), state, weights, (y, gx), near_ready=True, send=False)
        sums = lax.psum(jnp.sum(dsum + 0.5 * ds, axis=1), ("tp", "sp"))
        for start, blk in recv:
            gx = lax.dynamic_update_slice(gx, blk, ((off[1] + start) * ROWS, 0))
        dtau = jnp.sum(dtau[:groups].reshape(groups * GROUP // HEAD, HEAD), axis=1)
        dtau_far = lax.ppermute(dtau, "tp", swap)
        grad_temp = jnp.where(me == 0, jnp.concatenate([dtau, dtau_far]), jnp.concatenate([dtau_far, dtau]))
        return y, gx, grad_wqkv, grad_wout, sums[0], sums[1], grad_temp

    in_specs = (in_rows, in_rows, P(None, None, "tp"), P("tp", None), P(None), P(None), P(None))
    out_specs = (in_rows, in_rows, P(("dp", "sp"), None, "tp"), P(("dp", "tp", "sp"), None), P("dp"), P("dp"), P("dp"))
    return jax.shard_map(step, mesh=mesh, in_specs=in_specs, out_specs=out_specs, check_vma=False)
```

time: 5140 us -> 1310 us (0.25)
  waiting for transfers between devices: 4030 us -> 59.4 us
  Pallas kernels: 0 us -> 728 us
  matrix products: 680 us -> 188 us
  other arithmetic: 279 us -> 3.27 us
  blocking collectives: 31.8 us -> 269 us
  local copies, waits for them, and re-layouts: 100 us -> 27.5 us
    psum x3 -> x0, waiting for transfers between devices: 4000 us -> none  [the longest x1 2120 us: local_step(): lax.psum(y_part, 'tp')]
    pallas_call x0 -> x10, Pallas kernels: none -> 728 us  [the longest x5 415 us: rows_call(): pl.pallas_call(functools.partial(rows_body, near_ready=near_ready, n_alia...]
    dot_general x12 -> x2, matrix products: 680 us -> 188 us  [the longest x1 141 us: step(): lax.dot_general(u, r, (((0,), (1,)), ((), ())), preferred_element_type=F32)]
    psum x2 -> x1, blocking collectives: 26.3 us -> 269 us  [step(): sums = lax.psum(jnp.sum(dsum + 0.5 * ds, axis=1), ('tp', 'sp'))]
    convert_element_type x1 -> x0, other arithmetic: 126 us -> none  [local_step(): (grad_blk.astype(jnp.float32) + layer_norm_bwd(grad_u, x_hat, inv_std, ln...]
    another operation x3 -> x0, local copies, waits for them, and re-layouts: 97.8 us -> none  [local_step(): jnp.stack([dq_act, dk_act, dv_act], axis=1).reshape(tokens, 3, local_cols)]
    reduce_sum x3 -> x2, other arithmetic: 86.9 us -> 1.07 us  [the longest x1 0.95 us: step(): sums = lax.psum(jnp.sum(dsum + 0.5 * ds, axis=1), ('tp', 'sp'))]
    ppermute x0 -> x11, waiting for transfers between devices: none -> 58.7 us  [the longest x7 44.5 us: exchange(): return lax.ppermute(t, 'tp', swap)]
  transfers between devices with their start and end apart: 5 -> 13, of which waited for: 3 -> 4; matrix products, arithmetic and copies ran while one was open for 9% -> 2% of each run, Pallas kernels for 0% -> 29%
where the time goes in v2:
time: 1310 us; the launch traced here: 1300 us
  Pallas kernels  728 us (56%)
  blocking collectives  269 us (21%)
  matrix products  188 us (14%)
  waiting for transfers between devices  59.4 us (5%)
  local copies, waits for them, and re-layouts  27.5 us (2%)
  between operations  14.6 us (1%)
    pallas_call x5, Pallas kernels, rows_call(): pl.pallas_call(functools.partial(rows_body, near_ready=near_ready, n_alia...  415 us
    psum x1, blocking collectives, step(): sums = lax.psum(jnp.sum(dsum + 0.5 * ds, axis=1), ('tp', 'sp'))  269 us
    pallas_call x1, Pallas kernels, project(): pl.pallas_call(project_body, grid=(tokens // PROJ_ROWS,), in_specs=[row(w...  199 us
    dot_general x1, matrix products, step(): lax.dot_general(u, r, (((0,), (1,)), ((), ())), preferred_element_type=F32)  141 us
    pallas_call x2, Pallas kernels, local_call(): pl.pallas_call(functools.partial(local_body, with_y=with_y), grid_spec=pl...  86.9 us
    dot_general x1, matrix products, dot(): return lax.dot_general(a, b, dims, preferred_element_type=F32)  46.8 us
    ppermute x7, waiting for transfers between devices, exchange(): return lax.ppermute(t, 'tp', swap)  44.5 us
  transfers between devices with their start and end apart: 13, of which 4 were waited for; matrix products, arithmetic and copies ran while one was open for 2% of the time, Pallas kernels for 29%

profile of v2, /device:TPU:0, one launch (start us, length us, event | category | flops | bytes accessed | tf_op | source)
XLA Modules:
  0.0 1299.2 jit_solution(9682848782559349669)
XLA Ops:
  7.2 0.0 reduce-scatter.5.cloned.1.call-start
  7.2 3.4 collective-permute-start.4
  10.6 1.3 reshape.28.gm_ref.refs_15_.refs_13_
  11.9 1.3 reshape.29.bt_ref
  13.2 199.0 %project.1 = (bf16[16384,1536]{1,0:T(8,128)(2,1)}, bf16[16384,768]{1,0:T(8,128)(2,1)}, bf16[16384,768]{1,0:T(8,128)(2,1)}, bf16[16384,768]{1,0:T(8,128)(2,1)}, b...) custom-call(bf16[16384,1536]{1,0:T(8,128)(2,1)} %refs_1_.9, bf16[16384,1536]{1,0:T(8,128)(2,1)} %refs_2_.9, ...), custom_call_target="tpu_custom_call" | custom-call | flops 170080698368 | bytes 251658240 | tf_op jit(solution)/shard_map/project/pallas_call | solution.py:100
  212.1 0.0 collective-permute-start
  212.2 1.5 collective-permute-start.1
  213.7 0.3 collective-permute-start.2
  214.0 0.3 collective-permute-start.5
  214.3 0.1 broadcast_in_dim.7
  214.4 0.1 broadcast_in_dim.8
  214.4 0.1 broadcast_in_dim.9
  214.5 0.1 rev.3
  214.6 0.0 collective-permute-done
  214.6 6.6 collective-permute-done.1
  221.2 4.3 collective-permute-done.2
  225.5 1.0 add_add_fusion.near_ref
  226.5 0.0 copy-start.1
  226.5 0.5 collective-permute-start.3
  227.1 0.6 reshape.30.tau_ref
  227.7 0.6 pad_add_fusion.off_ref.refs_0_
  228.3 44.5 %collective-permute-done.3.far_ref = f32[240,256]{1,0:T(8,128)S(1)} collective-permute-done((f32[240,256]{1,0:T(8,128)S(1)}, f32[240,256]{1,0:T(8,128)S(1)}, u32[]{:S(2)}, u32[]{:S(2)}) %collective-permute-start.3) | collective-permute-done | bytes 245792 | tf_op jit(solution)/shard_map/ppermute | solution.py:353
  272.8 0.7 copy-done.8
  273.5 4.6 head_state.1
  278.0 0.0 collective-permute-done.4.refs_12_.refs_10_
  278.0 3.2 slice_bitcast_fusion.w_ref
  281.3 22.3 %far_v.1.refs_6_ = bf16[6144,768]{1,0:T(8,128)(2,1)} custom-call(s32[3]{0:T(128)} %pad_add_fusion.off_ref.refs_0_, bf16[16384,1536]{1,0:T(8,128)(2,1)} %get-tuple-element.53.u_ref.refs_3_, bf16[1536,768]{1,0:T(8,128)(2,1)} %slice_bitcast_fusion.w_ref), custom_call_target="tpu_custom_call" | custom-call | flops 14495514624 | bytes 28311552 | tf_op jit(solution)/shard_map/far_v/pallas_call | solution.py:120
  303.5 0.0 collective-permute-done.5.refs_14_.refs_11_.refs_12_
  303.5 48.0 %rows.5 = (bf16[16384,1536]{1,0:T(8,128)(2,1)}, bf16[16384,1536]{1,0:T(8,128)(2,1)}, bf16[16384,768]{1,0:T(8,128)(2,1)}, bf16[3,16384,768]{2,1,0:T(8,128)(2,1)},...) custom-call(s32[3]{0:T(128)} %pad_add_fusion.off_ref.refs_0_, bf16[16384,1536]{1,0:T(8,128)(2,1)} %refs_1_.9, ...), custom_call_target="tpu_custom_call" | custom-call | flops 31406948352 | bytes 28311552 | tf_op jit(solution)/shard_map/rows/pallas_call | solution.py:273
  351.6 66.1 %rows.6 = (bf16[16384,1536]{1,0:T(8,128)(2,1)}, bf16[16384,1536]{1,0:T(8,128)(2,1)}, bf16[16384,768]{1,0:T(8,128)(2,1)}, bf16[3,16384,768]{2,1,0:T(8,128)(2,1)},...) custom-call(s32[3]{0:T(128)} %pad_add_fusion.off_ref.refs_0_, ...), custom_call_target="tpu_custom_call", output_to_operand_aliasing={{0}: (16, {}), {1}: (17, {}), {2}: (18, {}), {3}: (19, {})} | custom-call | flops 47110422528 | bytes 42467328 | tf_op jit(solution)/shard_map/rows/pallas_call | solution.py:273
  417.7 84.6 %rows.7 = (bf16[16384,1536]{1,0:T(8,128)(2,1)}, bf16[16384,1536]{1,0:T(8,128)(2,1)}, bf16[16384,768]{1,0:T(8,128)(2,1)}, bf16[3,16384,768]{2,1,0:T(8,128)(2,1)},...) custom-call(s32[3]{0:T(128)} %pad_add_fusion.off_ref.refs_0_, ...), custom_call_target="tpu_custom_call", output_to_operand_aliasing={{0}: (16, {}), {1}: (17, {}), {2}: (18, {}), {3}: (19, {})} | custom-call | flops 62813896704 | bytes 56623104 | tf_op jit(solution)/shard_map/rows/pallas_call | solution.py:273
  502.3 66.3 %rows.8 = (bf16[16384,1536]{1,0:T(8,128)(2,1)}, bf16[16384,1536]{1,0:T(8,128)(2,1)}, bf16[16384,768]{1,0:T(8,128)(2,1)}, bf16[3,16384,768]{2,1,0:T(8,128)(2,1)},...) custom-call(s32[3]{0:T(128)} %pad_add_fusion.off_ref.refs_0_, ...), custom_call_target="tpu_custom_call", output_to_operand_aliasing={{0}: (16, {}), {1}: (17, {}), {2}: (18, {}), {3}: (19, {})} | custom-call | flops 47110422528 | bytes 42467328 | tf_op jit(solution)/shard_map/rows/pallas_call | solution.py:273
  568.6 60.3 %local_y.1 = (bf16[16384,1536]{1,0:T(8,128)(2,1)}, bf16[16384,768]{1,0:T(8,128)(2,1)}, bf16[3,16384,768]{2,1,0:T(8,128)(2,1)}) custom-call(s32[3]{0:T(128)} %pad_add_fusion.off_ref.refs_0_, bf16[16384,768]{1,0:T(8,128)(2,1)} %get-tuple-element.54.refs_4_.refs_1_, ...), custom_call_target="tpu_custom_call", output_to_operand_aliasing={{0}: (12, {}), {1}: (13, {}), {2}: (14, {})} | custom-call | flops 40587440128 | bytes 122683392 | tf_op jit(solution)/shard_map/local_y/pallas_call | solution.py:329
  628.8 26.6 %local.1 = (bf16[16384,768]{1,0:T(8,128)(2,1)}, bf16[3,16384,768]{2,1,0:T(8,128)(2,1)}) custom-call(s32[3]{0:T(128)} %pad_add_fusion.off_ref.refs_0_, bf16[16384,768]{1,0:T(8,128)(2,1)} %get-tuple-element.54.refs_4_.refs_1_, bf16[16384,768]{1,0:T(8,128)(2,1)} %get-tuple-element.55.refs_5_.refs_2_, ...), custom_call_target="tpu_custom_call", output_to_operand_aliasing={{0}: (8, {}), {1}: (9, {})} | custom-call | flops 6442450944 | bytes 50331648 | tf_op jit(solution)/shard_map/local/pallas_call | solution.py:329
  655.4 141.0 %fusion = f32[1536,3,768]{2,0,1:T(8,128)} fusion(bf16[3,16384,768]{2,1,0:T(8,128)(2,1)} %get-tuple-element.80.refs_5_, bf16[16384,1536]{1,0:T(8,128)(2,1)} %get-tuple-element.53.u_ref.refs_3_), kind=kOutput, calls=%fused_computation | convolution fusion | flops 115964116992 | bytes 139984896 | tf_op jit(solution)/shard_map/dot_general | solution.py:389
  796.4 0.0 copy-start.6
  796.4 46.8 %fusion.2 = f32[768,1536]{1,0:T(8,128)} fusion(bf16[16384,768]{1,0:T(8,128)(2,1)} %get-tuple-element.81.refs_4_, bf16[16384,1536]{1,0:T(8,128)(2,1)} %refs_2_.9), kind=kOutput, calls=%fused_computation.14 | convolution fusion | flops 38654705664 | bytes 80216064 | tf_op jit(solution)/shard_map/dot_general | solution.py:25
  843.2 0.0 reduce-scatter.5.cloned.1.call-update
  843.2 0.0 reduce-scatter.3.cloned.1.call-start
  843.3 0.7 reduce-scatter.3.cloned.1.call-update
  844.0 0.0 copy-done.6
  844.0 0.1 reshape.31
  844.1 0.1 reduce_sum.19
  844.2 0.3 collective-permute-start.10
  844.5 3.3 collective-permute-done.10
  847.8 0.6 broadcast_select_fusion.1
  848.4 0.3 collective-permute-start.6
  848.7 1.7 collective-permute-start.7
  850.4 0.3 collective-permute-start.8
  850.7 1.7 collective-permute-start.9
  852.4 149.9 %rows.9 = (bf16[16384,1536]{1,0:T(8,128)(2,1)}, bf16[16384,1536]{1,0:T(8,128)(2,1)}, f32[2,8,1536]{2,1,0:T(8,128)}) custom-call(s32[3]{0:T(128)} %pad_add_fusion.off_ref.refs_0_, bf16[16384,1536]{1,0:T(8,128)(2,1)} %refs_1_.9, bf16[16384,1536]{1,0:T(8,128)(2,1)} %refs_2_.9, ...), custom_call_target="tpu_custom_call", output_to_operand_aliasing={{0}: (14, {}), {1}: (15, {})} | custom-call | flops 125627793408 | bytes 113246208 | tf_op jit(solution)/shard_map/rows/pallas_call | solution.py:273
  1002.4 0.0 copy-done.2
  1002.4 0.0 copy-done.3
  1002.4 1.0 add_reduce_fusion
  1003.4 268.7 %psum.7 = f32[2,1536]{1,0:T(2,128)S(1)} all-reduce(f32[2,1536]{1,0:T(2,128)S(1)} %add_reduce_fusion), channel_id=1, replica_groups=mesh['dp'=1,'tp'=2,'sp'=4] {'tp','sp'}, use_global_device_ids=true, to_apply=%region_3.4 | all-reduce | flops 3072 | bytes 24576 | tf_op jit(solution)/shard_map/psum | solution.py:396
  1272.0 0.6 slice_reduce_fusion
  1272.7 0.0 collective-permute-done.6
  1272.7 3.8 constant_dynamic-update-slice_fusion.3
  1276.4 0.0 collective-permute-done.7
  1276.4 4.8 constant_dynamic-update-slice_fusion.2
  1281.2 0.0 collective-permute-done.8
  1281.2 5.9 constant_dynamic-update-slice_fusion.1
  1287.1 0.0 collective-permute-done.9
  1287.1 4.8 constant_dynamic-update-slice_fusion
  (18 shorter events, 0.0 us)
Async XLA Ops:
  7.2 1284.8 %reduce-scatter.5.cloned.1.call-start = ((), (), s32[]{:S(2)}) async-start(), calls=%async_computation.3 | async-start | bytes 5898240 | tf_op jit(solution)/shard_map/reduce_scatter | solution.py:394
  7.2 270.8 %collective-permute-start.4 = (bf16[3,1536,768]{2,1,0:T(8,128)(2,1)}, bf16[3,1536,768]{2,1,0:T(8,128)(2,1)}, u32[]{:S(2)}, u32[]{:S(2)}) collective-permute-start(bf16[3,1536,768]{2,1,0:T(8,128)(2,1)} %bitcast.15), channel_id=1, source_target_pairs={{0,4},{4,0},{1,5},{5,1},{2,6},{6,2},{3,7},{7,3}} | collective-permute-start | bytes 21233672 | tf_op jit(solution)/shard_map/ppermute | solution.py:353
  13.2 200.9 %copy-start = (bf16[768,1536]{1,0:T(8,128)(2,1)S(1)}, bf16[768,1536]{1,0:T(8,128)(2,1)}, u32[]{:S(2)}) copy-start(bf16[768,1536]{1,0:T(8,128)(2,1)} %refs_11_.1) | copy-start | bytes 7077892
  13.2 201.1 %copy-start.7 = (f32[48]{0:T(128)S(1)}, f32[48]{0:T(128)}, u32[]{:S(2)}) copy-start(f32[48]{0:T(128)} %param.13) | copy-start | bytes 580
  212.1 2.5 collective-permute-start
  212.2 9.1 collective-permute-start.1
  213.7 11.8 collective-permute-start.2
  214.0 89.5 %collective-permute-start.5 = (bf16[768,1536]{1,0:T(8,128)(2,1)S(1)}, bf16[768,1536]{1,0:T(8,128)(2,1)}, u32[]{:S(2)}, u32[]{:S(2)}) collective-permute-start(bf16[768,1536]{1,0:T(8,128)(2,1)S(1)} %copy-done), channel_id=1, source_target_pairs={{0,4},{4,0},{1,5},{5,1},{2,6},{6,2},{3,7},{7,3}} | collective-permute-start | bytes 7077896 | tf_op jit(solution)/shard_map/ppermute | solution.py:353
  226.5 46.2 %copy-start.1 = (f32[240,256]{1,0:T(8,128)}, f32[240,256]{1,0:T(8,128)S(1)}, u32[]{:S(2)}) copy-start(f32[240,256]{1,0:T(8,128)S(1)} %add_add_fusion.near_ref) | copy-start | bytes 737284
  226.5 46.2 %collective-permute-start.3 = (f32[240,256]{1,0:T(8,128)S(1)}, f32[240,256]{1,0:T(8,128)S(1)}, u32[]{:S(2)}, u32[]{:S(2)}) collective-permute-start(f32[240,256]{1,0:T(8,128)S(1)} %add_add_fusion.near_ref), channel_id=1, source_target_pairs={{0,4},{4,0},{1,5},{5,1},{2,6},{6,2},{3,7},{7,3}} | collective-permute-start | bytes 737288 | tf_op jit(solution)/shard_map/ppermute | solution.py:353
  272.8 0.7 copy-start.8
  796.4 47.6 %copy-start.6 = (f32[8,256]{1,0:T(8,128)S(1)}, f32[8,256]{1,0:T(8,128)}, u32[]{:S(2)}) copy-start(f32[8,256]{1,0:T(8,128)} %get-tuple-element.98) | copy-start | bytes 24580
  843.2 448.7 %reduce-scatter.3.cloned.1.call-start = ((), (), s32[]{:S(2)}) async-start(), calls=%async_computation.2 | async-start | bytes 17694720 | tf_op jit(solution)/shard_map/reduce_scatter | solution.py:391
  844.2 3.6 collective-permute-start.10
  848.4 424.3 %collective-permute-start.6 = (bf16[1024,1536]{1,0:T(8,128)(2,1)}, bf16[1024,1536]{1,0:T(8,128)(2,1)}, u32[]{:S(2)}, u32[]{:S(2)}) collective-permute-start(bf16[1024,1536]{1,0:T(8,128)(2,1)} %get-tuple-element.87), channel_id=1, source_target_pairs={{0,4},{4,0},{1,5},{5,1},{2,6},{6,2},{3,7},{7,3}} | collective-permute-start | bytes 9437192 | tf_op jit(solution)/shard_map/ppermute | solution.py:353
  848.7 427.8 %collective-permute-start.7 = (bf16[1536,1536]{1,0:T(8,128)(2,1)}, bf16[1536,1536]{1,0:T(8,128)(2,1)}, u32[]{:S(2)}, u32[]{:S(2)}) collective-permute-start(bf16[1536,1536]{1,0:T(8,128)(2,1)} %get-tuple-element.88), channel_id=1, source_target_pairs={{0,4},{4,0},{1,5},{5,1},{2,6},{6,2},{3,7},{7,3}} | collective-permute-start | bytes 14155784 | tf_op jit(solution)/shard_map/ppermute | solution.py:353
  850.4 430.8 %collective-permute-start.8 = (bf16[2048,1536]{1,0:T(8,128)(2,1)}, bf16[2048,1536]{1,0:T(8,128)(2,1)}, u32[]{:S(2)}, u32[]{:S(2)}) collective-permute-start(bf16[2048,1536]{1,0:T(8,128)(2,1)} %get-tuple-element.89), channel_id=1, source_target_pairs={{0,4},{4,0},{1,5},{5,1},{2,6},{6,2},{3,7},{7,3}} | collective-permute-start | bytes 18874376 | tf_op jit(solution)/shard_map/ppermute | solution.py:353
  850.7 436.5 %collective-permute-start.9 = (bf16[1536,1536]{1,0:T(8,128)(2,1)}, bf16[1536,1536]{1,0:T(8,128)(2,1)}, u32[]{:S(2)}, u32[]{:S(2)}) collective-permute-start(bf16[1536,1536]{1,0:T(8,128)(2,1)} %get-tuple-element.90), channel_id=1, source_target_pairs={{0,4},{4,0},{1,5},{5,1},{2,6},{6,2},{3,7},{7,3}} | collective-permute-start | bytes 14155784 | tf_op jit(solution)/shard_map/ppermute | solution.py:353
  852.4 149.9 %copy-start.2 = (f32[2,8,1536]{2,1,0:T(8,128)S(1)}, f32[2,8,1536]{2,1,0:T(8,128)}, u32[]{:S(2)}) copy-start(f32[2,8,1536]{2,1,0:T(8,128)} %get-tuple-element.93) | copy-start | bytes 294916
  852.4 149.9 %copy-start.3 = (f32[2,8,1536]{2,1,0:T(8,128)S(1)}, f32[2,8,1536]{2,1,0:T(8,128)}, u32[]{:S(2)}) copy-start(f32[2,8,1536]{2,1,0:T(8,128)} %get-tuple-element.94) | copy-start | bytes 294916
  852.4 149.9 %copy-start.4 = (f32[2,8,1536]{2,1,0:T(8,128)S(1)}, f32[2,8,1536]{2,1,0:T(8,128)}, u32[]{:S(2)}) copy-start(f32[2,8,1536]{2,1,0:T(8,128)} %get-tuple-element.95) | copy-start | bytes 294916
  852.4 150.0 %copy-start.5 = (f32[2,8,1536]{2,1,0:T(8,128)S(1)}, f32[2,8,1536]{2,1,0:T(8,128)}, u32[]{:S(2)}) copy-start(f32[2,8,1536]{2,1,0:T(8,128)} %get-tuple-element.96) | copy-start | bytes 294916
Sparse Core Ops, SparseCore 0:
  843.3 42.4 reduce-scatter.4
  888.9 101.3 reduce-scatter.2

commit v3 on v2

v3 whole, which is shorter than its diff:
```python
import functools

import jax
import jax.numpy as jnp
from jax import lax
from jax.experimental import pallas as pl
from jax.experimental.pallas import tpu as pltpu
from jax.sharding import PartitionSpec as P


LN_EPS = 1e-6
GROUP = 256
HEAD = 32
F32 = jnp.float32
BF16 = jnp.bfloat16
NN = (((1,), (0,)), ((), ()))
NT = (((1,), (1,)), ((), ()))
TN = (((0,), (0,)), ((), ()))
PROJ_ROWS = 512
ROWS = 256
OWN_CHUNKS = (4, 6, 9, 13)
EARLY_V = 12


def dot(a, b, dims=NN):
    return lax.dot_general(a, b, dims, preferred_element_type=F32)


def normalize(x):
    cen = x - jnp.mean(x, axis=-1, keepdims=True)
    inv = lax.rsqrt(jnp.mean(cen * cen, axis=-1, keepdims=True) + LN_EPS)
    return cen * inv, inv


def row_spec(rows, cols, index):
    return pl.BlockSpec((rows, cols), lambda *a: (index(*a), 0))


def half_spec(rows, cols, which, start):
    return pl.BlockSpec((1, rows, cols), lambda j, off: (off[which], start + j, 0))


def both_spec(lead, rows, cols, start):
    zeros = (0,) * len(lead)
    return pl.BlockSpec((*lead, 2, rows, cols), lambda j, off: (*zeros, 0, start + j, 0))


def whole(shape):
    return pl.BlockSpec(shape, lambda *a: (0,) * len(shape), pipeline_mode=pl.Buffered(1))


def sds(shape, dtype):
    return jax.ShapeDtypeStruct(shape, dtype)


def params(**kw):
    return pltpu.CompilerParams(vmem_limit_bytes=64_000_000, **kw)


def cost(flops, nbytes):
    return pl.CostEstimate(flops=int(flops), bytes_accessed=int(nbytes), transcendentals=0)


def project_body(x_ref, g_ref, w_ref, wo_ref, gm_ref, bt_ref, u_ref, q_ref, k_ref, v_ref, do_ref, part_ref, gr, da, qs, ks):
    i = pl.program_id(0)
    rows, cols = q_ref.shape
    groups = cols // GROUP
    do_ref[...] = dot(g_ref[...], wo_ref[...], NT).astype(BF16)
    xh, _ = normalize(x_ref[...].astype(F32))
    u_ref[...] = (xh * gm_ref[...] + bt_ref[...]).astype(BF16)
    u = u_ref[...]
    for e, out in enumerate((q_ref, k_ref, v_ref)):
        out[...] = dot(u, w_ref[e]).astype(BF16)

    def add(acc, s, val):
        acc[s] = jnp.where(i == 0, val, acc[s] + val)

    for s in range(groups):
        c = slice(s * GROUP, (s + 1) * GROUP)
        add(gr, s, dot(q_ref[:, c], k_ref[:, c], TN))
        add(da, s, dot(do_ref[:, c], v_ref[:, c], TN))
    for acc, t in ((qs, q_ref), (ks, k_ref)):
        f = t[...].astype(F32)
        val = jnp.sum((f * f).reshape(rows // 8, 8, cols), axis=0)
        acc[...] = jnp.where(i == 0, val, acc[...] + val)

    @pl.when(i == pl.num_programs(0) - 1)
    def _():
        col_head = lax.broadcasted_iota(jnp.int32, (HEAD, GROUP), 1) // HEAD
        for a, acc in enumerate((gr, da)):
            for s in range(groups):
                tot = jnp.zeros((HEAD, GROUP), F32)
                for h in range(GROUP // HEAD):
                    tot += jnp.where(col_head == h, acc[s, h * HEAD:(h + 1) * HEAD, :], 0.0)
                part_ref[(a * groups + s) * HEAD:(a * groups + s + 1) * HEAD, :] = tot
        base = 2 * groups * HEAD
        for a, acc in enumerate((qs, ks)):
            tot = jnp.sum(acc[...], axis=0, keepdims=True)
            for s in range(groups):
                part_ref[base + 8 * (a * groups + s):base + 8 * (a * groups + s + 1), :] = jnp.broadcast_to(
                    tot[:, s * GROUP:(s + 1) * GROUP], (8, GROUP))


def project(x, g, w3, wo, gamma, beta):
    tokens, width = x.shape
    cols = wo.shape[0]
    groups = cols // GROUP
    part_rows = 2 * groups * (HEAD + 8)
    row = lambda c: row_spec(PROJ_ROWS, c, lambda i: i)
    return pl.pallas_call(
        project_body,
        grid=(tokens // PROJ_ROWS,),
        in_specs=[row(width), row(width), whole(w3.shape), whole(wo.shape), whole((1, width)), whole((1, width))],
        out_specs=[row(width)] + [row(cols)] * 4 + [pl.BlockSpec((part_rows, GROUP), lambda i: (0, 0))],
        out_shape=[sds((tokens, width), BF16)] + [sds((tokens, cols), BF16)] * 4 + [sds((part_rows, GROUP), F32)],
        scratch_shapes=[pltpu.VMEM((groups, GROUP, GROUP), F32)] * 2 + [pltpu.VMEM((8, cols), F32)] * 2,
        name="project",
        compiler_params=params(),
        cost_estimate=cost(2 * tokens * width * cols * 4.4, 2 * tokens * (3 * width + 4 * cols)),
    )(x, g, w3, wo, gamma, beta)


def far_v_body(off_ref, u_ref, w_ref, v_ref):
    v_ref[...] = dot(u_ref[0], w_ref[0]).astype(BF16)


def far_v(off, u2, w3, blocks):
    width, cols = w3.shape[1:]
    rows = 2 * ROWS
    return pl.pallas_call(
        far_v_body,
        grid_spec=pltpu.PrefetchScalarGridSpec(
            num_scalar_prefetch=1,
            grid=(blocks // 2,),
            in_specs=[half_spec(rows, width, 1, 0),
                      pl.BlockSpec((1, width, cols), lambda j, off: (2, 0, 0), pipeline_mode=pl.Buffered(1))],
            out_specs=pl.BlockSpec((rows, cols), lambda j, off: (j, 0)),
        ),
        out_shape=sds((blocks * ROWS, cols), BF16),
        name="far_v",
        compiler_params=params(),
        cost_estimate=cost(2 * blocks * ROWS * width * cols, 2 * blocks * ROWS * (width + cols)),
    )(off, u2, w3)


def state_body(near_ref, far_ref, tau_ref, attn_ref, dgram_ref, coef_ref, dtau_ref, *, groups):
    r_head = lax.broadcasted_iota(jnp.int32, (GROUP, GROUP), 0)
    c_head = lax.broadcasted_iota(jnp.int32, (GROUP, GROUP), 1)
    eye = r_head == c_head
    mask = (r_head // HEAD) == (c_head // HEAD)
    spread = lambda t: jnp.concatenate([t] * (GROUP // HEAD), axis=0)
    to_col = lambda t: jnp.sum(jnp.where(eye, t, 0.0), axis=1, keepdims=True)
    to_row = lambda t: jnp.sum(jnp.where(eye, t, 0.0), axis=0, keepdims=True)
    base = 2 * groups * HEAD
    coef_ref[...] = jnp.zeros_like(coef_ref)
    dtau_ref[...] = jnp.zeros_like(dtau_ref)
    for side, ref in enumerate((near_ref, far_ref)):
        for s in range(groups):
            gram_mat = spread(ref[s * HEAD:(s + 1) * HEAD, :])
            d_attn = spread(ref[(groups + s) * HEAD:(groups + s + 1) * HEAD, :])
            b_row = ref[base + 8 * (groups + s):base + 8 * (groups + s) + 1, :]
            a_col = to_col(ref[base + 8 * s:base + 8 * s + 1, :])
            g = side * groups + s
            tau = to_col(tau_ref[g:g + 1, :])
            norm_prod = jnp.sqrt(a_col) * jnp.sqrt(b_row)
            gram_n = gram_mat / norm_prod
            logit = jnp.where(mask, tau * gram_n, -jnp.inf)
            e = jnp.exp(logit - jnp.max(logit, axis=1, keepdims=True))
            attn = e / jnp.sum(e, axis=1, keepdims=True)
            d_attn = jnp.where(mask, d_attn, 0.0)
            d_logit = jnp.where(mask, attn * (d_attn - jnp.sum(attn * d_attn, axis=1, keepdims=True)), 0.0)
            gram_n = jnp.where(mask, gram_n, 0.0)
            grad_sn = tau * d_logit
            prod = grad_sn * gram_n
            attn_ref[g] = attn.astype(BF16)
            dgram_ref[g] = jnp.where(mask, grad_sn / norm_prod, 0.0).astype(BF16)
            coef_ref[2 * side:2 * side + 1, s * GROUP:(s + 1) * GROUP] = to_row(-jnp.sum(prod, axis=1, keepdims=True) / a_col)
            coef_ref[2 * side + 1:2 * side + 2, s * GROUP:(s + 1) * GROUP] = -jnp.sum(prod, axis=0, keepdims=True) / b_row
            if side == 0:
                dtau_ref[s:s + 1, :] = to_row(jnp.sum(d_logit * gram_n, axis=1, keepdims=True))


def head_state(near, far, tau_rows):
    groups = tau_rows.shape[0] // 2
    vm = pl.BlockSpec(memory_space=pltpu.VMEM)
    return pl.pallas_call(
        functools.partial(state_body, groups=groups),
        in_specs=[vm] * 3,
        out_specs=[vm] * 4,
        out_shape=[sds((2 * groups, GROUP, GROUP), BF16)] * 2 + [sds((8, groups * GROUP), F32), sds((8, GROUP), F32)],
        name="head_state",
        cost_estimate=cost(10**9, 2 * 10**6),
    )(near, far, tau_rows)


def mix_block(q, k, v, do, attn_ref, dgram_ref, coef_ref, side, s):
    groups = attn_ref.shape[0] // 2
    am, gm = attn_ref[side * groups + s], dgram_ref[side * groups + s]
    c = slice(s * GROUP, (s + 1) * GROUP)
    dq = dot(k, gm, NT) + q.astype(F32) * coef_ref[2 * side:2 * side + 1, c]
    dk = dot(q, gm, NN) + k.astype(F32) * coef_ref[2 * side + 1:2 * side + 2, c]
    return dot(v, am, NT).astype(BF16), dq.astype(BF16), dk.astype(BF16), dot(do, am, NN).astype(BF16)


def finish_rows(j, x_ref, g_ref, du, gm_ref, dx_refs, dsum_ref):
    rows, width = x_ref.shape[1:]
    xh, inv = normalize(x_ref[0].astype(F32))
    fold = lambda t: jnp.sum(t.reshape(rows // 8, 8, width), axis=0)
    for a, val in enumerate((fold(du * xh), fold(du))):
        dsum_ref[a] = jnp.where(j == 0, val, dsum_ref[a] + val)
    gh = du * gm_ref[...]
    m1 = jnp.mean(gh, axis=-1, keepdims=True)
    m2 = jnp.mean(gh * xh, axis=-1, keepdims=True)
    dx = (g_ref[0].astype(F32) + inv * (gh - m1 - xh * m2)).astype(BF16)
    for ref in dx_refs:
        ref[0] = dx


def rows_body(*refs, n_alias):
    it = iter(refs)
    nxt = lambda n: [next(it) for _ in range(n)]
    off_ref, x_ref, g_ref, u_ref, q_ref, k_ref, v_ref, do_ref = nxt(8)
    attn_ref, dgram_ref, coef_ref, wn_ref, wf_ref, won_ref, wof_ref, gm_ref = nxt(8)
    nxt(n_alias)
    y_ref, gx_ref, o_ref, rqk_ref, rv_ref, send_ref, dsum_ref = nxt(7)
    on_s, rn_s, of_s, rf_s, qf_s, kf_s, vf_s, dof_s = nxt(8)
    j = pl.program_id(0)
    own, other = off_ref[0], off_ref[1]
    groups = attn_ref.shape[0] // 2
    u = u_ref[0]
    for e, t in enumerate((qf_s, kf_s, vf_s)):
        t[...] = dot(u, wf_ref[e]).astype(BF16)
    dof_s[...] = dot(g_ref[0], wof_ref[...], NT).astype(BF16)
    state = (attn_ref, dgram_ref, coef_ref)
    for s in range(groups):
        c = slice(s * GROUP, (s + 1) * GROUP)
        for half in (own, other):
            o, dq, dk, dv = mix_block(q_ref[half, :, c], k_ref[half, :, c], v_ref[half, :, c], do_ref[half, :, c], *state, 0, s)
            o_ref[half, :, c], rqk_ref[0, half, :, c], rqk_ref[1, half, :, c], rv_ref[half, :, c] = o, dq, dk, dv
            if half is own:
                on_s[:, c], rn_s[0, :, c], rn_s[1, :, c], rn_s[2, :, c] = o, dq, dk, dv
    for s in range(groups):
        c = slice(s * GROUP, (s + 1) * GROUP)
        of_s[:, c], rf_s[0, :, c], rf_s[1, :, c], rf_s[2, :, c] = mix_block(
            qf_s[:, c], kf_s[:, c], vf_s[:, c], dof_s[:, c], *state, 1, s)
    du = dot(rn_s[0], wn_ref[0], NT)
    for e in range(1, 3):
        du += dot(rn_s[e], wn_ref[e], NT)
    for e in range(3):
        du += dot(rf_s[e], wf_ref[e], NT)
    y_ref[0] = (x_ref[0].astype(F32) + (dot(on_s[...], won_ref[...]) + dot(of_s[...], wof_ref[...]))).astype(BF16)
    finish_rows(j, x_ref, g_ref, du, gm_ref, [gx_ref, send_ref], dsum_ref)


def rows_call(off, start, blocks, acts, state, weights, prev):
    _, half, width = acts[0].shape
    cols = weights[2].shape[0]
    row = half_spec(ROWS, width, 0, start)
    both = lambda *lead: both_spec(lead, ROWS, cols, start)
    consts = list(state) + list(weights)
    first = 1 + len(acts) + len(consts)
    return pl.pallas_call(
        functools.partial(rows_body, n_alias=len(prev)),
        grid_spec=pltpu.PrefetchScalarGridSpec(
            num_scalar_prefetch=1,
            grid=(blocks,),
            in_specs=[row] * 3 + [both()] * 4 + [whole(t.shape) for t in consts] + [pl.BlockSpec(memory_space=pl.ANY)] * len(prev),
            out_specs=[row, row, both(), both(2), both(),
                       pl.BlockSpec((1, ROWS, width), lambda j, off: (0, j, 0)),
                       pl.BlockSpec((2, 8, width), lambda j, off: (0, 0, 0))],
            scratch_shapes=[pltpu.VMEM((ROWS, cols), BF16), pltpu.VMEM((3, ROWS, cols), BF16)] * 2 + [pltpu.VMEM((ROWS, cols), BF16)] * 4,
        ),
        out_shape=[sds((2, half, width), BF16)] * 2 + [sds((2, half, cols), BF16), sds((2, 2, half, cols), BF16), sds((2, half, cols), BF16),
                                                       sds((1, blocks * ROWS, width), BF16), sds((2, 8, width), F32)],
        input_output_aliases={first + a: a for a in range(len(prev))},
        name="rows",
        compiler_params=params(),
        cost_estimate=cost(2 * blocks * ROWS * width * cols * 13, 2 * blocks * ROWS * (6 * width + 16 * cols)),
    )(off, *acts, *consts, *prev)


def far_y_body(off_ref, x_ref, o_ref, vu_ref, *refs, fused):
    it = iter(refs)
    nxt = lambda n: [next(it) for _ in range(n)]
    attn_ref, won_ref, wof_ref = nxt(3)
    if fused:
        (wv_ref,) = nxt(1)
    _, y_ref, of_s = nxt(3)
    if fused:
        vf_ref = nxt(1)[0]
        vf_ref[...] = dot(vu_ref[0], wv_ref[0]).astype(BF16)
    else:
        vf_ref = vu_ref
    groups = attn_ref.shape[0] // 2
    for s in range(groups):
        c = slice(s * GROUP, (s + 1) * GROUP)
        of_s[:, c] = dot(vf_ref[:, c], attn_ref[groups + s], NT).astype(BF16)
    y_ref[0] = (x_ref[0].astype(F32) + (dot(o_ref[0], won_ref[...]) + dot(of_s[...], wof_ref[...]))).astype(BF16)


def far_y(off, start, blocks, x2, o2, vu, attn, wo_near, wo_far, w_far, y2):
    fused = vu.ndim == 3
    width, cols = x2.shape[2], o2.shape[2]
    row = lambda c: half_spec(ROWS, c, 1, start)
    args = [x2, o2, vu, attn, wo_near, wo_far]
    specs = [row(width), row(cols), row(width) if fused else pl.BlockSpec((ROWS, cols), lambda j, off: (start + j, 0)),
             whole(attn.shape), whole(wo_near.shape), whole(wo_far.shape)]
    if fused:
        args.append(w_far)
        specs.append(pl.BlockSpec((1, width, cols), lambda j, off: (2, 0, 0), pipeline_mode=pl.Buffered(1)))
    return pl.pallas_call(
        functools.partial(far_y_body, fused=fused),
        grid_spec=pltpu.PrefetchScalarGridSpec(
            num_scalar_prefetch=1,
            grid=(blocks,),
            in_specs=specs + [pl.BlockSpec(memory_space=pl.ANY)],
            out_specs=row(width),
            scratch_shapes=[pltpu.VMEM((ROWS, cols), BF16)] * (2 if fused else 1),
        ),
        out_shape=sds(y2.shape, y2.dtype),
        input_output_aliases={len(args) + 1: 0},
        name="far_y",
        compiler_params=params(),
        cost_estimate=cost(2 * blocks * ROWS * width * cols * (3.2 if fused else 2.2), 2 * blocks * ROWS * (2 * width + 2 * cols)),
    )(off, *args, y2)


def solution(mesh):
    tp_size = mesh.shape["tp"]
    sp_size = mesh.shape["sp"]
    in_rows = P(("dp", "sp"), None)
    swap = [(0, 1), (1, 0)]

    def exchange(t):
        return lax.ppermute(t, "tp", swap)

    def step(x, g, w_qkv, w_out, ln_gamma, ln_beta, temps):
        tokens, width = x.shape
        cols = w_qkv.shape[2]
        groups = cols // GROUP
        me = lax.axis_index("tp")
        w_near = jnp.transpose(w_qkv, (1, 0, 2))
        w_far = exchange(w_near)
        wo_far = exchange(w_out)
        gamma, beta = ln_gamma.reshape(1, width), ln_beta.reshape(1, width)
        half = tokens // 2
        off = jnp.stack([me, 1 - me]).astype(jnp.int32)
        halves = lambda t: t.reshape(2, half, t.shape[-1])

        u, q, k, v, do, part = project(x, g, w_near, w_out, gamma, beta)
        x2, g2, u2 = halves(x), halves(g), halves(u)
        near = tuple(halves(t) for t in (q, k, v, do))
        peers = [lax.ppermute(part, "sp", [(s, s ^ d) for s in range(sp_size)]) for d in (1, 2, 3)]
        part = (part + peers[0]) + (peers[1] + peers[2])
        part_far = exchange(part)
        vf0 = far_v(off, u2, w_far, EARLY_V)
        tau = jnp.repeat(temps, HEAD).reshape(tp_size, groups, GROUP)
        tau = jnp.where(me == 0, tau, tau[::-1]).reshape(2 * groups, GROUP)
        attn, dgram, coef, dtau = head_state(part, part_far, tau)
        state = (attn, dgram, coef)
        dtau = jnp.sum(dtau[:groups].reshape(groups * GROUP // HEAD, HEAD), axis=1)
        dtau_far = exchange(dtau)
        grad_temp = jnp.where(me == 0, jnp.concatenate([dtau, dtau_far]), jnp.concatenate([dtau_far, dtau]))

        prev, dsum, recv, start = (), None, [], 0
        for blocks in OWN_CHUNKS:
            *prev, sent, ds = rows_call(off, start, blocks, (x2, g2, u2) + near, state, (w_near, w_far, w_out, wo_far, gamma), prev)
            recv.append((start, exchange(sent)))
            dsum = ds if dsum is None else dsum + ds
            start += blocks
        y2, gx2, o2, rqk, rv = prev

        dw_qk = lax.dot_general(u, rqk.reshape(2, tokens, cols), (((0,), (1,)), ((), ())), preferred_element_type=F32)
        o2, dw_qk = lax.optimization_barrier((o2, dw_qk))
        dw_qk = lax.psum_scatter(dw_qk, "sp", scatter_dimension=0, tiled=True)
        dw_o = dot(o2.reshape(tokens, cols), g, TN)
        rv, dw_o = lax.optimization_barrier((rv, dw_o))
        grad_wout = lax.psum_scatter(dw_o, "sp", scatter_dimension=0, tiled=True)
        dw_v = dot(u, rv.reshape(tokens, cols), TN)
        y2, dw_v = lax.optimization_barrier((y2, dw_v))
        dw_v = lax.psum_scatter(dw_v, "sp", scatter_dimension=0, tiled=True)
        y2 = far_y(off, 0, EARLY_V, x2, o2, vf0, attn, w_out, wo_far, w_far, y2)
        y2 = far_y(off, EARLY_V, half // ROWS - EARLY_V, x2, o2, u2, attn, w_out, wo_far, w_far, y2)
        grad_wqkv = jnp.concatenate([dw_qk, dw_v[:, None]], axis=1)

        sums = jnp.sum(dsum, axis=1)
        for axis, perm in (("tp", swap), ("sp", [(s, s ^ 1) for s in range(sp_size)]), ("sp", [(s, s ^ 2) for s in range(sp_size)])):
            sums = sums + lax.ppermute(sums, axis, perm)
        for start, blk in recv:
            gx2 = lax.dynamic_update_slice(gx2, blk, (off[1], start * ROWS, 0))
        return y2.reshape(tokens, width), gx2.reshape(tokens, width), grad_wqkv, grad_wout, sums[0], sums[1], grad_temp

    in_specs = (in_rows, in_rows, P(None, None, "tp"), P("tp", None), P(None), P(None), P(None))
    out_specs = (in_rows, in_rows, P(("dp", "sp"), None, "tp"), P(("dp", "tp", "sp"), None), P("dp"), P("dp"), P("dp"))
    return jax.shard_map(step, mesh=mesh, in_specs=in_specs, out_specs=out_specs, check_vma=False)
```

time: 1310 us -> 1360 us (1.038)
  waiting for transfers between devices: 59.4 us -> 455 us
  blocking collectives: 269 us -> 0 us
  Pallas kernels: 728 us -> 646 us
    psum x1 -> x0, blocking collectives: 269 us -> none  [step(): sums = lax.psum(jnp.sum(dsum + 0.5 * ds, axis=1), ('tp', 'sp'))]
    ppermute x7 -> x8, waiting for transfers between devices: 44.5 us -> 310 us  [exchange(): return lax.ppermute(t, 'tp', swap)]
    ppermute x1 -> x3, waiting for transfers between devices: 3.29 us -> 133 us  [step(): sums = sums + lax.ppermute(sums, axis, perm)]
    pallas_call x7 -> x6, Pallas kernels: 502 us -> 429 us  [the longest x4 354 us: rows_call(): pl.pallas_call(functools.partial(rows_body, n_alias=len(prev)), grid_spec...]
    dot_general x1, matrix products: 141 us -> 88.8 us  [step(): lax.dot_general(u, rqk.reshape(2, tokens, cols), (((0,), (1,)), ((), ()))...]
    dot_general x1 -> x2, matrix products: 46.8 us -> 94.1 us  [dot(): return lax.dot_general(a, b, dims, preferred_element_type=F32)]
  transfers between devices with their start and end apart: 13 -> 17, of which waited for: 4 -> 6; matrix products, arithmetic and copies ran while one was open for 2% -> 3% of each run, Pallas kernels for 29% -> 22%
where the time goes in v3:
time: 1360 us; the launch traced here: 1350 us
  Pallas kernels  646 us (48%)
  waiting for transfers between devices  455 us (33%)
  matrix products  183 us (13%)
  local copies, waits for them, and re-layouts  28.5 us (2%)
  starting transfers between devices  16.6 us (1%)
  between operations  14.4 us (1%)
    pallas_call x4, Pallas kernels, rows_call(): pl.pallas_call(functools.partial(rows_body, n_alias=len(prev)), grid_spec...  354 us
    ppermute x8, waiting for transfers between devices, exchange(): return lax.ppermute(t, 'tp', swap)  310 us
    pallas_call x1, Pallas kernels, project(): pl.pallas_call(project_body, grid=(tokens // PROJ_ROWS,), in_specs=[row(w...  199 us
    ppermute x3, waiting for transfers between devices, step(): sums = sums + lax.ppermute(sums, axis, perm)  133 us
    dot_general x2, matrix products, dot(): return lax.dot_general(a, b, dims, preferred_element_type=F32)  94.1 us
    dot_general x1, matrix products, step(): lax.dot_general(u, rqk.reshape(2, tokens, cols), (((0,), (1,)), ((), ()))...  88.8 us
    pallas_call x2, Pallas kernels, far_y(): pl.pallas_call(functools.partial(far_y_body, fused=fused), grid_spec=pltp...  75.2 us
  transfers between devices with their start and end apart: 17, of which 6 were waited for; matrix products, arithmetic and copies ran while one was open for 3% of the time, Pallas kernels for 22%

profile of v3, /device:TPU:0, one launch (start us, length us, event | category | flops | bytes accessed | tf_op | source)
XLA Modules:
  0.0 1350.7 jit_solution(14738637682066810864)
XLA Ops:
  7.2 0.0 reduce-scatter.6.cloned.1.call-start
  7.2 3.4 collective-permute-start.4
  10.6 0.0 collective-permute-start.5
  10.6 1.3 reshape.66.gm_ref.refs_15_
  11.9 1.3 reshape.67.bt_ref
  13.2 198.8 %project.1 = (bf16[16384,1536]{1,0:T(8,128)(2,1)}, bf16[16384,768]{1,0:T(8,128)(2,1)}, bf16[16384,768]{1,0:T(8,128)(2,1)}, bf16[16384,768]{1,0:T(8,128)(2,1)}, b...) custom-call(bf16[16384,1536]{1,0:T(8,128)(2,1)} %x_ref.1, bf16[16384,1536]{1,0:T(8,128)(2,1)} %g_ref.1, ...), custom_call_target="tpu_custom_call" | custom-call | flops 170080698368 | bytes 251658240 | tf_op jit(solution)/shard_map/project/pallas_call | solution.py:110
  212.1 0.0 collective-permute-start
  212.1 2.0 collective-permute-start.1
  214.1 0.1 collective-permute-start.2
  214.2 0.1 broadcast_in_dim.10
  214.2 0.1 broadcast_in_dim.11
  214.3 0.1 broadcast_in_dim.12
  214.4 0.1 rev.3
  214.5 0.0 collective-permute-done
  214.5 6.6 collective-permute-done.1
  221.1 4.7 collective-permute-done.2
  225.9 1.0 add_add_fusion.near_ref
  226.9 0.0 copy-start
  226.9 1.6 collective-permute-start.3
  228.5 0.6 reshape.73.tau_ref
  229.1 0.6 pad_add_fusion.refs_0_.off_ref
  229.7 5.2 collective-permute-done.3.far_ref
  234.9 0.7 copy-done.7
  235.6 4.5 head_state.1
  240.1 0.0 collective-permute-done.5.refs_14_.refs_2_
  240.1 0.0 collective-permute-done.4.refs_12_.w_ref.refs_3_
  240.1 49.9 %rows.4 = (bf16[2,8192,1536]{2,1,0:T(8,128)(2,1)}, bf16[2,8192,1536]{2,1,0:T(8,128)(2,1)}, bf16[2,8192,768]{2,1,0:T(8,128)(2,1)}, bf16[2,2,8192,768]{3,2,1,0:T(8...) custom-call(s32[2]{0:T(128)} %pad_add_fusion.refs_0_.off_ref, ...), custom_call_target="tpu_custom_call" | custom-call | flops 31406948352 | bytes 44040192 | tf_op jit(solution)/shard_map/rows/pallas_call | solution.py:262
  290.0 69.2 %rows.5 = (bf16[2,8192,1536]{2,1,0:T(8,128)(2,1)}, bf16[2,8192,1536]{2,1,0:T(8,128)(2,1)}, bf16[2,8192,768]{2,1,0:T(8,128)(2,1)}, bf16[2,2,8192,768]{3,2,1,0:T(8...) custom-call(s32[2]{0:T(128)} %pad_add_fusion.refs_0_.off_ref, ...), custom_call_target="tpu_custom_call", output_to_operand_aliasing={{0}: (16, {}), {1}: (17, {}), {2}: (18, {}), {3}: (19, {}),... | custom-call | flops 47110422528 | bytes 66060288 | tf_op jit(solution)/shard_map/rows/pallas_call | solution.py:262
  359.2 98.3 %rows.6 = (bf16[2,8192,1536]{2,1,0:T(8,128)(2,1)}, bf16[2,8192,1536]{2,1,0:T(8,128)(2,1)}, bf16[2,8192,768]{2,1,0:T(8,128)(2,1)}, bf16[2,2,8192,768]{3,2,1,0:T(8...) custom-call(s32[2]{0:T(128)} %pad_add_fusion.refs_0_.off_ref, ...), custom_call_target="tpu_custom_call", output_to_operand_aliasing={{0}: (16, {}), {1}: (17, {}), {2}: (18, {}), {3}: (19, {}),... | custom-call | flops 70665633792 | bytes 99090432 | tf_op jit(solution)/shard_map/rows/pallas_call | solution.py:262
  457.5 136.5 %rows.7 = (bf16[2,8192,1536]{2,1,0:T(8,128)(2,1)}, bf16[2,8192,1536]{2,1,0:T(8,128)(2,1)}, bf16[2,8192,768]{2,1,0:T(8,128)(2,1)}, bf16[2,2,8192,768]{3,2,1,0:T(8...) custom-call(s32[2]{0:T(128)} %pad_add_fusion.refs_0_.off_ref, ...), custom_call_target="tpu_custom_call", output_to_operand_aliasing={{0}: (16, {}), {1}: (17, {}), {2}: (18, {}), {3}: (19, {}),... | custom-call | flops 102072582144 | bytes 143130624 | tf_op jit(solution)/shard_map/rows/pallas_call | solution.py:262
  594.0 88.8 %fusion = f32[1536,2,768]{2,0,1:T(8,128)} fusion(bf16[2,16384,768]{2,1,0:T(8,128)(2,1)} %bitcast.47, bf16[16384,1536]{1,0:T(8,128)(2,1)} %get-tuple-element.51), kind=kOutput, calls=%fused_computation | convolution fusion | flops 77309411328 | bytes 110100480 | tf_op jit(solution)/shard_map/dot_general | solution.py:373
  682.8 47.0 %fusion.2 = f32[768,1536]{1,0:T(8,128)} fusion(bf16[16384,768]{1,0:T(8,128)(2,1)} %bitcast.45, bf16[16384,1536]{1,0:T(8,128)(2,1)} %g_ref.1), kind=kOutput, calls=%fused_computation.14 | convolution fusion | flops 38654705664 | bytes 80216064 | tf_op jit(solution)/shard_map/dot_general | solution.py:26
  729.9 47.1 %fusion.3 = f32[1536,768]{1,0:T(8,128)} fusion(bf16[16384,1536]{1,0:T(8,128)(2,1)} %get-tuple-element.51, bf16[16384,768]{1,0:T(8,128)(2,1)} %bitcast.64), kind=kOutput, calls=%fused_computation.15 | convolution fusion | flops 38654705664 | bytes 80216064 | tf_op jit(solution)/shard_map/dot_general | solution.py:26
  776.9 0.0 reduce-scatter.6.cloned.1.call-update
  777.0 0.0 reduce-scatter.4.cloned.1.call-start
  777.0 0.7 reduce-scatter.4.cloned.1.call-update
  777.7 0.0 reduce-scatter.8.cloned.1.call-start
  777.8 1.8 collective-permute-start.9
  779.6 0.1 reshape.79
  779.7 0.1 reduce_sum.19
  779.8 0.2 collective-permute-start.13
  780.0 1.8 collective-permute-start.8
  781.8 218.9 %collective-permute-done.13 = f32[24]{0:T(128)S(1)} collective-permute-done((f32[24]{0:T(128)S(1)}, f32[24]{0:T(128)S(1)}, u32[]{:S(2)}, u32[]{:S(2)}) %collective-permute-start.13) | collective-permute-done | bytes 128 | tf_op jit(solution)/shard_map/ppermute | solution.py:335
  1000.8 0.6 broadcast_select_fusion.1
  1001.3 0.0 reduce-scatter.8.cloned.1.call-update
  1001.4 0.1 add_reduce_fusion
  1001.5 1.8 collective-permute-start.10
  1003.3 0.2 collective-permute-start.6
  1003.5 1.8 collective-permute-start.7
  1005.3 13.8 %far_v.1.vu_ref = bf16[3072,768]{1,0:T(8,128)(2,1)} custom-call(s32[2]{0:T(128)} %pad_add_fusion.refs_0_.off_ref, bf16[2,8192,1536]{2,1,0:T(8,128)(2,1)} %bitcast.32, bf16[3,1536,768]{2,1,0:T(8,128)(2,1)} %collective-permute-done.4.refs_12_.w_ref.refs_3_), custom_call_target="tpu_custom_call" | custom-call | flops 7247757312 | bytes 14155776 | tf_op jit(solution)/shard_map/far_v/pallas_call | solution.py:130
  1019.1 133.5 %collective-permute-done.10 = f32[2,1536]{1,0:T(2,128)S(1)} collective-permute-done((f32[2,1536]{1,0:T(2,128)S(1)}, f32[2,1536]{1,0:T(2,128)S(1)}, u32[]{:S(2)}, u32[]{:S(2)}) %collective-permute-start.10) | collective-permute-done | bytes 12320 | tf_op jit(solution)/shard_map/ppermute | solution.py:388
  1152.6 0.0 collective-permute-start.11
  1152.6 23.9 %far_y.2.refs_4_ = bf16[2,8192,1536]{2,1,0:T(8,128)(2,1)} custom-call(s32[2]{0:T(128)} %pad_add_fusion.refs_0_.off_ref, bf16[2,8192,1536]{2,1,0:T(8,128)(2,1)} %bitcast.38, bf16[2,8192,768]{2,1,0:T(8,128)(2,1)} %get-tuple-element.77.o_ref, bf16[3072,768]{1,0:T(8,128)(2,1)} %far_v.1.vu_ref, ...), custom_call_target="tpu_custom_call", output_to_operand_aliasing={{}: (7, {})} | custom-call | flops 15945066496 | bytes 28311552 | tf_op jit(solution)/shard_map/far_y/pallas_call | solution.py:311
  1176.6 1.7 collective-permute-start.12
  1178.3 51.3 %far_y.3 = bf16[2,8192,1536]{2,1,0:T(8,128)(2,1)} custom-call(s32[2]{0:T(128)} %pad_add_fusion.refs_0_.off_ref, bf16[2,8192,1536]{2,1,0:T(8,128)(2,1)} %bitcast.39, bf16[2,8192,768]{2,1,0:T(8,128)(2,1)} %get-tuple-element.77.o_ref, bf16[2,8192,1536]{2,1,0:T(8,128)(2,1)} %bitcast.33, ...), custom_call_target="tpu_custom_call", output_to_operand_aliasing={{}: (8, {})} | custom-call | flops 38654705664 | bytes 47185920 | tf_op jit(solution)/shard_map/far_y/pallas_call | solution.py:311
  1229.5 0.0 collective-permute-done.12
  1229.6 0.6 slice_reduce_fusion
  1230.2 3.8 constant_dynamic-update-slice_fusion.3
  1233.9 85.8 %collective-permute-done.7 = bf16[1,1536,1536]{2,1,0:T(8,128)(2,1)} collective-permute-done((bf16[1,1536,1536]{2,1,0:T(8,128)(2,1)}, bf16[1,1536,1536]{2,1,0:T(8,128)(2,1)}, u32[]{:S(2)}, u32[]{:S(2)}) %collective-permute-start.7) | collective-permute-done | bytes 4718624 | tf_op jit(solution)/shard_map/ppermute | solution.py:335
  1319.8 4.8 constant_dynamic-update-slice_fusion.2
  1324.6 0.0 collective-permute-done.8
  1324.6 6.4 constant_dynamic-update-slice_fusion.1
  1331.0 8.6 constant_dynamic-update-slice_fusion
  1339.6 4.1 pad_maximum_fusion
  (27 shorter events, 0.1 us)
Async XLA Ops:
  7.2 1332.4 %reduce-scatter.6.cloned.1.call-start = ((), (), s32[]{:S(2)}) async-start(), calls=%async_computation.4 | async-start | bytes 5898240 | tf_op jit(solution)/shard_map/reduce_scatter | solution.py:381
  7.2 232.9 %collective-permute-start.4 = (bf16[3,1536,768]{2,1,0:T(8,128)(2,1)}, bf16[3,1536,768]{2,1,0:T(8,128)(2,1)}, u32[]{:S(2)}, u32[]{:S(2)}) collective-permute-start(bf16[3,1536,768]{2,1,0:T(8,128)(2,1)} %bitcast.65), channel_id=1, source_target_pairs={{0,4},{4,0},{1,5},{5,1},{2,6},{6,2},{3,7},{7,3}} | collective-permute-start | bytes 21233672 | tf_op jit(solution)/shard_map/ppermute | solution.py:335
  10.6 229.5 %collective-permute-start.5 = (bf16[768,1536]{1,0:T(8,128)(2,1)}, bf16[768,1536]{1,0:T(8,128)(2,1)}, u32[]{:S(2)}, u32[]{:S(2)}) collective-permute-start(bf16[768,1536]{1,0:T(8,128)(2,1)} %refs_1_.3), channel_id=1, source_target_pairs={{0,4},{4,0},{1,5},{5,1},{2,6},{6,2},{3,7},{7,3}} | collective-permute-start | bytes 7077896 | tf_op jit(solution)/shard_map/ppermute | solution.py:335
  13.2 201.0 %copy-start.6 = (f32[48]{0:T(128)S(1)}, f32[48]{0:T(128)}, u32[]{:S(2)}) copy-start(f32[48]{0:T(128)} %param.13) | copy-start | bytes 580
  212.1 2.5 collective-permute-start
  212.1 9.1 collective-permute-start.1
  214.1 11.8 collective-permute-start.2
  226.9 8.0 copy-start
  226.9 8.0 collective-permute-start.3
  234.9 0.7 copy-start.7
  729.8 49.8 %copy-start.5 = (f32[8,256]{1,0:T(8,128)S(1)}, f32[8,256]{1,0:T(8,128)}, u32[]{:S(2)}) copy-start(f32[8,256]{1,0:T(8,128)} %get-tuple-element.94) | copy-start | bytes 24580
  729.8 271.5 %copy-start.1 = (f32[2,8,1536]{2,1,0:T(8,128)S(1)}, f32[2,8,1536]{2,1,0:T(8,128)}, u32[]{:S(2)}) copy-start(f32[2,8,1536]{2,1,0:T(8,128)} %get-tuple-element.90) | copy-start | bytes 294916
  729.8 271.5 %copy-start.2 = (f32[2,8,1536]{2,1,0:T(8,128)S(1)}, f32[2,8,1536]{2,1,0:T(8,128)}, u32[]{:S(2)}) copy-start(f32[2,8,1536]{2,1,0:T(8,128)} %get-tuple-element.91) | copy-start | bytes 294916
  729.8 271.6 %copy-start.3 = (f32[2,8,1536]{2,1,0:T(8,128)S(1)}, f32[2,8,1536]{2,1,0:T(8,128)}, u32[]{:S(2)}) copy-start(f32[2,8,1536]{2,1,0:T(8,128)} %get-tuple-element.92) | copy-start | bytes 294916
  729.8 271.6 %copy-start.4 = (f32[2,8,1536]{2,1,0:T(8,128)S(1)}, f32[2,8,1536]{2,1,0:T(8,128)}, u32[]{:S(2)}) copy-start(f32[2,8,1536]{2,1,0:T(8,128)} %get-tuple-element.93) | copy-start | bytes 294916
  777.0 562.6 %reduce-scatter.4.cloned.1.call-start = ((), (), s32[]{:S(2)}) async-start(), calls=%async_computation.3 | async-start | bytes 11796480 | tf_op jit(solution)/shard_map/reduce_scatter | solution.py:375
  777.7 565.9 %reduce-scatter.8.cloned.1.call-start = ((), (), s32[]{:S(2)}) async-start(), calls=%async_computation.5 | async-start | bytes 5898240 | tf_op jit(solution)/shard_map/reduce_scatter | solution.py:378
  777.8 553.3 %collective-permute-start.9 = (bf16[1,3328,1536]{2,1,0:T(8,128)(2,1)}, bf16[1,3328,1536]{2,1,0:T(8,128)(2,1)}, u32[]{:S(2)}, u32[]{:S(2)}) collective-permute-start(bf16[1,3328,1536]{2,1,0:T(8,128)(2,1)} %get-tuple-element.86), channel_id=1, source_target_pairs={{0,4},{4,0},{1,5},{5,1},{2,6},{6,2},{3,7},{7,3}} | collective-permute-start | bytes 30670856 | tf_op jit(solution)/shard_map/ppermute | solution.py:335
  779.8 221.0 %collective-permute-start.13 = (f32[24]{0:T(128)S(1)}, f32[24]{0:T(128)S(1)}, u32[]{:S(2)}, u32[]{:S(2)}) collective-permute-start(f32[24]{0:T(128)S(1)} %reduce_sum.19), channel_id=1, source_target_pairs={{0,4},{4,0},{1,5},{5,1},{2,6},{6,2},{3,7},{7,3}} | collective-permute-start | bytes 296 | tf_op jit(solution)/shard_map/ppermute | solution.py:335
  780.0 544.6 %collective-permute-start.8 = (bf16[1,2304,1536]{2,1,0:T(8,128)(2,1)}, bf16[1,2304,1536]{2,1,0:T(8,128)(2,1)}, u32[]{:S(2)}, u32[]{:S(2)}) collective-permute-start(bf16[1,2304,1536]{2,1,0:T(8,128)(2,1)} %get-tuple-element.85), channel_id=1, source_target_pairs={{0,4},{4,0},{1,5},{5,1},{2,6},{6,2},{3,7},{7,3}} | collective-permute-start | bytes 21233672 | tf_op jit(solution)/shard_map/ppermute | solution.py:335
  1001.5 151.1 %collective-permute-start.10 = (f32[2,1536]{1,0:T(2,128)S(1)}, f32[2,1536]{1,0:T(2,128)S(1)}, u32[]{:S(2)}, u32[]{:S(2)}) collective-permute-start(f32[2,1536]{1,0:T(2,128)S(1)} %add_reduce_fusion), channel_id=1, source_target_pairs={{0,4},{4,0},{1,5},{5,1},{2,6},{6,2},{3,7},{7,3}} | collective-permute-start | bytes 36872 | tf_op jit(solution)/shard_map/ppermute | solution.py:388
  1003.3 226.9 %collective-permute-start.6 = (bf16[1,1024,1536]{2,1,0:T(8,128)(2,1)}, bf16[1,1024,1536]{2,1,0:T(8,128)(2,1)}, u32[]{:S(2)}, u32[]{:S(2)}) collective-permute-start(bf16[1,1024,1536]{2,1,0:T(8,128)(2,1)} %get-tuple-element.83), channel_id=1, source_target_pairs={{0,4},{4,0},{1,5},{5,1},{2,6},{6,2},{3,7},{7,3}} | collective-permute-start | bytes 9437192 | tf_op jit(solution)/shard_map/ppermute | solution.py:335
  1003.5 316.3 %collective-permute-start.7 = (bf16[1,1536,1536]{2,1,0:T(8,128)(2,1)}, bf16[1,1536,1536]{2,1,0:T(8,128)(2,1)}, u32[]{:S(2)}, u32[]{:S(2)}) collective-permute-start(bf16[1,1536,1536]{2,1,0:T(8,128)(2,1)} %get-tuple-element.84), channel_id=1, source_target_pairs={{0,4},{4,0},{1,5},{5,1},{2,6},{6,2},{3,7},{7,3}} | collective-permute-start | bytes 14155784 | tf_op jit(solution)/shard_map/ppermute | solution.py:335
  1152.6 23.9 %collective-permute-start.11 = (f32[2,1536]{1,0:T(2,128)S(1)}, f32[2,1536]{1,0:T(2,128)S(1)}, u32[]{:S(2)}, u32[]{:S(2)}) collective-permute-start(f32[2,1536]{1,0:T(2,128)S(1)} %add.47), channel_id=1, source_target_pairs={{0,1},{1,0},{2,3},{3,2},{4,5},{5,4},{6,7},{7,6}} | collective-permute-start | bytes 36872 | tf_op jit(solution)/shard_map/ppermute | solution.py:388
  1176.6 53.0 %collective-permute-start.12 = (f32[2,1536]{1,0:T(2,128)S(1)}, f32[2,1536]{1,0:T(2,128)S(1)}, u32[]{:S(2)}, u32[]{:S(2)}) collective-permute-start(f32[2,1536]{1,0:T(2,128)S(1)} %add.48), channel_id=1, source_target_pairs={{0,2},{1,3},{2,0},{3,1},{4,6},{5,7},{6,4},{7,5}} | collective-permute-start | bytes 36872 | tf_op jit(solution)/shard_map/ppermute | solution.py:388
Sparse Core Ops, SparseCore 0:
  777.1 43.6 reduce-scatter.5
  823.4 72.3 reduce-scatter.3
  1001.5 43.6 reduce-scatter.7

commit v4 on v3

--- a/solution.py
+++ b/solution.py
@@ -11,6 +11,7 @@
 LN_EPS = 1e-6
 GROUP = 256
 HEAD = 32
+LANES = 128
 F32 = jnp.float32
 BF16 = jnp.bfloat16
 NN = (((1,), (0,)), ((), ()))
@@ -18,7 +19,8 @@
 TN = (((0,), (0,)), ((), ()))
 PROJ_ROWS = 512
 ROWS = 256
-OWN_CHUNKS = (4, 6, 9, 13)
+SUM_ROWS = 1024
+OWN_CHUNKS = ((4,), (6,), (10,), (8, 4))
 EARLY_V = 12
 
 
@@ -27,9 +29,10 @@
 
 
 def normalize(x):
-    cen = x - jnp.mean(x, axis=-1, keepdims=True)
+    mean = jnp.mean(x, axis=-1, keepdims=True)
+    cen = x - mean
     inv = lax.rsqrt(jnp.mean(cen * cen, axis=-1, keepdims=True) + LN_EPS)
-    return cen * inv, inv
+    return cen * inv, mean, inv
 
 
 def row_spec(rows, cols, index):
@@ -61,13 +64,14 @@
     return pl.CostEstimate(flops=int(flops), bytes_accessed=int(nbytes), transcendentals=0)
 
 
-def project_body(x_ref, g_ref, w_ref, wo_ref, gm_ref, bt_ref, u_ref, q_ref, k_ref, v_ref, do_ref, part_ref, gr, da, qs, ks):
+def project_body(x_ref, g_ref, w_ref, wo_ref, gm_ref, bt_ref, u_ref, q_ref, k_ref, v_ref, do_ref, st_ref, part_ref, gr, da, qs, ks):
     i = pl.program_id(0)
     rows, cols = q_ref.shape
     groups = cols // GROUP
     do_ref[...] = dot(g_ref[...], wo_ref[...], NT).astype(BF16)
-    xh, _ = normalize(x_ref[...].astype(F32))
+    xh, mean, inv = normalize(x_ref[...].astype(F32))
     u_ref[...] = (xh * gm_ref[...] + bt_ref[...]).astype(BF16)
+    st_ref[...] = jnp.where(lax.broadcasted_iota(jnp.int32, st_ref.shape, 1) < LANES // 2, mean, inv)
     u = u_ref[...]
     for e, out in enumerate((q_ref, k_ref, v_ref)):
         out[...] = dot(u, w_ref[e]).astype(BF16)
@@ -111,8 +115,8 @@
         project_body,
         grid=(tokens // PROJ_ROWS,),
         in_specs=[row(width), row(width), whole(w3.shape), whole(wo.shape), whole((1, width)), whole((1, width))],
-        out_specs=[row(width)] + [row(cols)] * 4 + [pl.BlockSpec((part_rows, GROUP), lambda i: (0, 0))],
-        out_shape=[sds((tokens, width), BF16)] + [sds((tokens, cols), BF16)] * 4 + [sds((part_rows, GROUP), F32)],
+        out_specs=[row(width)] + [row(cols)] * 4 + [row(LANES), pl.BlockSpec((part_rows, GROUP), lambda i: (0, 0))],
+        out_shape=[sds((tokens, width), BF16)] + [sds((tokens, cols), BF16)] * 4 + [sds((tokens, LANES), F32), sds((part_rows, GROUP), F32)],
         scratch_shapes=[pltpu.VMEM((groups, GROUP, GROUP), F32)] * 2 + [pltpu.VMEM((8, cols), F32)] * 2,
         name="project",
         compiler_params=params(),
@@ -120,27 +124,30 @@
     )(x, g, w3, wo, gamma, beta)
 
 
-def far_v_body(off_ref, u_ref, w_ref, v_ref):
-    v_ref[...] = dot(u_ref[0], w_ref[0]).astype(BF16)
-
-
-def far_v(off, u2, w3, blocks):
+def far_v_body(off_ref, u_ref, w_ref, *refs):
+    refs[-1][...] = dot(u_ref[0], w_ref[0]).astype(BF16)
+
+
+def far_v(off, u2, w3, blocks, part, parts, prev=()):
     width, cols = w3.shape[1:]
     rows = 2 * ROWS
+    steps = blocks * ROWS // rows // parts
     return pl.pallas_call(
         far_v_body,
         grid_spec=pltpu.PrefetchScalarGridSpec(
             num_scalar_prefetch=1,
-            grid=(blocks // 2,),
-            in_specs=[half_spec(rows, width, 1, 0),
-                      pl.BlockSpec((1, width, cols), lambda j, off: (2, 0, 0), pipeline_mode=pl.Buffered(1))],
-            out_specs=pl.BlockSpec((rows, cols), lambda j, off: (j, 0)),
+            grid=(steps,),
+            in_specs=[half_spec(rows, width, 1, part * steps),
+                      pl.BlockSpec((1, width, cols), lambda j, off: (2, 0, 0), pipeline_mode=pl.Buffered(1))]
+            + [pl.BlockSpec(memory_space=pl.ANY)] * len(prev),
+            out_specs=pl.BlockSpec((rows, cols), lambda j, off: (part * steps + j, 0)),
         ),
         out_shape=sds((blocks * ROWS, cols), BF16),
+        input_output_aliases={3: 0} if prev else {},
         name="far_v",
         compiler_params=params(),
-        cost_estimate=cost(2 * blocks * ROWS * width * cols, 2 * blocks * ROWS * (width + cols)),
-    )(off, u2, w3)
+        cost_estimate=cost(2 * steps * rows * width * cols, 2 * steps * rows * (width + cols)),
+    )(off, u2, w3, *prev)
 
 
 def state_body(near_ref, far_ref, tau_ref, attn_ref, dgram_ref, coef_ref, dtau_ref, *, groups):
@@ -176,8 +183,7 @@
             dgram_ref[g] = jnp.where(mask, grad_sn / norm_prod, 0.0).astype(BF16)
             coef_ref[2 * side:2 * side + 1, s * GROUP:(s + 1) * GROUP] = to_row(-jnp.sum(prod, axis=1, keepdims=True) / a_col)
             coef_ref[2 * side + 1:2 * side + 2, s * GROUP:(s + 1) * GROUP] = -jnp.sum(prod, axis=0, keepdims=True) / b_row
-            if side == 0:
-                dtau_ref[s:s + 1, :] = to_row(jnp.sum(d_logit * gram_n, axis=1, keepdims=True))
+            dtau_ref[g:g + 1, :] = to_row(jnp.sum(d_logit * gram_n, axis=1, keepdims=True))
 
 
 def head_state(near, far, tau_rows):
@@ -202,9 +208,10 @@
     return dot(v, am, NT).astype(BF16), dq.astype(BF16), dk.astype(BF16), dot(do, am, NN).astype(BF16)
 
 
-def finish_rows(j, x_ref, g_ref, du, gm_ref, dx_refs, dsum_ref):
+def finish_rows(j, x_ref, g_ref, st_ref, du, gm_ref, dx_refs, dsum_ref):
     rows, width = x_ref.shape[1:]
-    xh, inv = normalize(x_ref[0].astype(F32))
+    mean, inv = st_ref[0, :, :1], st_ref[0, :, LANES // 2:LANES // 2 + 1]
+    xh = (x_ref[0].astype(F32) - mean) * inv
     fold = lambda t: jnp.sum(t.reshape(rows // 8, 8, width), axis=0)
     for a, val in enumerate((fold(du * xh), fold(du))):
         dsum_ref[a] = jnp.where(j == 0, val, dsum_ref[a] + val)
@@ -216,13 +223,15 @@
         ref[0] = dx
 
 
-def rows_body(*refs, n_alias):
+def rows_body(*refs, n_alias, send_blocks):
     it = iter(refs)
     nxt = lambda n: [next(it) for _ in range(n)]
-    off_ref, x_ref, g_ref, u_ref, q_ref, k_ref, v_ref, do_ref = nxt(8)
+    off_ref, x_ref, g_ref, u_ref, st_ref, q_ref, k_ref, v_ref, do_ref = nxt(9)
     attn_ref, dgram_ref, coef_ref, wn_ref, wf_ref, won_ref, wof_ref, gm_ref = nxt(8)
     nxt(n_alias)
-    y_ref, gx_ref, o_ref, rqk_ref, rv_ref, send_ref, dsum_ref = nxt(7)
+    y_ref, gx_ref, o_ref, rqk_ref, rv_ref = nxt(5)
+    send_refs = nxt(len(send_blocks))
+    (dsum_ref,) = nxt(1)
     on_s, rn_s, of_s, rf_s, qf_s, kf_s, vf_s, dof_s = nxt(8)
     j = pl.program_id(0)
     own, other = off_ref[0], off_ref[1]
@@ -249,29 +258,43 @@
     for e in range(3):
         du += dot(rf_s[e], wf_ref[e], NT)
     y_ref[0] = (x_ref[0].astype(F32) + (dot(on_s[...], won_ref[...]) + dot(of_s[...], wof_ref[...]))).astype(BF16)
-    finish_rows(j, x_ref, g_ref, du, gm_ref, [gx_ref, send_ref], dsum_ref)
-
-
-def rows_call(off, start, blocks, acts, state, weights, prev):
+    if len(send_refs) == 1:
+        finish_rows(j, x_ref, g_ref, st_ref, du, gm_ref, [gx_ref] + send_refs, dsum_ref)
+        return
+    finish_rows(j, x_ref, g_ref, st_ref, du, gm_ref, [gx_ref], dsum_ref)
+    start = 0
+    for ref, n in zip(send_refs, send_blocks):
+
+        @pl.when((j >= start) & (j < start + n))
+        def _(ref=ref):
+            ref[0] = gx_ref[0]
+
+        start += n
+
+
+def rows_call(off, start, send_blocks, acts, state, weights, prev):
     _, half, width = acts[0].shape
+    blocks = sum(send_blocks)
+    firsts = [sum(send_blocks[:n]) for n in range(len(send_blocks))]
+    send_spec = lambda first, n: pl.BlockSpec((1, ROWS, width), lambda j, off: (0, jnp.clip(j - first, 0, n - 1), 0))
     cols = weights[2].shape[0]
     row = half_spec(ROWS, width, 0, start)
     both = lambda *lead: both_spec(lead, ROWS, cols, start)
     consts = list(state) + list(weights)
     first = 1 + len(acts) + len(consts)
     return pl.pallas_call(
-        functools.partial(rows_body, n_alias=len(prev)),
+        functools.partial(rows_body, n_alias=len(prev), send_blocks=send_blocks),
         grid_spec=pltpu.PrefetchScalarGridSpec(
             num_scalar_prefetch=1,
             grid=(blocks,),
-            in_specs=[row] * 3 + [both()] * 4 + [whole(t.shape) for t in consts] + [pl.BlockSpec(memory_space=pl.ANY)] * len(prev),
+            in_specs=[row] * 3 + [half_spec(ROWS, LANES, 0, start)] + [both()] * 4 + [whole(t.shape) for t in consts] + [pl.BlockSpec(memory_space=pl.ANY)] * len(prev),
             out_specs=[row, row, both(), both(2), both(),
-                       pl.BlockSpec((1, ROWS, width), lambda j, off: (0, j, 0)),
+                       *[send_spec(first, n) for first, n in zip(firsts, send_blocks)],
                        pl.BlockSpec((2, 8, width), lambda j, off: (0, 0, 0))],
             scratch_shapes=[pltpu.VMEM((ROWS, cols), BF16), pltpu.VMEM((3, ROWS, cols), BF16)] * 2 + [pltpu.VMEM((ROWS, cols), BF16)] * 4,
         ),
         out_shape=[sds((2, half, width), BF16)] * 2 + [sds((2, half, cols), BF16), sds((2, 2, half, cols), BF16), sds((2, half, cols), BF16),
-                                                       sds((1, blocks * ROWS, width), BF16), sds((2, 8, width), F32)],
+                                                       *[sds((1, n * ROWS, width), BF16) for n in send_blocks], sds((2, 8, width), F32)],
         input_output_aliases={first + a: a for a in range(len(prev))},
         name="rows",
         compiler_params=params(),
@@ -279,50 +302,93 @@
     )(off, *acts, *consts, *prev)
 
 
-def far_y_body(off_ref, x_ref, o_ref, vu_ref, *refs, fused):
+def far_y_body(*refs, early, copies):
     it = iter(refs)
     nxt = lambda n: [next(it) for _ in range(n)]
-    attn_ref, won_ref, wof_ref = nxt(3)
-    if fused:
-        (wv_ref,) = nxt(1)
-    _, y_ref, of_s = nxt(3)
-    if fused:
-        vf_ref = nxt(1)[0]
-        vf_ref[...] = dot(vu_ref[0], wv_ref[0]).astype(BF16)
-    else:
-        vf_ref = vu_ref
+    _, x_ref, o_ref, u_ref, v_ref, attn_ref, won_ref, wof_ref, wv_ref = nxt(9)
+    recv = nxt(len(copies))
+    _, _, y_ref, gx_ref, vf_s, of_s = nxt(6)
+    j = pl.program_id(0)
+    start = 0
+    for ref, n in zip(recv, copies):
+
+        @pl.when((j >= start) & (j < start + n))
+        def _(ref=ref):
+            gx_ref[0] = ref[0]
+
+        start += n
+
+    @pl.when(j < early)
+    def _():
+        vf_s[...] = v_ref[...]
+
+    @pl.when(j >= early)
+    def _():
+        vf_s[...] = dot(u_ref[0], wv_ref[0]).astype(BF16)
+
     groups = attn_ref.shape[0] // 2
     for s in range(groups):
         c = slice(s * GROUP, (s + 1) * GROUP)
-        of_s[:, c] = dot(vf_ref[:, c], attn_ref[groups + s], NT).astype(BF16)
+        of_s[:, c] = dot(vf_s[:, c], attn_ref[groups + s], NT).astype(BF16)
     y_ref[0] = (x_ref[0].astype(F32) + (dot(o_ref[0], won_ref[...]) + dot(of_s[...], wof_ref[...]))).astype(BF16)
 
 
-def far_y(off, start, blocks, x2, o2, vu, attn, wo_near, wo_far, w_far, y2):
-    fused = vu.ndim == 3
-    width, cols = x2.shape[2], o2.shape[2]
-    row = lambda c: half_spec(ROWS, c, 1, start)
-    args = [x2, o2, vu, attn, wo_near, wo_far]
-    specs = [row(width), row(cols), row(width) if fused else pl.BlockSpec((ROWS, cols), lambda j, off: (start + j, 0)),
-             whole(attn.shape), whole(wo_near.shape), whole(wo_far.shape)]
-    if fused:
-        args.append(w_far)
-        specs.append(pl.BlockSpec((1, width, cols), lambda j, off: (2, 0, 0), pipeline_mode=pl.Buffered(1)))
-    return pl.pallas_call(
-        functools.partial(far_y_body, fused=fused),
+def far_y(off, x2, o2, u2, vf, attn, wo_near, wo_far, w_far, recv, y2, gx2):
+    half, width = x2.shape[1:]
+    cols = o2.shape[2]
+    rows = 2 * ROWS
+    steps = half // rows
+    early = vf.shape[0] // rows
+    copies = [t.shape[1] // rows for t in recv]
+    row = lambda c: half_spec(rows, c, 1, 0)
+    specs = [row(width), row(cols),
+             pl.BlockSpec((1, rows, width), lambda j, off: (off[1], jnp.maximum(j, early), 0)),
+             pl.BlockSpec((rows, cols), lambda j, off: (jnp.minimum(j, early - 1), 0)),
+             whole(attn.shape), whole(wo_near.shape), whole(wo_far.shape),
+             pl.BlockSpec((1, width, cols), lambda j, off: (2, 0, 0), pipeline_mode=pl.Buffered(1))]
+    for k, n in enumerate(copies):
+        first = sum(copies[:k])
+        specs.append(pl.BlockSpec((1, rows, width), lambda j, off, first=first, n=n: (0, jnp.clip(j - first, 0, n - 1), 0)))
+    args = [x2, o2, u2, vf, attn, wo_near, wo_far, w_far, *recv]
+    return pl.pallas_call(
+        functools.partial(far_y_body, early=early, copies=copies),
         grid_spec=pltpu.PrefetchScalarGridSpec(
             num_scalar_prefetch=1,
-            grid=(blocks,),
-            in_specs=specs + [pl.BlockSpec(memory_space=pl.ANY)],
-            out_specs=row(width),
-            scratch_shapes=[pltpu.VMEM((ROWS, cols), BF16)] * (2 if fused else 1),
+            grid=(steps,),
+            in_specs=specs + [pl.BlockSpec(memory_space=pl.ANY)] * 2,
+            out_specs=[row(width), pl.BlockSpec((1, rows, width), lambda j, off: (off[1], jnp.minimum(j, sum(copies) - 1), 0))],
+            scratch_shapes=[pltpu.VMEM((rows, cols), BF16)] * 2,
         ),
-        out_shape=sds(y2.shape, y2.dtype),
-        input_output_aliases={len(args) + 1: 0},
+        out_shape=[sds(y2.shape, y2.dtype), sds(gx2.shape, gx2.dtype)],
+        input_output_aliases={len(args) + 1: 0, len(args) + 2: 1},
         name="far_y",
         compiler_params=params(),
-        cost_estimate=cost(2 * blocks * ROWS * width * cols * (3.2 if fused else 2.2), 2 * blocks * ROWS * (2 * width + 2 * cols)),
-    )(off, *args, y2)
+        cost_estimate=cost(2 * half * width * cols * 2.8, 2 * half * (4 * width + 3 * cols)),
+    )(off, *args, y2, gx2)
+
+
+def token_sum_body(l_ref, r_ref, o_ref):
+    @pl.when(pl.program_id(0) == 0)
+    def _():
+        o_ref[...] = jnp.zeros_like(o_ref)
+
+    for e in range(r_ref.shape[0]):
+        o_ref[e] += dot(l_ref[...], r_ref[e], TN)
+
+
+def token_sum(lhs, rhs):
+    planes, tokens, cols = rhs.shape
+    width = lhs.shape[1]
+    return pl.pallas_call(
+        token_sum_body,
+        grid=(tokens // SUM_ROWS,),
+        in_specs=[row_spec(SUM_ROWS, width, lambda i: i), pl.BlockSpec((planes, SUM_ROWS, cols), lambda i: (0, i, 0))],
+        out_specs=pl.BlockSpec((planes, width, cols), lambda i: (0, 0, 0)),
+        out_shape=sds((planes, width, cols), F32),
+        name="token_sum",
+        compiler_params=params(),
+        cost_estimate=cost(2 * planes * tokens * width * cols, 2 * tokens * (width + planes * cols)),
+    )(lhs, rhs)
 
 
 def solution(mesh):
@@ -347,47 +413,47 @@
         off = jnp.stack([me, 1 - me]).astype(jnp.int32)
         halves = lambda t: t.reshape(2, half, t.shape[-1])
 
-        u, q, k, v, do, part = project(x, g, w_near, w_out, gamma, beta)
-        x2, g2, u2 = halves(x), halves(g), halves(u)
+        u, q, k, v, do, stats, part = project(x, g, w_near, w_out, gamma, beta)
+        x2, g2, u2, stats2 = halves(x), halves(g), halves(u), halves(stats)
         near = tuple(halves(t) for t in (q, k, v, do))
         peers = [lax.ppermute(part, "sp", [(s, s ^ d) for s in range(sp_size)]) for d in (1, 2, 3)]
         part = (part + peers[0]) + (peers[1] + peers[2])
         part_far = exchange(part)
-        vf0 = far_v(off, u2, w_far, EARLY_V)
+        vf = far_v(off, u2, w_far, EARLY_V, 0, 2)
+        vf = far_v(off, u2, w_far, EARLY_V, 1, 2, (vf,))
         tau = jnp.repeat(temps, HEAD).reshape(tp_size, groups, GROUP)
         tau = jnp.where(me == 0, tau, tau[::-1]).reshape(2 * groups, GROUP)
         attn, dgram, coef, dtau = head_state(part, part_far, tau)
         state = (attn, dgram, coef)
-        dtau = jnp.sum(dtau[:groups].reshape(groups * GROUP // HEAD, HEAD), axis=1)
-        dtau_far = exchange(dtau)
-        grad_temp = jnp.where(me == 0, jnp.concatenate([dtau, dtau_far]), jnp.concatenate([dtau_far, dtau]))
 
         prev, dsum, recv, start = (), None, [], 0
-        for blocks in OWN_CHUNKS:
-            *prev, sent, ds = rows_call(off, start, blocks, (x2, g2, u2) + near, state, (w_near, w_far, w_out, wo_far, gamma), prev)
-            recv.append((start, exchange(sent)))
+        for sizes in OWN_CHUNKS:
+            out = rows_call(off, start, sizes, (x2, g2, u2, stats2) + near, state, (w_near, w_far, w_out, wo_far, gamma), prev)
+            prev, sent, ds = out[:5], out[5:-1], out[-1]
+            recv += [exchange(t) for t in sent]
             dsum = ds if dsum is None else dsum + ds
-            start += blocks
+            start += sum(sizes)
         y2, gx2, o2, rqk, rv = prev
-
-        dw_qk = lax.dot_general(u, rqk.reshape(2, tokens, cols), (((0,), (1,)), ((), ())), preferred_element_type=F32)
+        dtau, rqk = lax.optimization_barrier((dtau, rqk))
+        dtau = jnp.sum(dtau[:2 * groups].reshape(tp_size, cols // HEAD, HEAD), axis=2)
+        grad_temp = jnp.where(me == 0, dtau, dtau[::-1]).reshape(-1)
+
+        dw_qk = token_sum(u, rqk.reshape(2, tokens, cols))
         o2, dw_qk = lax.optimization_barrier((o2, dw_qk))
-        dw_qk = lax.psum_scatter(dw_qk, "sp", scatter_dimension=0, tiled=True)
-        dw_o = dot(o2.reshape(tokens, cols), g, TN)
+        dw_qk = lax.psum_scatter(dw_qk, "sp", scatter_dimension=1, tiled=True)
+        dw_o = token_sum(o2.reshape(tokens, cols), g[None])[0]
         rv, dw_o = lax.optimization_barrier((rv, dw_o))
         grad_wout = lax.psum_scatter(dw_o, "sp", scatter_dimension=0, tiled=True)
-        dw_v = dot(u, rv.reshape(tokens, cols), TN)
+        dw_v = token_sum(u, rv.reshape(1, tokens, cols))
         y2, dw_v = lax.optimization_barrier((y2, dw_v))
-        dw_v = lax.psum_scatter(dw_v, "sp", scatter_dimension=0, tiled=True)
-        y2 = far_y(off, 0, EARLY_V, x2, o2, vf0, attn, w_out, wo_far, w_far, y2)
-        y2 = far_y(off, EARLY_V, half // ROWS - EARLY_V, x2, o2, u2, attn, w_out, wo_far, w_far, y2)
-        grad_wqkv = jnp.concatenate([dw_qk, dw_v[:, None]], axis=1)
+        dw_v = lax.psum_scatter(dw_v, "sp", scatter_dimension=1, tiled=True)
+        y2, gx2 = far_y(off, x2, o2, u2, vf, attn, w_out, wo_far, w_far, recv[:-1], y2, gx2)
+        grad_wqkv = jnp.transpose(jnp.concatenate([dw_qk, dw_v], axis=0), (1, 0, 2))
 
         sums = jnp.sum(dsum, axis=1)
         for axis, perm in (("tp", swap), ("sp", [(s, s ^ 1) for s in range(sp_size)]), ("sp", [(s, s ^ 2) for s in range(sp_size)])):
             sums = sums + lax.ppermute(sums, axis, perm)
-        for start, blk in recv:
-            gx2 = lax.dynamic_update_slice(gx2, blk, (off[1], start * ROWS, 0))
+        gx2 = lax.dynamic_update_slice(gx2, recv[-1], (off[1], half - recv[-1].shape[1], 0))
         return y2.reshape(tokens, width), gx2.reshape(tokens, width), grad_wqkv, grad_wout, sums[0], sums[1], grad_temp
 
     in_specs = (in_rows, in_rows, P(None, None, "tp"), P("tp", None), P(None), P(None), P(None))

time: 1360 us -> 1360 us (level)
  Pallas kernels: 646 us -> 833 us
  matrix products: 183 us -> 0 us
  waiting for transfers between devices: 455 us -> 478 us
  local copies, waits for them, and re-layouts: 28.5 us -> 9.35 us
    ppermute x3, waiting for transfers between devices: 133 us -> 461 us  [step(): sums = sums + lax.ppermute(sums, axis, perm)]
    ppermute x8, waiting for transfers between devices: 310 us -> 5.18 us  [exchange(): return lax.ppermute(t, 'tp', swap)]
    pallas_call x6 -> x8, Pallas kernels: 429 us -> 612 us  [the longest x4 354 us: rows_call(): pl.pallas_call(functools.partial(rows_body, n_alias=len(prev), send_block...]
    dot_general x3 -> x0, matrix products: 183 us -> none  [the longest x2 94.1 us: dot(): return lax.dot_general(a, b, dims, preferred_element_type=F32)]
    dynamic_update_slice x4 -> x1, local copies, waits for them, and re-layouts: 23.6 us -> 3.76 us  [step(): lax.dynamic_update_slice(gx2, recv[-1], (off[1], half - recv[-1].shape[1]...]
  transfers between devices with their start and end apart: 17 -> 17, of which waited for: 6 -> 5; matrix products, arithmetic and copies ran while one was open for 3% -> 1% of each run, Pallas kernels for 22% -> 22%
where the time goes in v4:
time: 1360 us
  Pallas kernels  833 us (61%)
  waiting for transfers between devices  478 us (35%)
  starting transfers between devices  16.5 us (1%)
  between operations  14.1 us (1%)
    ppermute x3, waiting for transfers between devices, step(): sums = sums + lax.ppermute(sums, axis, perm)  461 us
    pallas_call x4, Pallas kernels, rows_call(): pl.pallas_call(functools.partial(rows_body, n_alias=len(prev), send_block...  354 us
    pallas_call x1, Pallas kernels, project(): pl.pallas_call(project_body, grid=(tokens // PROJ_ROWS,), in_specs=[row(w...  199 us
    pallas_call x3, Pallas kernels, token_sum(): pl.pallas_call(token_sum_body, grid=(tokens // SUM_ROWS,), in_specs=[row_...  185 us
    pallas_call x1, Pallas kernels, far_y(): pl.pallas_call(functools.partial(far_y_body, early=early, copies=copies),...  73.2 us
  transfers between devices with their start and end apart: 17, of which 5 were waited for; matrix products, arithmetic and copies ran while one was open for 1% of the time, Pallas kernels for 22%

profile of v4, /device:TPU:0, one launch (start us, length us, event | category | flops | bytes accessed | tf_op | source)
XLA Modules:
  0.0 1357.5 jit_solution(15615102169072513585)
XLA Ops:
  7.2 0.0 reduce-scatter.6.cloned.1.call-start
  7.2 3.4 collective-permute-start.4
  10.6 0.0 collective-permute-start.5
  10.6 1.3 reshape.72.gm_ref.refs_16_
  11.9 1.3 reshape.73.bt_ref
  13.2 199.2 %project.1 = (bf16[16384,1536]{1,0:T(8,128)(2,1)}, bf16[16384,768]{1,0:T(8,128)(2,1)}, bf16[16384,768]{1,0:T(8,128)(2,1)}, bf16[16384,768]{1,0:T(8,128)(2,1)}, b...) custom-call(bf16[16384,1536]{1,0:T(8,128)(2,1)} %x_ref.1, bf16[16384,1536]{1,0:T(8,128)(2,1)} %g_ref.1, ...), custom_call_target="tpu_custom_call" | custom-call | flops 170080698368 | bytes 251658240 | tf_op jit(solution)/shard_map/project/pallas_call | solution.py:114
  212.4 0.0 collective-permute-start
  212.4 2.0 collective-permute-start.1
  214.4 0.1 collective-permute-start.2
  214.5 0.1 broadcast_in_dim.10
  214.6 0.1 broadcast_in_dim.11
  214.7 0.1 broadcast_in_dim.12
  214.7 0.1 rev.6
  214.9 0.0 collective-permute-done
  214.9 6.6 collective-permute-done.1
  221.5 4.7 collective-permute-done.2
  226.2 1.0 add_add_fusion.near_ref
  227.2 0.0 copy-start
  227.2 1.6 collective-permute-start.3
  228.8 0.6 reshape.80.tau_ref
  229.4 0.6 pad_add_fusion.refs_0_.off_ref
  230.1 5.2 collective-permute-done.3.far_ref
  235.2 0.7 copy-done.7
  235.9 4.7 head_state.1
  240.6 0.0 collective-permute-done.5.refs_15_.refs_7_
  240.6 0.0 collective-permute-done.4.refs_13_.w_ref.refs_8_
  240.6 49.8 %rows.4 = (bf16[2,8192,1536]{2,1,0:T(8,128)(2,1)}, bf16[2,8192,1536]{2,1,0:T(8,128)(2,1)}, bf16[2,8192,768]{2,1,0:T(8,128)(2,1)}, bf16[2,2,8192,768]{3,2,1,0:T(8...) custom-call(s32[2]{0:T(128)} %pad_add_fusion.refs_0_.off_ref, ...), custom_call_target="tpu_custom_call" | custom-call | flops 31406948352 | bytes 44040192 | tf_op jit(solution)/shard_map/rows/pallas_call | solution.py:285
  290.4 69.0 %rows.5 = (bf16[2,8192,1536]{2,1,0:T(8,128)(2,1)}, bf16[2,8192,1536]{2,1,0:T(8,128)(2,1)}, bf16[2,8192,768]{2,1,0:T(8,128)(2,1)}, bf16[2,2,8192,768]{3,2,1,0:T(8...) custom-call(s32[2]{0:T(128)} %pad_add_fusion.refs_0_.off_ref, ...), custom_call_target="tpu_custom_call", output_to_operand_aliasing={{0}: (17, {}), {1}: (18, {}), {2}: (19, {}), {3}: (20, {}),... | custom-call | flops 47110422528 | bytes 66060288 | tf_op jit(solution)/shard_map/rows/pallas_call | solution.py:285
  359.4 107.4 %rows.6 = (bf16[2,8192,1536]{2,1,0:T(8,128)(2,1)}, bf16[2,8192,1536]{2,1,0:T(8,128)(2,1)}, bf16[2,8192,768]{2,1,0:T(8,128)(2,1)}, bf16[2,2,8192,768]{3,2,1,0:T(8...) custom-call(s32[2]{0:T(128)} %pad_add_fusion.refs_0_.off_ref, ...), custom_call_target="tpu_custom_call", output_to_operand_aliasing={{0}: (17, {}), {1}: (18, {}), {2}: (19, {}), {3}: (20, {}),... | custom-call | flops 78517370880 | bytes 110100480 | tf_op jit(solution)/shard_map/rows/pallas_call | solution.py:285
  466.9 128.1 %rows.7 = (bf16[2,8192,1536]{2,1,0:T(8,128)(2,1)}, bf16[2,8192,1536]{2,1,0:T(8,128)(2,1)}, bf16[2,8192,768]{2,1,0:T(8,128)(2,1)}, bf16[2,2,8192,768]{3,2,1,0:T(8...) custom-call(s32[2]{0:T(128)} %pad_add_fusion.refs_0_.off_ref, ...), custom_call_target="tpu_custom_call", output_to_operand_aliasing={{0}: (17, {}), {1}: (18, {}), {2}: (19, {}), {3}: (20, {}),... | custom-call | flops 94220845056 | bytes 132120576 | tf_op jit(solution)/shard_map/rows/pallas_call | solution.py:285
  595.0 89.5 %token_sum.3 = f32[2,1536,768]{2,1,0:T(8,128)} custom-call(bf16[16384,1536]{1,0:T(8,128)(2,1)} %get-tuple-element.57.l_ref, bf16[2,16384,768]{2,1,0:T(8,128)(2,1)} %bitcast.44), custom_call_target="tpu_custom_call" | custom-call | flops 77309411328 | bytes 100663296 | tf_op jit(solution)/shard_map/token_sum/pallas_call | solution.py:382
  684.5 47.2 %token_sum.4 = f32[1,768,1536]{2,1,0:T(8,128)} custom-call(bf16[16384,768]{1,0:T(8,128)(2,1)} %bitcast.61, bf16[1,16384,1536]{2,1,0:T(8,128)(2,1)} %bitcast.41), custom_call_target="tpu_custom_call" | custom-call | flops 38654705664 | bytes 75497472 | tf_op jit(solution)/shard_map/token_sum/pallas_call | solution.py:382
  731.7 48.2 %token_sum.5 = f32[1,1536,768]{2,1,0:T(8,128)} custom-call(bf16[16384,1536]{1,0:T(8,128)(2,1)} %get-tuple-element.57.l_ref, bf16[1,16384,768]{2,1,0:T(8,128)(2,1)} %bitcast.62), custom_call_target="tpu_custom_call" | custom-call | flops 38654705664 | bytes 75497472 | tf_op jit(solution)/shard_map/token_sum/pallas_call | solution.py:382
  779.8 0.0 reduce-scatter.6.cloned.1.call-update
  779.9 0.0 reduce-scatter.4.cloned.1.call-start
  779.9 0.7 reduce-scatter.4.cloned.1.call-update
  780.6 0.0 reduce-scatter.8.cloned.1.call-start
  780.7 1.8 collective-permute-start.8
  782.4 0.3 collective-permute-start.9
  782.7 1.7 collective-permute-start.7
  784.4 0.0 reduce-scatter.8.cloned.1.call-update
  784.5 0.3 collective-permute-start.6
  784.8 0.1 add_reduce_fusion
  784.8 1.8 collective-permute-start.11
  786.6 8.8 far_v.2.refs_0_
  795.4 459.7 %collective-permute-done.11 = f32[2,1536]{1,0:T(2,128)S(1)} collective-permute-done((f32[2,1536]{1,0:T(2,128)S(1)}, f32[2,1536]{1,0:T(2,128)S(1)}, u32[]{:S(2)}, u32[]{:S(2)}) %collective-permute-start.11) | collective-permute-done | bytes 12320 | tf_op jit(solution)/shard_map/ppermute | solution.py:455
  1255.1 0.0 copy-start.5
  1255.1 0.0 collective-permute-start.12
  1255.1 8.2 far_v.3.refs_4_
  1263.3 0.1 reshape.86
  1263.4 0.1 reduce_sum.19
  1263.5 0.0 collective-permute-done.12
  1263.6 1.7 collective-permute-start.13
  1265.3 0.6 reshape.87
  1265.9 1.4 collective-permute-done.13
  1267.3 1.7 collective-permute-start.10
  1269.0 0.6 slice_reduce_fusion
  1269.7 0.0 collective-permute-done.6.refs_9_
  1269.7 0.0 collective-permute-done.9.refs_12_
  1269.7 0.0 collective-permute-done.8.refs_11_
  1269.7 73.2 %far_y.1 = (bf16[2,8192,1536]{2,1,0:T(8,128)(2,1)}, bf16[2,8192,1536]{2,1,0:T(8,128)(2,1)}) custom-call(s32[2]{0:T(128)} %pad_add_fusion.refs_0_.off_ref, bf16[2,8192,1536]{2,1,0:T(8,128)(2,1)} %bitcast.36, bf16[2,8192,768]{2,1,0:T(8,128)(2,1)} %get-tuple-element.86.refs_2_, ...), custom_call_target="tpu_custom_call", output_to_operand_aliasing={{0}: (13, {}), {1}: (14, {})} | custom-call | flops 54116589568 | bytes 138412032 | tf_op jit(solution)/shard_map/far_y/pallas_call | solution.py:353
  1342.9 0.0 collective-permute-done.10
  1342.9 3.8 constant_dynamic-update-slice_fusion
  1346.7 4.1 maximum_bitcast_fusion
  (25 shorter events, 0.1 us)
Async XLA Ops:
  7.2 1339.5 %reduce-scatter.6.cloned.1.call-start = ((), (), s32[]{:S(2)}) async-start(), calls=%async_computation.4 | async-start | bytes 5898240 | tf_op jit(solution)/shard_map/reduce_scatter | solution.py:449
  7.2 233.4 %collective-permute-start.4 = (bf16[3,1536,768]{2,1,0:T(8,128)(2,1)}, bf16[3,1536,768]{2,1,0:T(8,128)(2,1)}, u32[]{:S(2)}, u32[]{:S(2)}) collective-permute-start(bf16[3,1536,768]{2,1,0:T(8,128)(2,1)} %bitcast.67), channel_id=1, source_target_pairs={{0,4},{4,0},{1,5},{5,1},{2,6},{6,2},{3,7},{7,3}} | collective-permute-start | bytes 21233672 | tf_op jit(solution)/shard_map/ppermute | solution.py:401
  10.6 230.0 %collective-permute-start.5 = (bf16[768,1536]{1,0:T(8,128)(2,1)}, bf16[768,1536]{1,0:T(8,128)(2,1)}, u32[]{:S(2)}, u32[]{:S(2)}) collective-permute-start(bf16[768,1536]{1,0:T(8,128)(2,1)} %refs_6_.1), channel_id=1, source_target_pairs={{0,4},{4,0},{1,5},{5,1},{2,6},{6,2},{3,7},{7,3}} | collective-permute-start | bytes 7077896 | tf_op jit(solution)/shard_map/ppermute | solution.py:401
  13.2 201.3 %copy-start.6 = (f32[48]{0:T(128)S(1)}, f32[48]{0:T(128)}, u32[]{:S(2)}) copy-start(f32[48]{0:T(128)} %param.13) | copy-start | bytes 580
  212.4 2.5 collective-permute-start
  212.4 9.1 collective-permute-start.1
  214.4 11.8 collective-permute-start.2
  227.2 8.0 copy-start
  227.2 8.0 collective-permute-start.3
  235.2 0.7 copy-start.7
  731.6 53.1 %copy-start.1 = (f32[2,8,1536]{2,1,0:T(8,128)S(1)}, f32[2,8,1536]{2,1,0:T(8,128)}, u32[]{:S(2)}) copy-start(f32[2,8,1536]{2,1,0:T(8,128)} %get-tuple-element.102) | copy-start | bytes 294916
  731.6 53.1 %copy-start.2 = (f32[2,8,1536]{2,1,0:T(8,128)S(1)}, f32[2,8,1536]{2,1,0:T(8,128)}, u32[]{:S(2)}) copy-start(f32[2,8,1536]{2,1,0:T(8,128)} %get-tuple-element.103) | copy-start | bytes 294916
  731.6 53.1 %copy-start.3 = (f32[2,8,1536]{2,1,0:T(8,128)S(1)}, f32[2,8,1536]{2,1,0:T(8,128)}, u32[]{:S(2)}) copy-start(f32[2,8,1536]{2,1,0:T(8,128)} %get-tuple-element.104) | copy-start | bytes 294916
  731.7 53.1 %copy-start.4 = (f32[2,8,1536]{2,1,0:T(8,128)S(1)}, f32[2,8,1536]{2,1,0:T(8,128)}, u32[]{:S(2)}) copy-start(f32[2,8,1536]{2,1,0:T(8,128)} %get-tuple-element.105) | copy-start | bytes 294916
  779.9 566.8 %reduce-scatter.4.cloned.1.call-start = ((), (), s32[]{:S(2)}) async-start(), calls=%async_computation.3 | async-start | bytes 11796480 | tf_op jit(solution)/shard_map/reduce_scatter | solution.py:443
  780.6 570.1 %reduce-scatter.8.cloned.1.call-start = ((), (), s32[]{:S(2)}) async-start(), calls=%async_computation.5 | async-start | bytes 5898240 | tf_op jit(solution)/shard_map/reduce_scatter | solution.py:446
  780.7 489.0 %collective-permute-start.8 = (bf16[1,2560,1536]{2,1,0:T(8,128)(2,1)}, bf16[1,2560,1536]{2,1,0:T(8,128)(2,1)}, u32[]{:S(2)}, u32[]{:S(2)}) collective-permute-start(bf16[1,2560,1536]{2,1,0:T(8,128)(2,1)} %get-tuple-element.89), channel_id=1, source_target_pairs={{0,4},{4,0},{1,5},{5,1},{2,6},{6,2},{3,7},{7,3}} | collective-permute-start | bytes 23592968 | tf_op jit(solution)/shard_map/ppermute | solution.py:401
  782.4 487.3 %collective-permute-start.9 = (bf16[1,2048,1536]{2,1,0:T(8,128)(2,1)}, bf16[1,2048,1536]{2,1,0:T(8,128)(2,1)}, u32[]{:S(2)}, u32[]{:S(2)}) collective-permute-start(bf16[1,2048,1536]{2,1,0:T(8,128)(2,1)} %get-tuple-element.90), channel_id=1, source_target_pairs={{0,4},{4,0},{1,5},{5,1},{2,6},{6,2},{3,7},{7,3}} | collective-permute-start | bytes 18874376 | tf_op jit(solution)/shard_map/ppermute | solution.py:401
  782.7 487.0 %collective-permute-start.7 = (bf16[1,1536,1536]{2,1,0:T(8,128)(2,1)}, bf16[1,1536,1536]{2,1,0:T(8,128)(2,1)}, u32[]{:S(2)}, u32[]{:S(2)}) collective-permute-start(bf16[1,1536,1536]{2,1,0:T(8,128)(2,1)} %get-tuple-element.88), channel_id=1, source_target_pairs={{0,4},{4,0},{1,5},{5,1},{2,6},{6,2},{3,7},{7,3}} | collective-permute-start | bytes 14155784 | tf_op jit(solution)/shard_map/ppermute | solution.py:401
  784.5 485.2 %collective-permute-start.6 = (bf16[1,1024,1536]{2,1,0:T(8,128)(2,1)}, bf16[1,1024,1536]{2,1,0:T(8,128)(2,1)}, u32[]{:S(2)}, u32[]{:S(2)}) collective-permute-start(bf16[1,1024,1536]{2,1,0:T(8,128)(2,1)} %get-tuple-element.87), channel_id=1, source_target_pairs={{0,4},{4,0},{1,5},{5,1},{2,6},{6,2},{3,7},{7,3}} | collective-permute-start | bytes 9437192 | tf_op jit(solution)/shard_map/ppermute | solution.py:401
  784.8 470.2 %collective-permute-start.11 = (f32[2,1536]{1,0:T(2,128)S(1)}, f32[2,1536]{1,0:T(2,128)S(1)}, u32[]{:S(2)}, u32[]{:S(2)}) collective-permute-start(f32[2,1536]{1,0:T(2,128)S(1)} %add_reduce_fusion), channel_id=1, source_target_pairs={{0,4},{4,0},{1,5},{5,1},{2,6},{6,2},{3,7},{7,3}} | collective-permute-start | bytes 36872 | tf_op jit(solution)/shard_map/ppermute | solution.py:455
  1255.1 8.2 copy-start.5
  1255.1 8.4 collective-permute-start.12
  1263.6 3.7 collective-permute-start.13
  1267.3 75.6 %collective-permute-start.10 = (bf16[1,1024,1536]{2,1,0:T(8,128)(2,1)}, bf16[1,1024,1536]{2,1,0:T(8,128)(2,1)}, u32[]{:S(2)}, u32[]{:S(2)}) collective-permute-start(bf16[1,1024,1536]{2,1,0:T(8,128)(2,1)} %get-tuple-element.98), channel_id=1, source_target_pairs={{0,4},{4,0},{1,5},{5,1},{2,6},{6,2},{3,7},{7,3}} | collective-permute-start | bytes 9437192 | tf_op jit(solution)/shard_map/ppermute | solution.py:401
Sparse Core Ops, SparseCore 0:
  780.0 43.5 reduce-scatter.5
  826.2 72.3 reduce-scatter.3
  901.6 42.4 reduce-scatter.7

commit v5 on v4

--- a/solution.py
+++ b/solution.py
@@ -17,7 +17,7 @@
 NN = (((1,), (0,)), ((), ()))
 NT = (((1,), (1,)), ((), ()))
 TN = (((0,), (0,)), ((), ()))
-PROJ_ROWS = 512
+PROJ_ROWS = 1024
 ROWS = 256
 SUM_ROWS = 1024
 OWN_CHUNKS = ((4,), (6,), (10,), (8, 4))
@@ -70,7 +70,7 @@
     groups = cols // GROUP
     do_ref[...] = dot(g_ref[...], wo_ref[...], NT).astype(BF16)
     xh, mean, inv = normalize(x_ref[...].astype(F32))
-    u_ref[...] = (xh * gm_ref[...] + bt_ref[...]).astype(BF16)
+    u_ref[...] = (xh * gm_ref[...].reshape(1, -1) + bt_ref[...].reshape(1, -1)).astype(BF16)
     st_ref[...] = jnp.where(lax.broadcasted_iota(jnp.int32, st_ref.shape, 1) < LANES // 2, mean, inv)
     u = u_ref[...]
     for e, out in enumerate((q_ref, k_ref, v_ref)):
@@ -114,7 +114,7 @@
     return pl.pallas_call(
         project_body,
         grid=(tokens // PROJ_ROWS,),
-        in_specs=[row(width), row(width), whole(w3.shape), whole(wo.shape), whole((1, width)), whole((1, width))],
+        in_specs=[row(width), row(width), whole(w3.shape), whole(wo.shape), whole(gamma.shape), whole(beta.shape)],
         out_specs=[row(width)] + [row(cols)] * 4 + [row(LANES), pl.BlockSpec((part_rows, GROUP), lambda i: (0, 0))],
         out_shape=[sds((tokens, width), BF16)] + [sds((tokens, cols), BF16)] * 4 + [sds((tokens, LANES), F32), sds((part_rows, GROUP), F32)],
         scratch_shapes=[pltpu.VMEM((groups, GROUP, GROUP), F32)] * 2 + [pltpu.VMEM((8, cols), F32)] * 2,
@@ -215,7 +215,7 @@
     fold = lambda t: jnp.sum(t.reshape(rows // 8, 8, width), axis=0)
     for a, val in enumerate((fold(du * xh), fold(du))):
         dsum_ref[a] = jnp.where(j == 0, val, dsum_ref[a] + val)
-    gh = du * gm_ref[...]
+    gh = du * gm_ref[...].reshape(1, width)
     m1 = jnp.mean(gh, axis=-1, keepdims=True)
     m2 = jnp.mean(gh * xh, axis=-1, keepdims=True)
     dx = (g_ref[0].astype(F32) + inv * (gh - m1 - xh * m2)).astype(BF16)
@@ -227,49 +227,68 @@
     it = iter(refs)
     nxt = lambda n: [next(it) for _ in range(n)]
     off_ref, x_ref, g_ref, u_ref, st_ref, q_ref, k_ref, v_ref, do_ref = nxt(9)
-    attn_ref, dgram_ref, coef_ref, wn_ref, wf_ref, won_ref, wof_ref, gm_ref = nxt(8)
+    attn_ref, dgram_ref, coef_ref, gm_ref = nxt(4)
+    w_hbm = nxt(4)
     nxt(n_alias)
     y_ref, gx_ref, o_ref, rqk_ref, rv_ref = nxt(5)
     send_refs = nxt(len(send_blocks))
     (dsum_ref,) = nxt(1)
     on_s, rn_s, of_s, rf_s, qf_s, kf_s, vf_s, dof_s = nxt(8)
+    w_refs, w_sems = nxt(4), nxt(1)[0]
+    wf_ref, wof_ref, wn_ref, won_ref = w_refs
     j = pl.program_id(0)
     own, other = off_ref[0], off_ref[1]
     groups = attn_ref.shape[0] // 2
-    u = u_ref[0]
-    for e, t in enumerate((qf_s, kf_s, vf_s)):
-        t[...] = dot(u, wf_ref[e]).astype(BF16)
-    dof_s[...] = dot(g_ref[0], wof_ref[...], NT).astype(BF16)
     state = (attn_ref, dgram_ref, coef_ref)
-    for s in range(groups):
-        c = slice(s * GROUP, (s + 1) * GROUP)
-        for half in (own, other):
-            o, dq, dk, dv = mix_block(q_ref[half, :, c], k_ref[half, :, c], v_ref[half, :, c], do_ref[half, :, c], *state, 0, s)
-            o_ref[half, :, c], rqk_ref[0, half, :, c], rqk_ref[1, half, :, c], rv_ref[half, :, c] = o, dq, dk, dv
-            if half is own:
-                on_s[:, c], rn_s[0, :, c], rn_s[1, :, c], rn_s[2, :, c] = o, dq, dk, dv
-    for s in range(groups):
-        c = slice(s * GROUP, (s + 1) * GROUP)
-        of_s[:, c], rf_s[0, :, c], rf_s[1, :, c], rf_s[2, :, c] = mix_block(
-            qf_s[:, c], kf_s[:, c], vf_s[:, c], dof_s[:, c], *state, 1, s)
-    du = dot(rn_s[0], wn_ref[0], NT)
-    for e in range(1, 3):
-        du += dot(rn_s[e], wn_ref[e], NT)
-    for e in range(3):
-        du += dot(rf_s[e], wf_ref[e], NT)
-    y_ref[0] = (x_ref[0].astype(F32) + (dot(on_s[...], won_ref[...]) + dot(of_s[...], wof_ref[...]))).astype(BF16)
-    if len(send_refs) == 1:
-        finish_rows(j, x_ref, g_ref, st_ref, du, gm_ref, [gx_ref] + send_refs, dsum_ref)
-        return
-    finish_rows(j, x_ref, g_ref, st_ref, du, gm_ref, [gx_ref], dsum_ref)
-    start = 0
-    for ref, n in zip(send_refs, send_blocks):
-
-        @pl.when((j >= start) & (j < start + n))
-        def _(ref=ref):
-            ref[0] = gx_ref[0]
-
-        start += n
+    loads = [pltpu.make_async_copy(src, dst, w_sems.at[n]) for n, (src, dst) in enumerate(zip(w_hbm, w_refs))]
+
+    def compute(wait):
+        for s in range(groups):
+            c = slice(s * GROUP, (s + 1) * GROUP)
+            for half in (own, other):
+                o, dq, dk, dv = mix_block(q_ref[half, :, c], k_ref[half, :, c], v_ref[half, :, c], do_ref[half, :, c], *state, 0, s)
+                o_ref[half, :, c], rqk_ref[0, half, :, c], rqk_ref[1, half, :, c], rv_ref[half, :, c] = o, dq, dk, dv
+                if half is own:
+                    on_s[:, c], rn_s[0, :, c], rn_s[1, :, c], rn_s[2, :, c] = o, dq, dk, dv
+        wait(0)
+        wait(1)
+        u = u_ref[0]
+        for e, t in enumerate((qf_s, kf_s, vf_s)):
+            t[...] = dot(u, wf_ref[e]).astype(BF16)
+        dof_s[...] = dot(g_ref[0], wof_ref[...], NT).astype(BF16)
+        for s in range(groups):
+            c = slice(s * GROUP, (s + 1) * GROUP)
+            of_s[:, c], rf_s[0, :, c], rf_s[1, :, c], rf_s[2, :, c] = mix_block(
+                qf_s[:, c], kf_s[:, c], vf_s[:, c], dof_s[:, c], *state, 1, s)
+        wait(2)
+        wait(3)
+        du = dot(rn_s[0], wn_ref[0], NT)
+        for e in range(1, 3):
+            du += dot(rn_s[e], wn_ref[e], NT)
+        for e in range(3):
+            du += dot(rf_s[e], wf_ref[e], NT)
+        y_ref[0] = (x_ref[0].astype(F32) + (dot(on_s[...], won_ref[...]) + dot(of_s[...], wof_ref[...]))).astype(BF16)
+        finish_rows(j, x_ref, g_ref, st_ref, du, gm_ref, [gx_ref] + send_refs[:1] * (len(send_refs) == 1), dsum_ref)
+
+    @pl.when(j == 0)
+    def _():
+        for load in loads:
+            load.start()
+        compute(lambda n: loads[n].wait())
+
+    @pl.when(j > 0)
+    def _():
+        compute(lambda n: None)
+
+    if len(send_refs) > 1:
+        start = 0
+        for ref, n in zip(send_refs, send_blocks):
+
+            @pl.when((j >= start) & (j < start + n))
+            def _(ref=ref):
+                ref[0] = gx_ref[0]
+
+            start += n
 
 
 def rows_call(off, start, send_blocks, acts, state, weights, prev):
@@ -280,18 +299,21 @@
     cols = weights[2].shape[0]
     row = half_spec(ROWS, width, 0, start)
     both = lambda *lead: both_spec(lead, ROWS, cols, start)
-    consts = list(state) + list(weights)
-    first = 1 + len(acts) + len(consts)
+    w_near, w_far, wo_near, wo_far, gamma = weights
+    consts = list(state) + [gamma]
+    loaded = [w_far, wo_far, w_near, wo_near]
+    first = 1 + len(acts) + len(consts) + len(loaded)
     return pl.pallas_call(
         functools.partial(rows_body, n_alias=len(prev), send_blocks=send_blocks),
         grid_spec=pltpu.PrefetchScalarGridSpec(
             num_scalar_prefetch=1,
             grid=(blocks,),
-            in_specs=[row] * 3 + [half_spec(ROWS, LANES, 0, start)] + [both()] * 4 + [whole(t.shape) for t in consts] + [pl.BlockSpec(memory_space=pl.ANY)] * len(prev),
+            in_specs=[row] * 3 + [half_spec(ROWS, LANES, 0, start)] + [both()] * 4 + [whole(t.shape) for t in consts] + [pl.BlockSpec(memory_space=pl.ANY)] * (len(loaded) + len(prev)),
             out_specs=[row, row, both(), both(2), both(),
                        *[send_spec(first, n) for first, n in zip(firsts, send_blocks)],
                        pl.BlockSpec((2, 8, width), lambda j, off: (0, 0, 0))],
-            scratch_shapes=[pltpu.VMEM((ROWS, cols), BF16), pltpu.VMEM((3, ROWS, cols), BF16)] * 2 + [pltpu.VMEM((ROWS, cols), BF16)] * 4,
+            scratch_shapes=[pltpu.VMEM((ROWS, cols), BF16), pltpu.VMEM((3, ROWS, cols), BF16)] * 2 + [pltpu.VMEM((ROWS, cols), BF16)] * 4
+            + [pltpu.VMEM(t.shape, t.dtype) for t in loaded] + [pltpu.SemaphoreType.DMA((len(loaded),))],
         ),
         out_shape=[sds((2, half, width), BF16)] * 2 + [sds((2, half, cols), BF16), sds((2, 2, half, cols), BF16), sds((2, half, cols), BF16),
                                                        *[sds((1, n * ROWS, width), BF16) for n in send_blocks], sds((2, 8, width), F32)],
@@ -299,24 +321,30 @@
         name="rows",
         compiler_params=params(),
         cost_estimate=cost(2 * blocks * ROWS * width * cols * 13, 2 * blocks * ROWS * (6 * width + 16 * cols)),
-    )(off, *acts, *consts, *prev)
+    )(off, *acts, *consts, *loaded, *prev)
 
 
 def far_y_body(*refs, early, copies):
     it = iter(refs)
     nxt = lambda n: [next(it) for _ in range(n)]
-    _, x_ref, o_ref, u_ref, v_ref, attn_ref, won_ref, wof_ref, wv_ref = nxt(9)
+    _, x_ref, o_ref, u_ref, v_ref, attn_ref, won_ref, wof_ref, wv_ref, qk_ref = nxt(10)
     recv = nxt(len(copies))
-    _, _, y_ref, gx_ref, vf_s, of_s = nxt(6)
+    _, _, y_ref, gx_ref, gw_ref, vf_s, of_s, sem = nxt(8)
     j = pl.program_id(0)
-    start = 0
-    for ref, n in zip(recv, copies):
-
-        @pl.when((j >= start) & (j < start + n))
-        def _(ref=ref):
-            gx_ref[0] = ref[0]
-
-        start += n
+    rows = gx_ref.shape[1]
+
+    def file_rows(act):
+        start = 0
+        for ref, n in zip(recv, copies):
+
+            @pl.when((j >= start) & (j < start + n))
+            def _(ref=ref, start=start):
+                act(pltpu.make_async_copy(ref.at[0, pl.ds((j - start) * rows, rows)], gx_ref.at[0], sem))
+
+            start += n
+
+    file_rows(lambda copy: copy.start())
+    gw_ref[...] = qk_ref[...]
 
     @pl.when(j < early)
     def _():
@@ -331,9 +359,10 @@
         c = slice(s * GROUP, (s + 1) * GROUP)
         of_s[:, c] = dot(vf_s[:, c], attn_ref[groups + s], NT).astype(BF16)
     y_ref[0] = (x_ref[0].astype(F32) + (dot(o_ref[0], won_ref[...]) + dot(of_s[...], wof_ref[...]))).astype(BF16)
-
-
-def far_y(off, x2, o2, u2, vf, attn, wo_near, wo_far, w_far, recv, y2, gx2):
+    file_rows(lambda copy: copy.wait())
+
+
+def far_y(off, x2, o2, u2, vf, attn, wo_near, wo_far, w_far, dw_qk, recv, y2, gx2):
     half, width = x2.shape[1:]
     cols = o2.shape[2]
     rows = 2 * ROWS
@@ -341,25 +370,25 @@
     early = vf.shape[0] // rows
     copies = [t.shape[1] // rows for t in recv]
     row = lambda c: half_spec(rows, c, 1, 0)
+    per = steps // 2
+    plane = pl.BlockSpec((1, dw_qk.shape[1] // per, cols), lambda j, off: (j // per, j % per, 0))
+    any_ = pl.BlockSpec(memory_space=pl.ANY)
     specs = [row(width), row(cols),
              pl.BlockSpec((1, rows, width), lambda j, off: (off[1], jnp.maximum(j, early), 0)),
              pl.BlockSpec((rows, cols), lambda j, off: (jnp.minimum(j, early - 1), 0)),
              whole(attn.shape), whole(wo_near.shape), whole(wo_far.shape),
-             pl.BlockSpec((1, width, cols), lambda j, off: (2, 0, 0), pipeline_mode=pl.Buffered(1))]
-    for k, n in enumerate(copies):
-        first = sum(copies[:k])
-        specs.append(pl.BlockSpec((1, rows, width), lambda j, off, first=first, n=n: (0, jnp.clip(j - first, 0, n - 1), 0)))
-    args = [x2, o2, u2, vf, attn, wo_near, wo_far, w_far, *recv]
+             pl.BlockSpec((1, width, cols), lambda j, off: (2, 0, 0), pipeline_mode=pl.Buffered(1)), plane]
+    args = [x2, o2, u2, vf, attn, wo_near, wo_far, w_far, dw_qk, *recv]
     return pl.pallas_call(
         functools.partial(far_y_body, early=early, copies=copies),
         grid_spec=pltpu.PrefetchScalarGridSpec(
             num_scalar_prefetch=1,
             grid=(steps,),
-            in_specs=specs + [pl.BlockSpec(memory_space=pl.ANY)] * 2,
-            out_specs=[row(width), pl.BlockSpec((1, rows, width), lambda j, off: (off[1], jnp.minimum(j, sum(copies) - 1), 0))],
-            scratch_shapes=[pltpu.VMEM((rows, cols), BF16)] * 2,
+            in_specs=specs + [any_] * (len(recv) + 2),
+            out_specs=[row(width), pl.BlockSpec((1, rows, width), lambda j, off: (off[1], jnp.minimum(j, sum(copies) - 1), 0)), plane],
+            scratch_shapes=[pltpu.VMEM((rows, cols), BF16)] * 2 + [pltpu.SemaphoreType.DMA],
         ),
-        out_shape=[sds(y2.shape, y2.dtype), sds(gx2.shape, gx2.dtype)],
+        out_shape=[sds(y2.shape, y2.dtype), sds(gx2.shape, gx2.dtype), sds((3, *dw_qk.shape[1:]), F32)],
         input_output_aliases={len(args) + 1: 0, len(args) + 2: 1},
         name="far_y",
         compiler_params=params(),
@@ -368,12 +397,10 @@
 
 
 def token_sum_body(l_ref, r_ref, o_ref):
-    @pl.when(pl.program_id(0) == 0)
-    def _():
-        o_ref[...] = jnp.zeros_like(o_ref)
-
+    first = pl.program_id(0) == 0
     for e in range(r_ref.shape[0]):
-        o_ref[e] += dot(l_ref[...], r_ref[e], TN)
+        val = dot(l_ref[...], r_ref[e], TN)
+        o_ref[e] = jnp.where(first, val, o_ref[e] + val)
 
 
 def token_sum(lhs, rhs):
@@ -408,12 +435,11 @@
         w_near = jnp.transpose(w_qkv, (1, 0, 2))
         w_far = exchange(w_near)
         wo_far = exchange(w_out)
-        gamma, beta = ln_gamma.reshape(1, width), ln_beta.reshape(1, width)
         half = tokens // 2
         off = jnp.stack([me, 1 - me]).astype(jnp.int32)
         halves = lambda t: t.reshape(2, half, t.shape[-1])
 
-        u, q, k, v, do, stats, part = project(x, g, w_near, w_out, gamma, beta)
+        u, q, k, v, do, stats, part = project(x, g, w_near, w_out, ln_gamma, ln_beta)
         x2, g2, u2, stats2 = halves(x), halves(g), halves(u), halves(stats)
         near = tuple(halves(t) for t in (q, k, v, do))
         peers = [lax.ppermute(part, "sp", [(s, s ^ d) for s in range(sp_size)]) for d in (1, 2, 3)]
@@ -428,7 +454,7 @@
 
         prev, dsum, recv, start = (), None, [], 0
         for sizes in OWN_CHUNKS:
-            out = rows_call(off, start, sizes, (x2, g2, u2, stats2) + near, state, (w_near, w_far, w_out, wo_far, gamma), prev)
+            out = rows_call(off, start, sizes, (x2, g2, u2, stats2) + near, state, (w_near, w_far, w_out, wo_far, ln_gamma), prev)
             prev, sent, ds = out[:5], out[5:-1], out[-1]
             recv += [exchange(t) for t in sent]
             dsum = ds if dsum is None else dsum + ds
@@ -447,8 +473,8 @@
         dw_v = token_sum(u, rv.reshape(1, tokens, cols))
         y2, dw_v = lax.optimization_barrier((y2, dw_v))
         dw_v = lax.psum_scatter(dw_v, "sp", scatter_dimension=1, tiled=True)
-        y2, gx2 = far_y(off, x2, o2, u2, vf, attn, w_out, wo_far, w_far, recv[:-1], y2, gx2)
-        grad_wqkv = jnp.transpose(jnp.concatenate([dw_qk, dw_v], axis=0), (1, 0, 2))
+        y2, gx2, gw = far_y(off, x2, o2, u2, vf, attn, w_out, wo_far, w_far, dw_qk, recv[:-1], y2, gx2)
+        grad_wqkv = jnp.transpose(lax.dynamic_update_slice(gw, dw_v, (2, 0, 0)), (1, 0, 2))
 
         sums = jnp.sum(dsum, axis=1)
         for axis, perm in (("tp", swap), ("sp", [(s, s ^ 1) for s in range(sp_size)]), ("sp", [(s, s ^ 2) for s in range(sp_size)])):

time: 1360 us -> 1360 us (level)
  transfers between devices with their start and end apart: 17 -> 17, of which waited for: 5 -> 5; matrix products, arithmetic and copies ran while one was open for 1% -> 1% of each run, Pallas kernels for 22% -> 29%
where the time goes in v5:
time: 1360 us; the launch traced here: 1350 us
  Pallas kernels  833 us (61%)
  waiting for transfers between devices  478 us (35%)
  starting transfers between devices  16.4 us (1%)
  between operations  14.4 us (1%)
    ppermute x3, waiting for transfers between devices, step(): sums = sums + lax.ppermute(sums, axis, perm)  461 us
    pallas_call x4, Pallas kernels, rows_call(): pl.pallas_call(functools.partial(rows_body, n_alias=len(prev), send_block...  356 us
    pallas_call x1, Pallas kernels, project(): pl.pallas_call(project_body, grid=(tokens // PROJ_ROWS,), in_specs=[row(w...  198 us
    pallas_call x3, Pallas kernels, token_sum(): pl.pallas_call(token_sum_body, grid=(tokens // SUM_ROWS,), in_specs=[row_...  185 us
    pallas_call x1, Pallas kernels, far_y(): pl.pallas_call(functools.partial(far_y_body, early=early, copies=copies),...  72 us
  transfers between devices with their start and end apart: 17, of which 5 were waited for; matrix products, arithmetic and copies ran while one was open for 1% of the time, Pallas kernels for 29%

profile of v5, /device:TPU:0, one launch (start us, length us, event | category | flops | bytes accessed | tf_op | source)
XLA Modules:
  0.0 1352.9 jit_solution(11383267887995833986)
XLA Ops:
  7.2 0.0 reduce-scatter.4.cloned.1.call-start
  7.2 3.4 collective-permute-start.4
  10.6 0.0 collective-permute-start.5
  10.6 198.0 %project.1 = (bf16[16384,1536]{1,0:T(8,128)(2,1)}, bf16[16384,768]{1,0:T(8,128)(2,1)}, bf16[16384,768]{1,0:T(8,128)(2,1)}, bf16[16384,768]{1,0:T(8,128)(2,1)}, b...) custom-call(bf16[16384,1536]{1,0:T(8,128)(2,1)} %x_ref.1, bf16[16384,1536]{1,0:T(8,128)(2,1)} %g_ref.1, ...), custom_call_target="tpu_custom_call" | custom-call | flops 170080698368 | bytes 251658240 | tf_op jit(solution)/shard_map/project/pallas_call | solution.py:114
  208.6 0.0 collective-permute-start
  208.6 2.0 collective-permute-start.1
  210.6 0.1 collective-permute-start.2
  210.7 0.1 broadcast_in_dim.10
  210.8 0.1 broadcast_in_dim.11
  210.9 0.1 broadcast_in_dim.12
  211.0 0.3 rev.6
  211.3 0.0 collective-permute-done
  211.3 6.4 collective-permute-done.1
  217.7 4.7 collective-permute-done.2
  222.4 1.0 add_add_fusion.near_ref
  223.4 0.0 copy-start
  223.4 1.6 collective-permute-start.3
  225.0 0.6 reshape.72.tau_ref
  225.6 0.6 pad_add_fusion.refs_0_.off_ref
  226.2 5.2 collective-permute-done.3.far_ref
  231.5 0.7 copy-done.7
  232.1 4.7 head_state.1
  236.8 0.0 collective-permute-done.5.refs_14_.refs_7_
  236.8 0.0 collective-permute-done.4.refs_13_.w_ref.refs_8_
  236.8 47.9 %rows.4 = (bf16[2,8192,1536]{2,1,0:T(8,128)(2,1)}, bf16[2,8192,1536]{2,1,0:T(8,128)(2,1)}, bf16[2,8192,768]{2,1,0:T(8,128)(2,1)}, bf16[2,2,8192,768]{3,2,1,0:T(8...) custom-call(s32[2]{0:T(128)} %pad_add_fusion.refs_0_.off_ref, ...), custom_call_target="tpu_custom_call" | custom-call | flops 31406948352 | bytes 44040192 | tf_op jit(solution)/shard_map/rows/pallas_call | solution.py:306
  284.7 78.0 %rows.5 = (bf16[2,8192,1536]{2,1,0:T(8,128)(2,1)}, bf16[2,8192,1536]{2,1,0:T(8,128)(2,1)}, bf16[2,8192,768]{2,1,0:T(8,128)(2,1)}, bf16[2,2,8192,768]{3,2,1,0:T(8...) custom-call(s32[2]{0:T(128)} %pad_add_fusion.refs_0_.off_ref, ...), custom_call_target="tpu_custom_call", output_to_operand_aliasing={{0}: (17, {}), {1}: (18, {}), {2}: (19, {}), {3}: (20, {}),... | custom-call | flops 47110422528 | bytes 66060288 | tf_op jit(solution)/shard_map/rows/pallas_call | solution.py:306
  362.7 105.2 %rows.6 = (bf16[2,8192,1536]{2,1,0:T(8,128)(2,1)}, bf16[2,8192,1536]{2,1,0:T(8,128)(2,1)}, bf16[2,8192,768]{2,1,0:T(8,128)(2,1)}, bf16[2,2,8192,768]{3,2,1,0:T(8...) custom-call(s32[2]{0:T(128)} %pad_add_fusion.refs_0_.off_ref, ...), custom_call_target="tpu_custom_call", output_to_operand_aliasing={{0}: (17, {}), {1}: (18, {}), {2}: (19, {}), {3}: (20, {}),... | custom-call | flops 78517370880 | bytes 110100480 | tf_op jit(solution)/shard_map/rows/pallas_call | solution.py:306
  467.9 125.1 %rows.7 = (bf16[2,8192,1536]{2,1,0:T(8,128)(2,1)}, bf16[2,8192,1536]{2,1,0:T(8,128)(2,1)}, bf16[2,8192,768]{2,1,0:T(8,128)(2,1)}, bf16[2,2,8192,768]{3,2,1,0:T(8...) custom-call(s32[2]{0:T(128)} %pad_add_fusion.refs_0_.off_ref, ...), custom_call_target="tpu_custom_call", output_to_operand_aliasing={{0}: (17, {}), {1}: (18, {}), {2}: (19, {}), {3}: (20, {}),... | custom-call | flops 94220845056 | bytes 132120576 | tf_op jit(solution)/shard_map/rows/pallas_call | solution.py:306
  593.1 88.9 %token_sum.3 = f32[2,1536,768]{2,1,0:T(8,128)} custom-call(bf16[16384,1536]{1,0:T(8,128)(2,1)} %get-tuple-element.58.l_ref, bf16[2,16384,768]{2,1,0:T(8,128)(2,1)} %bitcast.43), custom_call_target="tpu_custom_call" | custom-call | flops 77309411328 | bytes 100663296 | tf_op jit(solution)/shard_map/token_sum/pallas_call | solution.py:409
  682.0 0.0 reduce-scatter.4.cloned.1.call-update
  682.0 0.0 reduce-scatter.6.cloned.1.call-start
  682.0 48.3 %token_sum.4 = f32[1,768,1536]{2,1,0:T(8,128)} custom-call(bf16[16384,768]{1,0:T(8,128)(2,1)} %bitcast.60, bf16[1,16384,1536]{2,1,0:T(8,128)(2,1)} %bitcast.42), custom_call_target="tpu_custom_call" | custom-call | flops 38654705664 | bytes 75497472 | tf_op jit(solution)/shard_map/token_sum/pallas_call | solution.py:409
  730.4 47.9 %token_sum.5 = f32[1,1536,768]{2,1,0:T(8,128)} custom-call(bf16[16384,1536]{1,0:T(8,128)(2,1)} %get-tuple-element.58.l_ref, bf16[1,16384,768]{2,1,0:T(8,128)(2,1)} %bitcast.61), custom_call_target="tpu_custom_call" | custom-call | flops 38654705664 | bytes 75497472 | tf_op jit(solution)/shard_map/token_sum/pallas_call | solution.py:409
  778.3 0.0 reduce-scatter.6.cloned.1.call-update
  778.3 0.0 reduce-scatter.8.cloned.1.call-start
  778.4 1.7 collective-permute-start.8
  780.0 0.4 collective-permute-start.9
  780.4 1.6 collective-permute-start.7
  782.1 0.0 reduce-scatter.8.cloned.1.call-update
  782.1 0.4 collective-permute-start.6
  782.5 0.1 add_reduce_fusion
  782.6 1.7 collective-permute-start.11
  784.2 9.1 far_v.2.refs_0_
  793.3 459.8 %collective-permute-done.11 = f32[2,1536]{1,0:T(2,128)S(1)} collective-permute-done((f32[2,1536]{1,0:T(2,128)S(1)}, f32[2,1536]{1,0:T(2,128)S(1)}, u32[]{:S(2)}, u32[]{:S(2)}) %collective-permute-start.11) | collective-permute-done | bytes 12320 | tf_op jit(solution)/shard_map/ppermute | solution.py:481
  1253.1 0.0 copy-start.5
  1253.1 0.0 collective-permute-start.12
  1253.1 8.2 far_v.3.refs_4_
  1261.3 0.1 reshape.78
  1261.4 0.1 reduce_sum.19
  1261.5 0.0 collective-permute-done.12
  1261.6 1.7 collective-permute-start.13
  1263.3 0.6 reshape.79
  1263.9 1.4 collective-permute-done.13
  1265.3 1.7 collective-permute-start.10
  1267.0 0.6 slice_reduce_fusion
  1267.7 0.0 collective-permute-done.6.refs_10_
  1267.7 0.0 collective-permute-done.9.refs_13_
  1267.7 0.0 collective-permute-done.8.refs_12_
  1267.7 0.0 reduce-scatter.4.cloned.1.call-done.refs_9_
  1267.7 72.0 %far_y.1 = (bf16[2,8192,1536]{2,1,0:T(8,128)(2,1)}, bf16[2,8192,1536]{2,1,0:T(8,128)(2,1)}, f32[3,384,768]{2,1,0:T(8,128)}) custom-call(s32[2]{0:T(128)} %pad_add_fusion.refs_0_.off_ref, bf16[2,8192,1536]{2,1,0:T(8,128)(2,1)} %bitcast.35, bf16[2,8192,768]{2,1,0:T(8,128)(2,1)} %get-tuple-element.87.refs_2_, ...), custom_call_target="tpu_custom_call", output_to_operand_aliasing={{0}: (14, {}), {1}: (15, {})} | custom-call | flops 54116589568 | bytes 138412032 | tf_op jit(solution)/shard_map/far_y/pallas_call | solution.py:382
  1339.7 0.0 reduce-scatter.6.cloned.1.call-done
  1339.8 2.4 constant_dynamic-update-slice_fusion
  1342.1 0.0 collective-permute-done.10
  1342.1 3.8 constant_dynamic-update-slice_fusion.1
  (23 shorter events, 0.1 us)
Async XLA Ops:
  7.2 1260.5 %reduce-scatter.4.cloned.1.call-start = ((), (), s32[]{:S(2)}) async-start(), calls=%async_computation.3 | async-start | bytes 11796480 | tf_op jit(solution)/shard_map/reduce_scatter | solution.py:469
  7.2 229.6 %collective-permute-start.4 = (bf16[3,1536,768]{2,1,0:T(8,128)(2,1)}, bf16[3,1536,768]{2,1,0:T(8,128)(2,1)}, u32[]{:S(2)}, u32[]{:S(2)}) collective-permute-start(bf16[3,1536,768]{2,1,0:T(8,128)(2,1)} %bitcast.66), channel_id=1, source_target_pairs={{0,4},{4,0},{1,5},{5,1},{2,6},{6,2},{3,7},{7,3}} | collective-permute-start | bytes 21233672 | tf_op jit(solution)/shard_map/ppermute | solution.py:428
  10.6 226.2 %collective-permute-start.5 = (bf16[768,1536]{1,0:T(8,128)(2,1)}, bf16[768,1536]{1,0:T(8,128)(2,1)}, u32[]{:S(2)}, u32[]{:S(2)}) collective-permute-start(bf16[768,1536]{1,0:T(8,128)(2,1)} %refs_6_.1), channel_id=1, source_target_pairs={{0,4},{4,0},{1,5},{5,1},{2,6},{6,2},{3,7},{7,3}} | collective-permute-start | bytes 7077896 | tf_op jit(solution)/shard_map/ppermute | solution.py:428
  10.6 200.1 %copy-start.6 = (f32[48]{0:T(128)S(1)}, f32[48]{0:T(128)}, u32[]{:S(2)}) copy-start(f32[48]{0:T(128)} %param.13) | copy-start | bytes 580
  208.6 2.7 collective-permute-start
  208.6 9.1 collective-permute-start.1
  210.6 11.8 collective-permute-start.2
  223.4 8.0 copy-start
  223.4 8.0 collective-permute-start.3
  231.4 0.7 copy-start.7
  682.0 657.8 %reduce-scatter.6.cloned.1.call-start = ((), (), s32[]{:S(2)}) async-start(), calls=%async_computation.4 | async-start | bytes 5898240 | tf_op jit(solution)/shard_map/reduce_scatter | solution.py:475
  730.3 52.2 %copy-start.1 = (f32[2,8,1536]{2,1,0:T(8,128)S(1)}, f32[2,8,1536]{2,1,0:T(8,128)}, u32[]{:S(2)}) copy-start(f32[2,8,1536]{2,1,0:T(8,128)} %get-tuple-element.104) | copy-start | bytes 294916
  730.3 52.2 %copy-start.2 = (f32[2,8,1536]{2,1,0:T(8,128)S(1)}, f32[2,8,1536]{2,1,0:T(8,128)}, u32[]{:S(2)}) copy-start(f32[2,8,1536]{2,1,0:T(8,128)} %get-tuple-element.105) | copy-start | bytes 294916
  730.4 52.2 %copy-start.3 = (f32[2,8,1536]{2,1,0:T(8,128)S(1)}, f32[2,8,1536]{2,1,0:T(8,128)}, u32[]{:S(2)}) copy-start(f32[2,8,1536]{2,1,0:T(8,128)} %get-tuple-element.106) | copy-start | bytes 294916
  730.4 52.2 %copy-start.4 = (f32[2,8,1536]{2,1,0:T(8,128)S(1)}, f32[2,8,1536]{2,1,0:T(8,128)}, u32[]{:S(2)}) copy-start(f32[2,8,1536]{2,1,0:T(8,128)} %get-tuple-element.107) | copy-start | bytes 294916
  778.3 567.5 %reduce-scatter.8.cloned.1.call-start = ((), (), s32[]{:S(2)}) async-start(), calls=%async_computation.5 | async-start | bytes 5898240 | tf_op jit(solution)/shard_map/reduce_scatter | solution.py:472
  778.4 489.3 %collective-permute-start.8 = (bf16[1,2560,1536]{2,1,0:T(8,128)(2,1)}, bf16[1,2560,1536]{2,1,0:T(8,128)(2,1)}, u32[]{:S(2)}, u32[]{:S(2)}) collective-permute-start(bf16[1,2560,1536]{2,1,0:T(8,128)(2,1)} %get-tuple-element.91), channel_id=1, source_target_pairs={{0,4},{4,0},{1,5},{5,1},{2,6},{6,2},{3,7},{7,3}} | collective-permute-start | bytes 23592968 | tf_op jit(solution)/shard_map/ppermute | solution.py:428
  780.0 487.6 %collective-permute-start.9 = (bf16[1,2048,1536]{2,1,0:T(8,128)(2,1)}, bf16[1,2048,1536]{2,1,0:T(8,128)(2,1)}, u32[]{:S(2)}, u32[]{:S(2)}) collective-permute-start(bf16[1,2048,1536]{2,1,0:T(8,128)(2,1)} %get-tuple-element.92), channel_id=1, source_target_pairs={{0,4},{4,0},{1,5},{5,1},{2,6},{6,2},{3,7},{7,3}} | collective-permute-start | bytes 18874376 | tf_op jit(solution)/shard_map/ppermute | solution.py:428
  780.4 487.2 %collective-permute-start.7 = (bf16[1,1536,1536]{2,1,0:T(8,128)(2,1)}, bf16[1,1536,1536]{2,1,0:T(8,128)(2,1)}, u32[]{:S(2)}, u32[]{:S(2)}) collective-permute-start(bf16[1,1536,1536]{2,1,0:T(8,128)(2,1)} %get-tuple-element.90), channel_id=1, source_target_pairs={{0,4},{4,0},{1,5},{5,1},{2,6},{6,2},{3,7},{7,3}} | collective-permute-start | bytes 14155784 | tf_op jit(solution)/shard_map/ppermute | solution.py:428
  782.1 485.6 %collective-permute-start.6 = (bf16[1,1024,1536]{2,1,0:T(8,128)(2,1)}, bf16[1,1024,1536]{2,1,0:T(8,128)(2,1)}, u32[]{:S(2)}, u32[]{:S(2)}) collective-permute-start(bf16[1,1024,1536]{2,1,0:T(8,128)(2,1)} %get-tuple-element.89), channel_id=1, source_target_pairs={{0,4},{4,0},{1,5},{5,1},{2,6},{6,2},{3,7},{7,3}} | collective-permute-start | bytes 9437192 | tf_op jit(solution)/shard_map/ppermute | solution.py:428
  782.6 470.5 %collective-permute-start.11 = (f32[2,1536]{1,0:T(2,128)S(1)}, f32[2,1536]{1,0:T(2,128)S(1)}, u32[]{:S(2)}, u32[]{:S(2)}) collective-permute-start(f32[2,1536]{1,0:T(2,128)S(1)} %add_reduce_fusion), channel_id=1, source_target_pairs={{0,4},{4,0},{1,5},{5,1},{2,6},{6,2},{3,7},{7,3}} | collective-permute-start | bytes 36872 | tf_op jit(solution)/shard_map/ppermute | solution.py:481
  1253.1 8.2 copy-start.5
  1253.1 8.4 collective-permute-start.12
  1261.6 3.7 collective-permute-start.13
  1265.3 76.9 %collective-permute-start.10 = (bf16[1,1024,1536]{2,1,0:T(8,128)(2,1)}, bf16[1,1024,1536]{2,1,0:T(8,128)(2,1)}, u32[]{:S(2)}, u32[]{:S(2)}) collective-permute-start(bf16[1,1024,1536]{2,1,0:T(8,128)(2,1)} %get-tuple-element.100), channel_id=1, source_target_pairs={{0,4},{4,0},{1,5},{5,1},{2,6},{6,2},{3,7},{7,3}} | collective-permute-start | bytes 9437192 | tf_op jit(solution)/shard_map/ppermute | solution.py:428
Sparse Core Ops, SparseCore 0:
  682.1 73.5 reduce-scatter.3
  778.5 43.3 reduce-scatter.5
  825.0 42.4 reduce-scatter.7

commit v6 on v5

--- a/solution.py
+++ b/solution.py
@@ -19,6 +19,7 @@
 TN = (((0,), (0,)), ((), ()))
 PROJ_ROWS = 1024
 ROWS = 256
+LOAD_PIECES = 2
 SUM_ROWS = 1024
 OWN_CHUNKS = ((4,), (6,), (10,), (8, 4))
 EARLY_V = 12
@@ -208,21 +209,6 @@
     return dot(v, am, NT).astype(BF16), dq.astype(BF16), dk.astype(BF16), dot(do, am, NN).astype(BF16)
 
 
-def finish_rows(j, x_ref, g_ref, st_ref, du, gm_ref, dx_refs, dsum_ref):
-    rows, width = x_ref.shape[1:]
-    mean, inv = st_ref[0, :, :1], st_ref[0, :, LANES // 2:LANES // 2 + 1]
-    xh = (x_ref[0].astype(F32) - mean) * inv
-    fold = lambda t: jnp.sum(t.reshape(rows // 8, 8, width), axis=0)
-    for a, val in enumerate((fold(du * xh), fold(du))):
-        dsum_ref[a] = jnp.where(j == 0, val, dsum_ref[a] + val)
-    gh = du * gm_ref[...].reshape(1, width)
-    m1 = jnp.mean(gh, axis=-1, keepdims=True)
-    m2 = jnp.mean(gh * xh, axis=-1, keepdims=True)
-    dx = (g_ref[0].astype(F32) + inv * (gh - m1 - xh * m2)).astype(BF16)
-    for ref in dx_refs:
-        ref[0] = dx
-
-
 def rows_body(*refs, n_alias, send_blocks):
     it = iter(refs)
     nxt = lambda n: [next(it) for _ in range(n)]
@@ -233,16 +219,25 @@
     y_ref, gx_ref, o_ref, rqk_ref, rv_ref = nxt(5)
     send_refs = nxt(len(send_blocks))
     (dsum_ref,) = nxt(1)
-    on_s, rn_s, of_s, rf_s, qf_s, kf_s, vf_s, dof_s = nxt(8)
+    on_s, rn_s, of_s, rf_s, qf_s, kf_s, vf_s, dof_s, gh_s = nxt(9)
     w_refs, w_sems = nxt(4), nxt(1)[0]
     wf_ref, wof_ref, wn_ref, won_ref = w_refs
     j = pl.program_id(0)
     own, other = off_ref[0], off_ref[1]
     groups = attn_ref.shape[0] // 2
     state = (attn_ref, dgram_ref, coef_ref)
-    loads = [pltpu.make_async_copy(src, dst, w_sems.at[n]) for n, (src, dst) in enumerate(zip(w_hbm, w_refs))]
-
-    def compute(wait):
+    waits = [pltpu.make_async_copy(src, dst, w_sems.at[n]) for n, (src, dst) in enumerate(zip(w_hbm, w_refs))]
+
+    def start_loads():
+        for n, (src, dst) in enumerate(zip(w_hbm, w_refs)):
+            pieces = [(e,) for e in range(src.shape[0])] if len(src.shape) == 3 else [()]
+            size = src.shape[-2] // LOAD_PIECES
+            for p in pieces:
+                for r in range(0, src.shape[-2], size):
+                    at = (*p, pl.ds(r, size))
+                    pltpu.make_async_copy(src.at[at], dst.at[at], w_sems.at[n]).start()
+
+    def compute(wait, first):
         for s in range(groups):
             c = slice(s * GROUP, (s + 1) * GROUP)
             for half in (own, other):
@@ -262,23 +257,44 @@
                 qf_s[:, c], kf_s[:, c], vf_s[:, c], dof_s[:, c], *state, 1, s)
         wait(2)
         wait(3)
-        du = dot(rn_s[0], wn_ref[0], NT)
-        for e in range(1, 3):
-            du += dot(rn_s[e], wn_ref[e], NT)
-        for e in range(3):
-            du += dot(rf_s[e], wf_ref[e], NT)
-        y_ref[0] = (x_ref[0].astype(F32) + (dot(on_s[...], won_ref[...]) + dot(of_s[...], wof_ref[...]))).astype(BF16)
-        finish_rows(j, x_ref, g_ref, st_ref, du, gm_ref, [gx_ref] + send_refs[:1] * (len(send_refs) == 1), dsum_ref)
+        rows, width = gh_s.shape
+        mean, inv = st_ref[0, :, :1], st_ref[0, :, LANES // 2:LANES // 2 + 1]
+        fold = lambda t: jnp.sum(t.reshape(rows // 8, 8, GROUP), axis=0)
+        lanes = lambda t: sum(t[:, k:k + LANES] for k in range(0, GROUP, LANES))
+        gamma = gm_ref[...].reshape(1, width)
+        tiles = [slice(n, n + GROUP) for n in range(0, width, GROUP)]
+        s1 = s2 = 0.0
+        for c in tiles:
+            du = dot(rn_s[0], wn_ref[0, c, :], NT)
+            for e in range(1, 3):
+                du += dot(rn_s[e], wn_ref[e, c, :], NT)
+            for e in range(3):
+                du += dot(rf_s[e], wf_ref[e, c, :], NT)
+            xh = (x_ref[0, :, c].astype(F32) - mean) * inv
+            for a, val in enumerate((fold(du * xh), fold(du))):
+                dsum_ref[a, :, c] = val if first else dsum_ref[a, :, c] + val
+            gh = du * gamma[:, c]
+            s1 += lanes(gh)
+            s2 += lanes(gh * xh)
+            gh_s[:, c] = gh
+        m1 = jnp.sum(s1, axis=1, keepdims=True) / width
+        m2 = jnp.sum(s2, axis=1, keepdims=True) / width
+        for c in tiles:
+            x = x_ref[0, :, c].astype(F32)
+            yp = dot(on_s[...], won_ref[:, c]) + dot(of_s[...], wof_ref[:, c])
+            y_ref[0, :, c] = (x + yp).astype(BF16)
+            dx = g_ref[0, :, c].astype(F32) + inv * (gh_s[:, c] - m1 - (x - mean) * inv * m2)
+            for ref in [gx_ref] + send_refs[:1] * (len(send_refs) == 1):
+                ref[0, :, c] = dx.astype(BF16)
 
     @pl.when(j == 0)
     def _():
-        for load in loads:
-            load.start()
-        compute(lambda n: loads[n].wait())
+        start_loads()
+        compute(lambda n: waits[n].wait(), True)
 
     @pl.when(j > 0)
     def _():
-        compute(lambda n: None)
+        compute(lambda n: None, False)
 
     if len(send_refs) > 1:
         start = 0
@@ -313,7 +329,7 @@
                        *[send_spec(first, n) for first, n in zip(firsts, send_blocks)],
                        pl.BlockSpec((2, 8, width), lambda j, off: (0, 0, 0))],
             scratch_shapes=[pltpu.VMEM((ROWS, cols), BF16), pltpu.VMEM((3, ROWS, cols), BF16)] * 2 + [pltpu.VMEM((ROWS, cols), BF16)] * 4
-            + [pltpu.VMEM(t.shape, t.dtype) for t in loaded] + [pltpu.SemaphoreType.DMA((len(loaded),))],
+            + [pltpu.VMEM((ROWS, width), F32)] + [pltpu.VMEM(t.shape, t.dtype) for t in loaded] + [pltpu.SemaphoreType.DMA((len(loaded),))],
         ),
         out_shape=[sds((2, half, width), BF16)] * 2 + [sds((2, half, cols), BF16), sds((2, 2, half, cols), BF16), sds((2, half, cols), BF16),
                                                        *[sds((1, n * ROWS, width), BF16) for n in send_blocks], sds((2, 8, width), F32)],

time: 1360 us -> 1350 us (level)
  no operation moved by 1% of the time
where the time goes in v6:
time: 1350 us
  Pallas kernels  826 us (61%)
  waiting for transfers between devices  478 us (35%)
  starting transfers between devices  16.4 us (1%)
  between operations  14.4 us (1%)
    ppermute x3, waiting for transfers between devices, step(): sums = sums + lax.ppermute(sums, axis, perm)  461 us
    pallas_call x4, Pallas kernels, rows_call(): pl.pallas_call(functools.partial(rows_body, n_alias=len(prev), send_block...  349 us
    pallas_call x1, Pallas kernels, project(): pl.pallas_call(project_body, grid=(tokens // PROJ_ROWS,), in_specs=[row(w...  198 us
    pallas_call x3, Pallas kernels, token_sum(): pl.pallas_call(token_sum_body, grid=(tokens // SUM_ROWS,), in_specs=[row_...  185 us
    pallas_call x1, Pallas kernels, far_y(): pl.pallas_call(functools.partial(far_y_body, early=early, copies=copies),...  72 us
  transfers between devices with their start and end apart: 17, of which 5 were waited for; matrix products, arithmetic and copies ran while one was open for 1% of the time, Pallas kernels for 29%

profile of v6, /device:TPU:0, one launch (start us, length us, event | category | flops | bytes accessed | tf_op | source)
XLA Modules:
  0.0 1345.1 jit_solution(7295308747592896777)
XLA Ops:
  7.2 0.0 reduce-scatter.4.cloned.1.call-start
  7.2 3.4 collective-permute-start.4
  10.6 0.0 collective-permute-start.5
  10.6 198.0 %project.1 = (bf16[16384,1536]{1,0:T(8,128)(2,1)}, bf16[16384,768]{1,0:T(8,128)(2,1)}, bf16[16384,768]{1,0:T(8,128)(2,1)}, bf16[16384,768]{1,0:T(8,128)(2,1)}, b...) custom-call(bf16[16384,1536]{1,0:T(8,128)(2,1)} %x_ref.1, bf16[16384,1536]{1,0:T(8,128)(2,1)} %g_ref.1, ...), custom_call_target="tpu_custom_call" | custom-call | flops 170080698368 | bytes 251658240 | tf_op jit(solution)/shard_map/project/pallas_call | solution.py:115
  208.6 0.0 collective-permute-start
  208.6 2.0 collective-permute-start.1
  210.6 0.1 collective-permute-start.2
  210.7 0.1 broadcast_in_dim.10
  210.8 0.1 broadcast_in_dim.11
  210.9 0.1 broadcast_in_dim.12
  211.0 0.3 rev.6
  211.3 0.0 collective-permute-done
  211.3 6.4 collective-permute-done.1
  217.7 4.7 collective-permute-done.2
  222.4 1.0 add_add_fusion.near_ref
  223.4 0.0 copy-start
  223.4 1.6 collective-permute-start.3
  225.0 0.6 reshape.72.tau_ref
  225.6 0.6 pad_add_fusion.refs_0_.off_ref
  226.2 5.2 collective-permute-done.3.far_ref
  231.5 0.7 copy-done.7
  232.1 4.7 head_state.1
  236.8 0.0 collective-permute-done.5.refs_14_.refs_7_
  236.8 0.0 collective-permute-done.4.refs_13_.w_ref.refs_8_
  236.8 47.0 %rows.4 = (bf16[2,8192,1536]{2,1,0:T(8,128)(2,1)}, bf16[2,8192,1536]{2,1,0:T(8,128)(2,1)}, bf16[2,8192,768]{2,1,0:T(8,128)(2,1)}, bf16[2,2,8192,768]{3,2,1,0:T(8...) custom-call(s32[2]{0:T(128)} %pad_add_fusion.refs_0_.off_ref, ...), custom_call_target="tpu_custom_call" | custom-call | flops 31406948352 | bytes 44040192 | tf_op jit(solution)/shard_map/rows/pallas_call | solution.py:322
  283.8 76.4 %rows.5 = (bf16[2,8192,1536]{2,1,0:T(8,128)(2,1)}, bf16[2,8192,1536]{2,1,0:T(8,128)(2,1)}, bf16[2,8192,768]{2,1,0:T(8,128)(2,1)}, bf16[2,2,8192,768]{3,2,1,0:T(8...) custom-call(s32[2]{0:T(128)} %pad_add_fusion.refs_0_.off_ref, ...), custom_call_target="tpu_custom_call", output_to_operand_aliasing={{0}: (17, {}), {1}: (18, {}), {2}: (19, {}), {3}: (20, {}),... | custom-call | flops 47110422528 | bytes 66060288 | tf_op jit(solution)/shard_map/rows/pallas_call | solution.py:322
  360.2 102.8 %rows.6 = (bf16[2,8192,1536]{2,1,0:T(8,128)(2,1)}, bf16[2,8192,1536]{2,1,0:T(8,128)(2,1)}, bf16[2,8192,768]{2,1,0:T(8,128)(2,1)}, bf16[2,2,8192,768]{3,2,1,0:T(8...) custom-call(s32[2]{0:T(128)} %pad_add_fusion.refs_0_.off_ref, ...), custom_call_target="tpu_custom_call", output_to_operand_aliasing={{0}: (17, {}), {1}: (18, {}), {2}: (19, {}), {3}: (20, {}),... | custom-call | flops 78517370880 | bytes 110100480 | tf_op jit(solution)/shard_map/rows/pallas_call | solution.py:322
  463.0 122.4 %rows.7 = (bf16[2,8192,1536]{2,1,0:T(8,128)(2,1)}, bf16[2,8192,1536]{2,1,0:T(8,128)(2,1)}, bf16[2,8192,768]{2,1,0:T(8,128)(2,1)}, bf16[2,2,8192,768]{3,2,1,0:T(8...) custom-call(s32[2]{0:T(128)} %pad_add_fusion.refs_0_.off_ref, ...), custom_call_target="tpu_custom_call", output_to_operand_aliasing={{0}: (17, {}), {1}: (18, {}), {2}: (19, {}), {3}: (20, {}),... | custom-call | flops 94220845056 | bytes 132120576 | tf_op jit(solution)/shard_map/rows/pallas_call | solution.py:322
  585.4 88.9 %token_sum.3 = f32[2,1536,768]{2,1,0:T(8,128)} custom-call(bf16[16384,1536]{1,0:T(8,128)(2,1)} %get-tuple-element.58.l_ref, bf16[2,16384,768]{2,1,0:T(8,128)(2,1)} %bitcast.43), custom_call_target="tpu_custom_call" | custom-call | flops 77309411328 | bytes 100663296 | tf_op jit(solution)/shard_map/token_sum/pallas_call | solution.py:425
  674.2 0.0 reduce-scatter.4.cloned.1.call-update
  674.3 0.0 reduce-scatter.6.cloned.1.call-start
  674.3 48.3 %token_sum.4 = f32[1,768,1536]{2,1,0:T(8,128)} custom-call(bf16[16384,768]{1,0:T(8,128)(2,1)} %bitcast.60, bf16[1,16384,1536]{2,1,0:T(8,128)(2,1)} %bitcast.42), custom_call_target="tpu_custom_call" | custom-call | flops 38654705664 | bytes 75497472 | tf_op jit(solution)/shard_map/token_sum/pallas_call | solution.py:425
  722.6 47.9 %token_sum.5 = f32[1,1536,768]{2,1,0:T(8,128)} custom-call(bf16[16384,1536]{1,0:T(8,128)(2,1)} %get-tuple-element.58.l_ref, bf16[1,16384,768]{2,1,0:T(8,128)(2,1)} %bitcast.61), custom_call_target="tpu_custom_call" | custom-call | flops 38654705664 | bytes 75497472 | tf_op jit(solution)/shard_map/token_sum/pallas_call | solution.py:425
  770.6 0.0 reduce-scatter.6.cloned.1.call-update
  770.6 0.0 reduce-scatter.8.cloned.1.call-start
  770.7 1.7 collective-permute-start.8
  772.3 0.4 collective-permute-start.9
  772.7 1.6 collective-permute-start.7
  774.3 0.0 reduce-scatter.8.cloned.1.call-update
  774.4 0.4 collective-permute-start.6
  774.8 0.1 add_reduce_fusion
  774.8 1.7 collective-permute-start.11
  776.5 9.1 far_v.2.refs_0_
  785.6 459.8 %collective-permute-done.11 = f32[2,1536]{1,0:T(2,128)S(1)} collective-permute-done((f32[2,1536]{1,0:T(2,128)S(1)}, f32[2,1536]{1,0:T(2,128)S(1)}, u32[]{:S(2)}, u32[]{:S(2)}) %collective-permute-start.11) | collective-permute-done | bytes 12320 | tf_op jit(solution)/shard_map/ppermute | solution.py:497
  1245.4 0.0 copy-start.5
  1245.4 0.0 collective-permute-start.12
  1245.4 8.2 far_v.3.refs_4_
  1253.6 0.1 reshape.78
  1253.7 0.1 reduce_sum.19
  1253.8 0.0 collective-permute-done.12
  1253.8 1.7 collective-permute-start.13
  1255.5 0.6 reshape.79
  1256.1 1.4 collective-permute-done.13
  1257.5 1.7 collective-permute-start.10
  1259.3 0.6 slice_reduce_fusion
  1259.9 0.0 collective-permute-done.6.refs_10_
  1259.9 0.0 collective-permute-done.7.refs_11_
  1259.9 0.0 collective-permute-done.9.refs_13_
  1259.9 0.0 collective-permute-done.8.refs_12_
  1259.9 0.0 reduce-scatter.4.cloned.1.call-done.refs_9_
  1260.0 72.0 %far_y.1 = (bf16[2,8192,1536]{2,1,0:T(8,128)(2,1)}, bf16[2,8192,1536]{2,1,0:T(8,128)(2,1)}, f32[3,384,768]{2,1,0:T(8,128)}) custom-call(s32[2]{0:T(128)} %pad_add_fusion.refs_0_.off_ref, bf16[2,8192,1536]{2,1,0:T(8,128)(2,1)} %bitcast.35, bf16[2,8192,768]{2,1,0:T(8,128)(2,1)} %get-tuple-element.87.refs_2_, ...), custom_call_target="tpu_custom_call", output_to_operand_aliasing={{0}: (14, {}), {1}: (15, {})} | custom-call | flops 54116589568 | bytes 138412032 | tf_op jit(solution)/shard_map/far_y/pallas_call | solution.py:398
  1332.0 0.0 reduce-scatter.6.cloned.1.call-done
  1332.0 2.4 constant_dynamic-update-slice_fusion
  1334.4 3.8 constant_dynamic-update-slice_fusion.1
  (23 shorter events, 0.1 us)
Async XLA Ops:
  7.2 1252.8 %reduce-scatter.4.cloned.1.call-start = ((), (), s32[]{:S(2)}) async-start(), calls=%async_computation.3 | async-start | bytes 11796480 | tf_op jit(solution)/shard_map/reduce_scatter | solution.py:485
  7.2 229.6 %collective-permute-start.4 = (bf16[3,1536,768]{2,1,0:T(8,128)(2,1)}, bf16[3,1536,768]{2,1,0:T(8,128)(2,1)}, u32[]{:S(2)}, u32[]{:S(2)}) collective-permute-start(bf16[3,1536,768]{2,1,0:T(8,128)(2,1)} %bitcast.66), channel_id=1, source_target_pairs={{0,4},{4,0},{1,5},{5,1},{2,6},{6,2},{3,7},{7,3}} | collective-permute-start | bytes 21233672 | tf_op jit(solution)/shard_map/ppermute | solution.py:444
  10.6 226.2 %collective-permute-start.5 = (bf16[768,1536]{1,0:T(8,128)(2,1)}, bf16[768,1536]{1,0:T(8,128)(2,1)}, u32[]{:S(2)}, u32[]{:S(2)}) collective-permute-start(bf16[768,1536]{1,0:T(8,128)(2,1)} %refs_6_.1), channel_id=1, source_target_pairs={{0,4},{4,0},{1,5},{5,1},{2,6},{6,2},{3,7},{7,3}} | collective-permute-start | bytes 7077896 | tf_op jit(solution)/shard_map/ppermute | solution.py:444
  10.6 200.1 %copy-start.6 = (f32[48]{0:T(128)S(1)}, f32[48]{0:T(128)}, u32[]{:S(2)}) copy-start(f32[48]{0:T(128)} %param.13) | copy-start | bytes 580
  208.6 2.7 collective-permute-start
  208.6 9.1 collective-permute-start.1
  210.6 11.8 collective-permute-start.2
  223.4 8.0 copy-start
  223.4 8.0 collective-permute-start.3
  231.4 0.7 copy-start.7
  674.3 657.8 %reduce-scatter.6.cloned.1.call-start = ((), (), s32[]{:S(2)}) async-start(), calls=%async_computation.4 | async-start | bytes 5898240 | tf_op jit(solution)/shard_map/reduce_scatter | solution.py:491
  722.6 52.2 %copy-start.1 = (f32[2,8,1536]{2,1,0:T(8,128)S(1)}, f32[2,8,1536]{2,1,0:T(8,128)}, u32[]{:S(2)}) copy-start(f32[2,8,1536]{2,1,0:T(8,128)} %get-tuple-element.104) | copy-start | bytes 294916
  722.6 52.2 %copy-start.2 = (f32[2,8,1536]{2,1,0:T(8,128)S(1)}, f32[2,8,1536]{2,1,0:T(8,128)}, u32[]{:S(2)}) copy-start(f32[2,8,1536]{2,1,0:T(8,128)} %get-tuple-element.105) | copy-start | bytes 294916
  722.6 52.2 %copy-start.3 = (f32[2,8,1536]{2,1,0:T(8,128)S(1)}, f32[2,8,1536]{2,1,0:T(8,128)}, u32[]{:S(2)}) copy-start(f32[2,8,1536]{2,1,0:T(8,128)} %get-tuple-element.106) | copy-start | bytes 294916
  722.6 52.2 %copy-start.4 = (f32[2,8,1536]{2,1,0:T(8,128)S(1)}, f32[2,8,1536]{2,1,0:T(8,128)}, u32[]{:S(2)}) copy-start(f32[2,8,1536]{2,1,0:T(8,128)} %get-tuple-element.107) | copy-start | bytes 294916
  770.6 567.5 %reduce-scatter.8.cloned.1.call-start = ((), (), s32[]{:S(2)}) async-start(), calls=%async_computation.5 | async-start | bytes 5898240 | tf_op jit(solution)/shard_map/reduce_scatter | solution.py:488
  770.7 489.3 %collective-permute-start.8 = (bf16[1,2560,1536]{2,1,0:T(8,128)(2,1)}, bf16[1,2560,1536]{2,1,0:T(8,128)(2,1)}, u32[]{:S(2)}, u32[]{:S(2)}) collective-permute-start(bf16[1,2560,1536]{2,1,0:T(8,128)(2,1)} %get-tuple-element.91), channel_id=1, source_target_pairs={{0,4},{4,0},{1,5},{5,1},{2,6},{6,2},{3,7},{7,3}} | collective-permute-start | bytes 23592968 | tf_op jit(solution)/shard_map/ppermute | solution.py:444
  772.3 487.6 %collective-permute-start.9 = (bf16[1,2048,1536]{2,1,0:T(8,128)(2,1)}, bf16[1,2048,1536]{2,1,0:T(8,128)(2,1)}, u32[]{:S(2)}, u32[]{:S(2)}) collective-permute-start(bf16[1,2048,1536]{2,1,0:T(8,128)(2,1)} %get-tuple-element.92), channel_id=1, source_target_pairs={{0,4},{4,0},{1,5},{5,1},{2,6},{6,2},{3,7},{7,3}} | collective-permute-start | bytes 18874376 | tf_op jit(solution)/shard_map/ppermute | solution.py:444
  772.7 487.2 %collective-permute-start.7 = (bf16[1,1536,1536]{2,1,0:T(8,128)(2,1)}, bf16[1,1536,1536]{2,1,0:T(8,128)(2,1)}, u32[]{:S(2)}, u32[]{:S(2)}) collective-permute-start(bf16[1,1536,1536]{2,1,0:T(8,128)(2,1)} %get-tuple-element.90), channel_id=1, source_target_pairs={{0,4},{4,0},{1,5},{5,1},{2,6},{6,2},{3,7},{7,3}} | collective-permute-start | bytes 14155784 | tf_op jit(solution)/shard_map/ppermute | solution.py:444
  774.4 485.5 %collective-permute-start.6 = (bf16[1,1024,1536]{2,1,0:T(8,128)(2,1)}, bf16[1,1024,1536]{2,1,0:T(8,128)(2,1)}, u32[]{:S(2)}, u32[]{:S(2)}) collective-permute-start(bf16[1,1024,1536]{2,1,0:T(8,128)(2,1)} %get-tuple-element.89), channel_id=1, source_target_pairs={{0,4},{4,0},{1,5},{5,1},{2,6},{6,2},{3,7},{7,3}} | collective-permute-start | bytes 9437192 | tf_op jit(solution)/shard_map/ppermute | solution.py:444
  774.8 470.5 %collective-permute-start.11 = (f32[2,1536]{1,0:T(2,128)S(1)}, f32[2,1536]{1,0:T(2,128)S(1)}, u32[]{:S(2)}, u32[]{:S(2)}) collective-permute-start(f32[2,1536]{1,0:T(2,128)S(1)} %add_reduce_fusion), channel_id=1, source_target_pairs={{0,4},{4,0},{1,5},{5,1},{2,6},{6,2},{3,7},{7,3}} | collective-permute-start | bytes 36872 | tf_op jit(solution)/shard_map/ppermute | solution.py:497
  1245.4 8.2 copy-start.5
  1245.4 8.4 collective-permute-start.12
  1253.8 3.7 collective-permute-start.13
  1257.5 76.9 %collective-permute-start.10 = (bf16[1,1024,1536]{2,1,0:T(8,128)(2,1)}, bf16[1,1024,1536]{2,1,0:T(8,128)(2,1)}, u32[]{:S(2)}, u32[]{:S(2)}) collective-permute-start(bf16[1,1024,1536]{2,1,0:T(8,128)(2,1)} %get-tuple-element.100), channel_id=1, source_target_pairs={{0,4},{4,0},{1,5},{5,1},{2,6},{6,2},{3,7},{7,3}} | collective-permute-start | bytes 9437192 | tf_op jit(solution)/shard_map/ppermute | solution.py:444
Sparse Core Ops, SparseCore 0:
  674.4 73.5 reduce-scatter.3
  770.7 43.3 reduce-scatter.5
  817.2 42.4 reduce-scatter.7

commit v7 on v6

--- a/solution.py
+++ b/solution.py
@@ -19,7 +19,8 @@
 TN = (((0,), (0,)), ((), ()))
 PROJ_ROWS = 1024
 ROWS = 256
-LOAD_PIECES = 2
+ROWS_LIMIT = 38_000_000
+HOLD_LIMIT = 36_000_000
 SUM_ROWS = 1024
 OWN_CHUNKS = ((4,), (6,), (10,), (8, 4))
 EARLY_V = 12
@@ -200,6 +201,30 @@
     )(near, far, tau_rows)
 
 
+def hold_body(*refs, planes):
+    n = len(planes)
+    srcs = [ref if e is None else ref.at[e] for ref, e in zip(refs[:n], planes)]
+    copies = [pltpu.make_async_copy(srcs[k], refs[n + k], refs[-1].at[k]) for k in range(n)]
+    for c in copies:
+        c.start()
+    for c in copies:
+        c.wait()
+
+
+def hold(*arrays):
+    parts = [(t, e) for t in arrays for e in (range(t.shape[0]) if t.ndim == 3 else (None,))]
+    return pl.pallas_call(
+        functools.partial(hold_body, planes=[e for _, e in parts]),
+        in_specs=[pl.BlockSpec(memory_space=pltpu.HBM)] * len(parts),
+        out_specs=[pl.BlockSpec(memory_space=pltpu.VMEM)] * len(parts),
+        out_shape=[sds(t.shape[-2:], t.dtype) for t, _ in parts],
+        scratch_shapes=[pltpu.SemaphoreType.DMA((len(parts),))],
+        name="hold",
+        compiler_params=pltpu.CompilerParams(vmem_limit_bytes=HOLD_LIMIT),
+        cost_estimate=cost(10**9, 4 * 10**7),
+    )(*[t for t, _ in parts])
+
+
 def mix_block(q, k, v, do, attn_ref, dgram_ref, coef_ref, side, s):
     groups = attn_ref.shape[0] // 2
     am, gm = attn_ref[side * groups + s], dgram_ref[side * groups + s]
@@ -214,30 +239,19 @@
     nxt = lambda n: [next(it) for _ in range(n)]
     off_ref, x_ref, g_ref, u_ref, st_ref, q_ref, k_ref, v_ref, do_ref = nxt(9)
     attn_ref, dgram_ref, coef_ref, gm_ref = nxt(4)
-    w_hbm = nxt(4)
+    wn_ref, wf_ref = nxt(3), nxt(3)
+    won_ref, wof_ref = nxt(2)
     nxt(n_alias)
     y_ref, gx_ref, o_ref, rqk_ref, rv_ref = nxt(5)
     send_refs = nxt(len(send_blocks))
     (dsum_ref,) = nxt(1)
     on_s, rn_s, of_s, rf_s, qf_s, kf_s, vf_s, dof_s, gh_s = nxt(9)
-    w_refs, w_sems = nxt(4), nxt(1)[0]
-    wf_ref, wof_ref, wn_ref, won_ref = w_refs
     j = pl.program_id(0)
     own, other = off_ref[0], off_ref[1]
     groups = attn_ref.shape[0] // 2
     state = (attn_ref, dgram_ref, coef_ref)
-    waits = [pltpu.make_async_copy(src, dst, w_sems.at[n]) for n, (src, dst) in enumerate(zip(w_hbm, w_refs))]
-
-    def start_loads():
-        for n, (src, dst) in enumerate(zip(w_hbm, w_refs)):
-            pieces = [(e,) for e in range(src.shape[0])] if len(src.shape) == 3 else [()]
-            size = src.shape[-2] // LOAD_PIECES
-            for p in pieces:
-                for r in range(0, src.shape[-2], size):
-                    at = (*p, pl.ds(r, size))
-                    pltpu.make_async_copy(src.at[at], dst.at[at], w_sems.at[n]).start()
-
-    def compute(wait, first):
+
+    def compute(first):
         for s in range(groups):
             c = slice(s * GROUP, (s + 1) * GROUP)
             for half in (own, other):
@@ -245,18 +259,14 @@
                 o_ref[half, :, c], rqk_ref[0, half, :, c], rqk_ref[1, half, :, c], rv_ref[half, :, c] = o, dq, dk, dv
                 if half is own:
                     on_s[:, c], rn_s[0, :, c], rn_s[1, :, c], rn_s[2, :, c] = o, dq, dk, dv
-        wait(0)
-        wait(1)
         u = u_ref[0]
         for e, t in enumerate((qf_s, kf_s, vf_s)):
-            t[...] = dot(u, wf_ref[e]).astype(BF16)
+            t[...] = dot(u, wf_ref[e][...]).astype(BF16)
         dof_s[...] = dot(g_ref[0], wof_ref[...], NT).astype(BF16)
         for s in range(groups):
             c = slice(s * GROUP, (s + 1) * GROUP)
             of_s[:, c], rf_s[0, :, c], rf_s[1, :, c], rf_s[2, :, c] = mix_block(
                 qf_s[:, c], kf_s[:, c], vf_s[:, c], dof_s[:, c], *state, 1, s)
-        wait(2)
-        wait(3)
         rows, width = gh_s.shape
         mean, inv = st_ref[0, :, :1], st_ref[0, :, LANES // 2:LANES // 2 + 1]
         fold = lambda t: jnp.sum(t.reshape(rows // 8, 8, GROUP), axis=0)
@@ -265,14 +275,14 @@
         tiles = [slice(n, n + GROUP) for n in range(0, width, GROUP)]
         s1 = s2 = 0.0
         for c in tiles:
-            du = dot(rn_s[0], wn_ref[0, c, :], NT)
+            du = dot(rn_s[0], wn_ref[0][c, :], NT)
             for e in range(1, 3):
-                du += dot(rn_s[e], wn_ref[e, c, :], NT)
+                du += dot(rn_s[e], wn_ref[e][c, :], NT)
             for e in range(3):
-                du += dot(rf_s[e], wf_ref[e, c, :], NT)
+                du += dot(rf_s[e], wf_ref[e][c, :], NT)
             xh = (x_ref[0, :, c].astype(F32) - mean) * inv
             for a, val in enumerate((fold(du * xh), fold(du))):
-                dsum_ref[a, :, c] = val if first else dsum_ref[a, :, c] + val
+                dsum_ref[a, :, c] = jnp.where(first, val, dsum_ref[a, :, c] + val)
             gh = du * gamma[:, c]
             s1 += lanes(gh)
             s2 += lanes(gh * xh)
@@ -287,14 +297,7 @@
             for ref in [gx_ref] + send_refs[:1] * (len(send_refs) == 1):
                 ref[0, :, c] = dx.astype(BF16)
 
-    @pl.when(j == 0)
-    def _():
-        start_loads()
-        compute(lambda n: waits[n].wait(), True)
-
-    @pl.when(j > 0)
-    def _():
-        compute(lambda n: None, False)
+    compute(j == 0)
 
     if len(send_refs) > 1:
         start = 0
@@ -312,30 +315,29 @@
     blocks = sum(send_blocks)
     firsts = [sum(send_blocks[:n]) for n in range(len(send_blocks))]
     send_spec = lambda first, n: pl.BlockSpec((1, ROWS, width), lambda j, off: (0, jnp.clip(j - first, 0, n - 1), 0))
-    cols = weights[2].shape[0]
+    cols = acts[4].shape[2]
     row = half_spec(ROWS, width, 0, start)
     both = lambda *lead: both_spec(lead, ROWS, cols, start)
-    w_near, w_far, wo_near, wo_far, gamma = weights
+    *loaded, gamma = weights
     consts = list(state) + [gamma]
-    loaded = [w_far, wo_far, w_near, wo_near]
     first = 1 + len(acts) + len(consts) + len(loaded)
     return pl.pallas_call(
         functools.partial(rows_body, n_alias=len(prev), send_blocks=send_blocks),
         grid_spec=pltpu.PrefetchScalarGridSpec(
             num_scalar_prefetch=1,
             grid=(blocks,),
-            in_specs=[row] * 3 + [half_spec(ROWS, LANES, 0, start)] + [both()] * 4 + [whole(t.shape) for t in consts] + [pl.BlockSpec(memory_space=pl.ANY)] * (len(loaded) + len(prev)),
+            in_specs=[row] * 3 + [half_spec(ROWS, LANES, 0, start)] + [both()] * 4 + [whole(t.shape) for t in consts] + [pl.BlockSpec(memory_space=pltpu.VMEM)] * len(loaded) + [pl.BlockSpec(memory_space=pl.ANY)] * len(prev),
             out_specs=[row, row, both(), both(2), both(),
                        *[send_spec(first, n) for first, n in zip(firsts, send_blocks)],
                        pl.BlockSpec((2, 8, width), lambda j, off: (0, 0, 0))],
             scratch_shapes=[pltpu.VMEM((ROWS, cols), BF16), pltpu.VMEM((3, ROWS, cols), BF16)] * 2 + [pltpu.VMEM((ROWS, cols), BF16)] * 4
-            + [pltpu.VMEM((ROWS, width), F32)] + [pltpu.VMEM(t.shape, t.dtype) for t in loaded] + [pltpu.SemaphoreType.DMA((len(loaded),))],
+            + [pltpu.VMEM((ROWS, width), F32)],
         ),
         out_shape=[sds((2, half, width), BF16)] * 2 + [sds((2, half, cols), BF16), sds((2, 2, half, cols), BF16), sds((2, half, cols), BF16),
                                                        *[sds((1, n * ROWS, width), BF16) for n in send_blocks], sds((2, 8, width), F32)],
         input_output_aliases={first + a: a for a in range(len(prev))},
         name="rows",
-        compiler_params=params(),
+        compiler_params=pltpu.CompilerParams(vmem_limit_bytes=ROWS_LIMIT),
         cost_estimate=cost(2 * blocks * ROWS * width * cols * 13, 2 * blocks * ROWS * (6 * width + 16 * cols)),
     )(off, *acts, *consts, *loaded, *prev)
 
@@ -469,8 +471,11 @@
         state = (attn, dgram, coef)
 
         prev, dsum, recv, start = (), None, [], 0
+        attn, wn_, wf_ = lax.optimization_barrier((attn, w_near, w_far))
+        state = (attn, dgram, coef)
+        held = (*hold(wn_, wf_), w_out, wo_far)
         for sizes in OWN_CHUNKS:
-            out = rows_call(off, start, sizes, (x2, g2, u2, stats2) + near, state, (w_near, w_far, w_out, wo_far, ln_gamma), prev)
+            out = rows_call(off, start, sizes, (x2, g2, u2, stats2) + near, state, (*held, ln_gamma), prev)
             prev, sent, ds = out[:5], out[5:-1], out[-1]
             recv += [exchange(t) for t in sent]
             dsum = ds if dsum is None else dsum + ds

time: 1350 us -> 1330 us (0.985)
  Pallas kernels: 826 us -> 806 us
    pallas_call x4, Pallas kernels: 349 us -> 324 us  [rows_call(): pl.pallas_call(functools.partial(rows_body, n_alias=len(prev), send_block...]
  transfers between devices with their start and end apart: 17 -> 17, of which waited for: 5 -> 5; matrix products, arithmetic and copies ran while one was open for 1% -> 1% of each run, Pallas kernels for 29% -> 30%
where the time goes in v7:
time: 1330 us
  Pallas kernels  806 us (61%)
  waiting for transfers between devices  478 us (36%)
  starting transfers between devices  16.4 us (1%)
  between operations  14.5 us (1%)
    ppermute x3, waiting for transfers between devices, step(): sums = sums + lax.ppermute(sums, axis, perm)  461 us
    pallas_call x4, Pallas kernels, rows_call(): pl.pallas_call(functools.partial(rows_body, n_alias=len(prev), send_block...  324 us
    pallas_call x1, Pallas kernels, project(): pl.pallas_call(project_body, grid=(tokens // PROJ_ROWS,), in_specs=[row(w...  198 us
    pallas_call x3, Pallas kernels, token_sum(): pl.pallas_call(token_sum_body, grid=(tokens // SUM_ROWS,), in_specs=[row_...  185 us
    pallas_call x1, Pallas kernels, far_y(): pl.pallas_call(functools.partial(far_y_body, early=early, copies=copies),...  72.1 us
  transfers between devices with their start and end apart: 17, of which 5 were waited for; matrix products, arithmetic and copies ran while one was open for 1% of the time, Pallas kernels for 30%

profile of v7, /device:TPU:0, one launch (start us, length us, event | category | flops | bytes accessed | tf_op | source)
XLA Modules:
  0.0 1326.7 jit_solution(4198278026098965243)
XLA Ops:
  7.2 0.0 reduce-scatter.4.cloned.1.call-start
  7.2 3.4 collective-permute-start.4
  10.6 0.0 collective-permute-start.5
  10.6 198.0 %project.1 = (bf16[16384,1536]{1,0:T(8,128)(2,1)}, bf16[16384,768]{1,0:T(8,128)(2,1)}, bf16[16384,768]{1,0:T(8,128)(2,1)}, bf16[16384,768]{1,0:T(8,128)(2,1)}, b...) custom-call(bf16[16384,1536]{1,0:T(8,128)(2,1)} %x_ref.1, bf16[16384,1536]{1,0:T(8,128)(2,1)} %g_ref.1, ...), custom_call_target="tpu_custom_call" | custom-call | flops 170080698368 | bytes 251658240 | tf_op jit(solution)/shard_map/project/pallas_call | solution.py:116
  208.6 0.0 collective-permute-start
  208.6 2.0 collective-permute-start.1
  210.6 0.1 collective-permute-start.2
  210.7 0.1 broadcast_in_dim.10
  210.8 0.1 broadcast_in_dim.11
  210.9 0.1 broadcast_in_dim.12
  211.0 0.3 rev.6
  211.3 0.0 collective-permute-done
  211.3 6.4 collective-permute-done.1
  217.7 4.7 collective-permute-done.2
  222.4 1.0 add_add_fusion.near_ref
  223.4 0.0 copy-start.6
  223.4 1.6 collective-permute-start.3
  225.0 0.6 reshape.72.tau_ref
  225.6 0.1 pad_add_fusion.refs_0_.off_ref
  225.7 5.7 collective-permute-done.3.far_ref
  231.5 0.7 copy-done.9
  232.1 4.7 head_state.1
  236.8 0.0 copy-start.2
  236.8 0.0 copy-start.3
  236.9 0.0 copy-start.4
  236.9 5.3 hold.1
  242.2 0.4 copy-done
  242.6 0.2 copy-done.1
  242.8 0.2 copy-done.2
  243.0 43.2 %rows.4 = (bf16[2,8192,1536]{2,1,0:T(8,128)(2,1)}, bf16[2,8192,1536]{2,1,0:T(8,128)(2,1)}, bf16[2,8192,768]{2,1,0:T(8,128)(2,1)}, bf16[2,2,8192,768]{3,2,1,0:T(8...) custom-call(s32[2]{0:T(128)S(1)} %pad_add_fusion.refs_0_.off_ref, ...), custom_call_target="tpu_custom_call" | custom-call | flops 31406948352 | bytes 44040192 | tf_op jit(solution)/shard_map/rows/pallas_call | solution.py:324
  286.2 62.2 %rows.5 = (bf16[2,8192,1536]{2,1,0:T(8,128)(2,1)}, bf16[2,8192,1536]{2,1,0:T(8,128)(2,1)}, bf16[2,8192,768]{2,1,0:T(8,128)(2,1)}, bf16[2,2,8192,768]{3,2,1,0:T(8...) custom-call(s32[2]{0:T(128)S(1)} %pad_add_fusion.refs_0_.off_ref, ...), custom_call_target="tpu_custom_call", output_to_operand_aliasing={{0}: (21, {}), {1}: (22, {}), {2}: (23, {}), {3}: (24, {}),... | custom-call | flops 47110422528 | bytes 66060288 | tf_op jit(solution)/shard_map/rows/pallas_call | solution.py:324
  348.4 99.2 %rows.6 = (bf16[2,8192,1536]{2,1,0:T(8,128)(2,1)}, bf16[2,8192,1536]{2,1,0:T(8,128)(2,1)}, bf16[2,8192,768]{2,1,0:T(8,128)(2,1)}, bf16[2,2,8192,768]{3,2,1,0:T(8...) custom-call(s32[2]{0:T(128)S(1)} %pad_add_fusion.refs_0_.off_ref, ...), custom_call_target="tpu_custom_call", output_to_operand_aliasing={{0}: (21, {}), {1}: (22, {}), {2}: (23, {}), {3}: (24, {}),... | custom-call | flops 78517370880 | bytes 110100480 | tf_op jit(solution)/shard_map/rows/pallas_call | solution.py:324
  447.7 119.0 %rows.7 = (bf16[2,8192,1536]{2,1,0:T(8,128)(2,1)}, bf16[2,8192,1536]{2,1,0:T(8,128)(2,1)}, bf16[2,8192,768]{2,1,0:T(8,128)(2,1)}, bf16[2,2,8192,768]{3,2,1,0:T(8...) custom-call(s32[2]{0:T(128)S(1)} %pad_add_fusion.refs_0_.off_ref, ...), custom_call_target="tpu_custom_call", output_to_operand_aliasing={{0}: (21, {}), {1}: (22, {}), {2}: (23, {}), {3}: (24, {}),... | custom-call | flops 94220845056 | bytes 132120576 | tf_op jit(solution)/shard_map/rows/pallas_call | solution.py:324
  566.7 89.1 %token_sum.3 = f32[2,1536,768]{2,1,0:T(8,128)} custom-call(bf16[16384,1536]{1,0:T(8,128)(2,1)} %get-tuple-element.67.l_ref, bf16[2,16384,768]{2,1,0:T(8,128)(2,1)} %bitcast.43), custom_call_target="tpu_custom_call" | custom-call | flops 77309411328 | bytes 100663296 | tf_op jit(solution)/shard_map/token_sum/pallas_call | solution.py:427
  655.8 0.0 reduce-scatter.4.cloned.1.call-update
  655.8 0.0 reduce-scatter.6.cloned.1.call-start
  655.9 48.3 %token_sum.4 = f32[1,768,1536]{2,1,0:T(8,128)} custom-call(bf16[16384,768]{1,0:T(8,128)(2,1)} %bitcast.60, bf16[1,16384,1536]{2,1,0:T(8,128)(2,1)} %bitcast.42), custom_call_target="tpu_custom_call" | custom-call | flops 38654705664 | bytes 75497472 | tf_op jit(solution)/shard_map/token_sum/pallas_call | solution.py:427
  704.2 47.9 %token_sum.5 = f32[1,1536,768]{2,1,0:T(8,128)} custom-call(bf16[16384,1536]{1,0:T(8,128)(2,1)} %get-tuple-element.67.l_ref, bf16[1,16384,768]{2,1,0:T(8,128)(2,1)} %bitcast.61), custom_call_target="tpu_custom_call" | custom-call | flops 38654705664 | bytes 75497472 | tf_op jit(solution)/shard_map/token_sum/pallas_call | solution.py:427
  752.1 0.0 reduce-scatter.6.cloned.1.call-update
  752.1 0.0 reduce-scatter.8.cloned.1.call-start
  752.2 1.7 collective-permute-start.8
  753.8 0.4 collective-permute-start.9
  754.2 1.6 collective-permute-start.7
  755.9 0.0 reduce-scatter.8.cloned.1.call-update
  755.9 0.4 collective-permute-start.6
  756.3 0.1 add_reduce_fusion
  756.3 1.7 collective-permute-start.11
  758.0 9.1 far_v.2.refs_0_
  767.1 459.8 %collective-permute-done.11 = f32[2,1536]{1,0:T(2,128)S(1)} collective-permute-done((f32[2,1536]{1,0:T(2,128)S(1)}, f32[2,1536]{1,0:T(2,128)S(1)}, u32[]{:S(2)}, u32[]{:S(2)}) %collective-permute-start.11) | collective-permute-done | bytes 12320 | tf_op jit(solution)/shard_map/ppermute | solution.py:502
  1226.9 0.0 copy-start.7
  1226.9 0.0 collective-permute-start.12
  1226.9 8.2 far_v.3.refs_4_
  1235.1 0.1 reshape.78
  1235.2 0.1 reduce_sum.19
  1235.3 1.7 collective-permute-start.13
  1237.1 0.6 reshape.79
  1237.7 1.4 collective-permute-done.13
  1239.1 1.7 collective-permute-start.10
  1240.8 0.6 slice_reduce_fusion
  1241.5 0.0 reduce-scatter.4.cloned.1.call-done.refs_9_
  1241.5 72.1 %far_y.1 = (bf16[2,8192,1536]{2,1,0:T(8,128)(2,1)}, bf16[2,8192,1536]{2,1,0:T(8,128)(2,1)}, f32[3,384,768]{2,1,0:T(8,128)}) custom-call(s32[2]{0:T(128)} %copy-done.5, bf16[2,8192,1536]{2,1,0:T(8,128)(2,1)} %bitcast.35, bf16[2,8192,768]{2,1,0:T(8,128)(2,1)} %get-tuple-element.105.refs_2_, ...), custom_call_target="tpu_custom_call", output_to_operand_aliasing={{0}: (14, {}), {1}: (15, {})} | custom-call | flops 54116589568 | bytes 138412032 | tf_op jit(solution)/shard_map/far_y/pallas_call | solution.py:400
  1313.6 0.0 reduce-scatter.6.cloned.1.call-done
  1313.6 2.4 constant_dynamic-update-slice_fusion
  1316.0 3.8 constant_dynamic-update-slice_fusion.1
  (28 shorter events, 0.1 us)
Async XLA Ops:
  7.2 1234.3 %reduce-scatter.4.cloned.1.call-start = ((), (), s32[]{:S(2)}) async-start(), calls=%async_computation.3 | async-start | bytes 11796480 | tf_op jit(solution)/shard_map/reduce_scatter | solution.py:490
  7.2 229.6 %collective-permute-start.4 = (bf16[3,1536,768]{2,1,0:T(8,128)(2,1)}, bf16[3,1536,768]{2,1,0:T(8,128)(2,1)}, u32[]{:S(2)}, u32[]{:S(2)}) collective-permute-start(bf16[3,1536,768]{2,1,0:T(8,128)(2,1)} %bitcast.66), channel_id=1, source_target_pairs={{0,4},{4,0},{1,5},{5,1},{2,6},{6,2},{3,7},{7,3}} | collective-permute-start | bytes 21233672 | tf_op jit(solution)/shard_map/ppermute | solution.py:446
  10.6 231.6 %collective-permute-start.5 = (bf16[768,1536]{1,0:T(8,128)(2,1)}, bf16[768,1536]{1,0:T(8,128)(2,1)}, u32[]{:S(2)}, u32[]{:S(2)}) collective-permute-start(bf16[768,1536]{1,0:T(8,128)(2,1)} %refs_6_.1), channel_id=1, source_target_pairs={{0,4},{4,0},{1,5},{5,1},{2,6},{6,2},{3,7},{7,3}} | collective-permute-start | bytes 7077896 | tf_op jit(solution)/shard_map/ppermute | solution.py:446
  10.6 200.1 %copy-start.8 = (f32[48]{0:T(128)S(1)}, f32[48]{0:T(128)}, u32[]{:S(2)}) copy-start(f32[48]{0:T(128)} %param.13) | copy-start | bytes 580
  208.6 2.7 collective-permute-start
  208.6 9.1 collective-permute-start.1
  210.6 11.8 collective-permute-start.2
  223.4 8.0 copy-start.6
  223.4 8.0 collective-permute-start.3
  225.7 222.0 %copy-start.5 = (s32[2]{0:T(128)}, s32[2]{0:T(128)S(1)}, u32[]{:S(2)}) copy-start(s32[2]{0:T(128)S(1)} %pad_add_fusion.refs_0_.off_ref) | copy-start | bytes 28
  231.4 0.7 copy-start.9
  236.8 5.8 copy-start
  236.8 5.9 copy-start.1
  236.8 6.2 copy-start.2
  236.8 6.2 copy-start.3
  236.9 6.2 copy-start.4
  655.8 657.7 %reduce-scatter.6.cloned.1.call-start = ((), (), s32[]{:S(2)}) async-start(), calls=%async_computation.4 | async-start | bytes 5898240 | tf_op jit(solution)/shard_map/reduce_scatter | solution.py:496
  752.1 567.6 %reduce-scatter.8.cloned.1.call-start = ((), (), s32[]{:S(2)}) async-start(), calls=%async_computation.5 | async-start | bytes 5898240 | tf_op jit(solution)/shard_map/reduce_scatter | solution.py:493
  752.2 489.3 %collective-permute-start.8 = (bf16[1,2560,1536]{2,1,0:T(8,128)(2,1)}, bf16[1,2560,1536]{2,1,0:T(8,128)(2,1)}, u32[]{:S(2)}, u32[]{:S(2)}) collective-permute-start(bf16[1,2560,1536]{2,1,0:T(8,128)(2,1)} %get-tuple-element.109), channel_id=1, source_target_pairs={{0,4},{4,0},{1,5},{5,1},{2,6},{6,2},{3,7},{7,3}} | collective-permute-start | bytes 23592968 | tf_op jit(solution)/shard_map/ppermute | solution.py:446
  753.8 487.6 %collective-permute-start.9 = (bf16[1,2048,1536]{2,1,0:T(8,128)(2,1)}, bf16[1,2048,1536]{2,1,0:T(8,128)(2,1)}, u32[]{:S(2)}, u32[]{:S(2)}) collective-permute-start(bf16[1,2048,1536]{2,1,0:T(8,128)(2,1)} %get-tuple-element.110), channel_id=1, source_target_pairs={{0,4},{4,0},{1,5},{5,1},{2,6},{6,2},{3,7},{7,3}} | collective-permute-start | bytes 18874376 | tf_op jit(solution)/shard_map/ppermute | solution.py:446
  754.2 487.2 %collective-permute-start.7 = (bf16[1,1536,1536]{2,1,0:T(8,128)(2,1)}, bf16[1,1536,1536]{2,1,0:T(8,128)(2,1)}, u32[]{:S(2)}, u32[]{:S(2)}) collective-permute-start(bf16[1,1536,1536]{2,1,0:T(8,128)(2,1)} %get-tuple-element.108), channel_id=1, source_target_pairs={{0,4},{4,0},{1,5},{5,1},{2,6},{6,2},{3,7},{7,3}} | collective-permute-start | bytes 14155784 | tf_op jit(solution)/shard_map/ppermute | solution.py:446
  755.9 485.6 %collective-permute-start.6 = (bf16[1,1024,1536]{2,1,0:T(8,128)(2,1)}, bf16[1,1024,1536]{2,1,0:T(8,128)(2,1)}, u32[]{:S(2)}, u32[]{:S(2)}) collective-permute-start(bf16[1,1024,1536]{2,1,0:T(8,128)(2,1)} %get-tuple-element.107), channel_id=1, source_target_pairs={{0,4},{4,0},{1,5},{5,1},{2,6},{6,2},{3,7},{7,3}} | collective-permute-start | bytes 9437192 | tf_op jit(solution)/shard_map/ppermute | solution.py:446
  756.3 470.5 %collective-permute-start.11 = (f32[2,1536]{1,0:T(2,128)S(1)}, f32[2,1536]{1,0:T(2,128)S(1)}, u32[]{:S(2)}, u32[]{:S(2)}) collective-permute-start(f32[2,1536]{1,0:T(2,128)S(1)} %add_reduce_fusion), channel_id=1, source_target_pairs={{0,4},{4,0},{1,5},{5,1},{2,6},{6,2},{3,7},{7,3}} | collective-permute-start | bytes 36872 | tf_op jit(solution)/shard_map/ppermute | solution.py:502
  1226.9 8.2 copy-start.7
  1226.9 8.4 collective-permute-start.12
  1235.3 3.7 collective-permute-start.13
  1239.1 76.9 %collective-permute-start.10 = (bf16[1,1024,1536]{2,1,0:T(8,128)(2,1)}, bf16[1,1024,1536]{2,1,0:T(8,128)(2,1)}, u32[]{:S(2)}, u32[]{:S(2)}) collective-permute-start(bf16[1,1024,1536]{2,1,0:T(8,128)(2,1)} %get-tuple-element.118), channel_id=1, source_target_pairs={{0,4},{4,0},{1,5},{5,1},{2,6},{6,2},{3,7},{7,3}} | collective-permute-start | bytes 9437192 | tf_op jit(solution)/shard_map/ppermute | solution.py:446
Sparse Core Ops, SparseCore 0:
  656.0 73.5 reduce-scatter.3
  752.2 43.4 reduce-scatter.5
  798.8 42.3 reduce-scatter.7

commit v8 on v7

--- a/solution.py
+++ b/solution.py
@@ -19,11 +19,12 @@
 TN = (((0,), (0,)), ((), ()))
 PROJ_ROWS = 1024
 ROWS = 256
+STATE_LIMIT = 16_000_000
 ROWS_LIMIT = 38_000_000
 HOLD_LIMIT = 36_000_000
 SUM_ROWS = 1024
 OWN_CHUNKS = ((4,), (6,), (10,), (8, 4))
-EARLY_V = 12
+EARLY_V = 6
 
 
 def dot(a, b, dims=NN):
@@ -197,6 +198,7 @@
         out_specs=[vm] * 4,
         out_shape=[sds((2 * groups, GROUP, GROUP), BF16)] * 2 + [sds((8, groups * GROUP), F32), sds((8, GROUP), F32)],
         name="head_state",
+        compiler_params=pltpu.CompilerParams(vmem_limit_bytes=STATE_LIMIT),
         cost_estimate=cost(10**9, 2 * 10**6),
     )(near, far, tau_rows)
 
@@ -345,7 +347,7 @@
 def far_y_body(*refs, early, copies):
     it = iter(refs)
     nxt = lambda n: [next(it) for _ in range(n)]
-    _, x_ref, o_ref, u_ref, v_ref, attn_ref, won_ref, wof_ref, wv_ref, qk_ref = nxt(10)
+    _, x_ref, o_ref, u_ref, v_ref, attn_ref, won_ref, wof_ref, wv_ref, pv_ref = nxt(10)
     recv = nxt(len(copies))
     _, _, y_ref, gx_ref, gw_ref, vf_s, of_s, sem = nxt(8)
     j = pl.program_id(0)
@@ -362,7 +364,7 @@
             start += n
 
     file_rows(lambda copy: copy.start())
-    gw_ref[...] = qk_ref[...]
+    gw_ref[...] = pv_ref[...]
 
     @pl.when(j < early)
     def _():
@@ -380,7 +382,7 @@
     file_rows(lambda copy: copy.wait())
 
 
-def far_y(off, x2, o2, u2, vf, attn, wo_near, wo_far, w_far, dw_qk, recv, y2, gx2):
+def far_y(off, x2, o2, u2, vf, attn, wo_near, wo_far, w_far, dw_v, recv, y2, gx2):
     half, width = x2.shape[1:]
     cols = o2.shape[2]
     rows = 2 * ROWS
@@ -388,25 +390,25 @@
     early = vf.shape[0] // rows
     copies = [t.shape[1] // rows for t in recv]
     row = lambda c: half_spec(rows, c, 1, 0)
-    per = steps // 2
-    plane = pl.BlockSpec((1, dw_qk.shape[1] // per, cols), lambda j, off: (j // per, j % per, 0))
+    part = (1, dw_v.shape[1] // steps, cols)
     any_ = pl.BlockSpec(memory_space=pl.ANY)
     specs = [row(width), row(cols),
              pl.BlockSpec((1, rows, width), lambda j, off: (off[1], jnp.maximum(j, early), 0)),
              pl.BlockSpec((rows, cols), lambda j, off: (jnp.minimum(j, early - 1), 0)),
              whole(attn.shape), whole(wo_near.shape), whole(wo_far.shape),
-             pl.BlockSpec((1, width, cols), lambda j, off: (2, 0, 0), pipeline_mode=pl.Buffered(1)), plane]
-    args = [x2, o2, u2, vf, attn, wo_near, wo_far, w_far, dw_qk, *recv]
+             pl.BlockSpec((1, width, cols), lambda j, off: (2, 0, 0), pipeline_mode=pl.Buffered(1)),
+             pl.BlockSpec(part, lambda j, off: (0, j, 0))]
+    args = [x2, o2, u2, vf, attn, wo_near, wo_far, w_far, dw_v, *recv]
     return pl.pallas_call(
         functools.partial(far_y_body, early=early, copies=copies),
         grid_spec=pltpu.PrefetchScalarGridSpec(
             num_scalar_prefetch=1,
             grid=(steps,),
             in_specs=specs + [any_] * (len(recv) + 2),
-            out_specs=[row(width), pl.BlockSpec((1, rows, width), lambda j, off: (off[1], jnp.minimum(j, sum(copies) - 1), 0)), plane],
+            out_specs=[row(width), pl.BlockSpec((1, rows, width), lambda j, off: (off[1], jnp.minimum(j, sum(copies) - 1), 0)), pl.BlockSpec(part, lambda j, off: (2, j, 0))],
             scratch_shapes=[pltpu.VMEM((rows, cols), BF16)] * 2 + [pltpu.SemaphoreType.DMA],
         ),
-        out_shape=[sds(y2.shape, y2.dtype), sds(gx2.shape, gx2.dtype), sds((3, *dw_qk.shape[1:]), F32)],
+        out_shape=[sds(y2.shape, y2.dtype), sds(gx2.shape, gx2.dtype), sds((3, *dw_v.shape[1:]), F32)],
         input_output_aliases={len(args) + 1: 0, len(args) + 2: 1},
         name="far_y",
         compiler_params=params(),
@@ -414,26 +416,33 @@
     )(off, *args, y2, gx2)
 
 
-def token_sum_body(l_ref, r_ref, o_ref):
+def token_sum_body(*refs, planes):
+    n = len(planes)
     first = pl.program_id(0) == 0
-    for e in range(r_ref.shape[0]):
-        val = dot(l_ref[...], r_ref[e], TN)
-        o_ref[e] = jnp.where(first, val, o_ref[e] + val)
-
-
-def token_sum(lhs, rhs):
-    planes, tokens, cols = rhs.shape
-    width = lhs.shape[1]
-    return pl.pallas_call(
-        token_sum_body,
+    out = 2 * n
+    for l_ref, r_ref, count in zip(refs[:n], refs[n:out], planes):
+        o_ref, out = refs[out], out + 1
+        for e in range(count):
+            val = dot(l_ref[...], r_ref[e], TN)
+            o_ref[e] = jnp.where(first, val, o_ref[e] + val)
+
+
+def token_sum(*pairs):
+    tokens = pairs[0][0].shape[0]
+    flops = sum(2 * r.shape[0] * tokens * l.shape[1] * r.shape[2] for l, r in pairs)
+    nbytes = sum(2 * tokens * (l.shape[1] + r.shape[0] * r.shape[2]) for l, r in pairs)
+    shapes = [(r.shape[0], l.shape[1], r.shape[2]) for l, r in pairs]
+    return pl.pallas_call(
+        functools.partial(token_sum_body, planes=[r.shape[0] for _, r in pairs]),
         grid=(tokens // SUM_ROWS,),
-        in_specs=[row_spec(SUM_ROWS, width, lambda i: i), pl.BlockSpec((planes, SUM_ROWS, cols), lambda i: (0, i, 0))],
-        out_specs=pl.BlockSpec((planes, width, cols), lambda i: (0, 0, 0)),
-        out_shape=sds((planes, width, cols), F32),
+        in_specs=[row_spec(SUM_ROWS, l.shape[1], lambda i: i) for l, _ in pairs]
+        + [pl.BlockSpec((r.shape[0], SUM_ROWS, r.shape[2]), lambda i: (0, i, 0)) for _, r in pairs],
+        out_specs=[pl.BlockSpec(s, lambda i: (0, 0, 0)) for s in shapes],
+        out_shape=[sds(s, F32) for s in shapes],
         name="token_sum",
         compiler_params=params(),
-        cost_estimate=cost(2 * planes * tokens * width * cols, 2 * tokens * (width + planes * cols)),
-    )(lhs, rhs)
+        cost_estimate=cost(flops, nbytes),
+    )(*[l for l, _ in pairs], *[r for _, r in pairs])
 
 
 def solution(mesh):
@@ -462,18 +471,16 @@
         near = tuple(halves(t) for t in (q, k, v, do))
         peers = [lax.ppermute(part, "sp", [(s, s ^ d) for s in range(sp_size)]) for d in (1, 2, 3)]
         part = (part + peers[0]) + (peers[1] + peers[2])
+        part, wn_, wf_ = lax.optimization_barrier((part, w_near, w_far))
         part_far = exchange(part)
-        vf = far_v(off, u2, w_far, EARLY_V, 0, 2)
-        vf = far_v(off, u2, w_far, EARLY_V, 1, 2, (vf,))
+        held = (*hold(wn_, wf_), w_out, wo_far)
+        vf = far_v(off, u2, w_far, EARLY_V, 0, 1)
         tau = jnp.repeat(temps, HEAD).reshape(tp_size, groups, GROUP)
         tau = jnp.where(me == 0, tau, tau[::-1]).reshape(2 * groups, GROUP)
         attn, dgram, coef, dtau = head_state(part, part_far, tau)
         state = (attn, dgram, coef)
 
         prev, dsum, recv, start = (), None, [], 0
-        attn, wn_, wf_ = lax.optimization_barrier((attn, w_near, w_far))
-        state = (attn, dgram, coef)
-        held = (*hold(wn_, wf_), w_out, wo_far)
         for sizes in OWN_CHUNKS:
             out = rows_call(off, start, sizes, (x2, g2, u2, stats2) + near, state, (*held, ln_gamma), prev)
             prev, sent, ds = out[:5], out[5:-1], out[-1]
@@ -485,17 +492,15 @@
         dtau = jnp.sum(dtau[:2 * groups].reshape(tp_size, cols // HEAD, HEAD), axis=2)
         grad_temp = jnp.where(me == 0, dtau, dtau[::-1]).reshape(-1)
 
-        dw_qk = token_sum(u, rqk.reshape(2, tokens, cols))
-        o2, dw_qk = lax.optimization_barrier((o2, dw_qk))
+        dw_o, dw_v = token_sum((o2.reshape(tokens, cols), g[None]), (u, rv.reshape(1, tokens, cols)))
+        rqk, dw_o, dw_v = lax.optimization_barrier((rqk, dw_o, dw_v))
+        grad_wout = lax.psum_scatter(dw_o[0], "sp", scatter_dimension=0, tiled=True)
+        dw_v = lax.psum_scatter(dw_v, "sp", scatter_dimension=1, tiled=True)
+        (dw_qk,) = token_sum((u, rqk.reshape(2, tokens, cols)))
+        y2, dw_qk = lax.optimization_barrier((y2, dw_qk))
         dw_qk = lax.psum_scatter(dw_qk, "sp", scatter_dimension=1, tiled=True)
-        dw_o = token_sum(o2.reshape(tokens, cols), g[None])[0]
-        rv, dw_o = lax.optimization_barrier((rv, dw_o))
-        grad_wout = lax.psum_scatter(dw_o, "sp", scatter_dimension=0, tiled=True)
-        dw_v = token_sum(u, rv.reshape(1, tokens, cols))
-        y2, dw_v = lax.optimization_barrier((y2, dw_v))
-        dw_v = lax.psum_scatter(dw_v, "sp", scatter_dimension=1, tiled=True)
-        y2, gx2, gw = far_y(off, x2, o2, u2, vf, attn, w_out, wo_far, w_far, dw_qk, recv[:-1], y2, gx2)
-        grad_wqkv = jnp.transpose(lax.dynamic_update_slice(gw, dw_v, (2, 0, 0)), (1, 0, 2))
+        y2, gx2, gw = far_y(off, x2, o2, u2, vf, attn, w_out, wo_far, w_far, dw_v, recv[:-1], y2, gx2)
+        grad_wqkv = jnp.transpose(lax.dynamic_update_slice(gw, dw_qk, (0, 0, 0)), (1, 0, 2))
 
         sums = jnp.sum(dsum, axis=1)
         for axis, perm in (("tp", swap), ("sp", [(s, s ^ 1) for s in range(sp_size)]), ("sp", [(s, s ^ 2) for s in range(sp_size)])):

time: 1330 us -> 1320 us (level)
  Pallas kernels: 806 us -> 789 us
    pallas_call x3 -> x2, Pallas kernels: 185 us -> 177 us  [token_sum(): pl.pallas_call(functools.partial(token_sum_body, planes=[r.shape[0] for _...]
  transfers between devices with their start and end apart: 17 -> 17, of which waited for: 5 -> 5; matrix products, arithmetic and copies ran while one was open for 1% -> 1% of each run, Pallas kernels for 30% -> 29%
where the time goes in v8:
time: 1320 us; the launch traced here: 1310 us
  Pallas kernels  789 us (60%)
  waiting for transfers between devices  482 us (37%)
  starting transfers between devices  16.5 us (1%)
  between operations  14.4 us (1%)
    ppermute x3, waiting for transfers between devices, step(): sums = sums + lax.ppermute(sums, axis, perm)  470 us
    pallas_call x4, Pallas kernels, rows_call(): pl.pallas_call(functools.partial(rows_body, n_alias=len(prev), send_block...  324 us
    pallas_call x1, Pallas kernels, project(): pl.pallas_call(project_body, grid=(tokens // PROJ_ROWS,), in_specs=[row(w...  198 us
    pallas_call x2, Pallas kernels, token_sum(): pl.pallas_call(functools.partial(token_sum_body, planes=[r.shape[0] for _...  177 us
    pallas_call x1, Pallas kernels, far_y(): pl.pallas_call(functools.partial(far_y_body, early=early, copies=copies),...  74 us
  transfers between devices with their start and end apart: 17, of which 5 were waited for; matrix products, arithmetic and copies ran while one was open for 1% of the time, Pallas kernels for 29%

profile of v8, /device:TPU:0, one launch (start us, length us, event | category | flops | bytes accessed | tf_op | source)
XLA Modules:
  0.0 1312.4 jit_solution(13605965229997353710)
XLA Ops:
  7.2 0.0 reduce-scatter.4.cloned.1.call-start
  7.2 3.4 collective-permute-start.3
  10.6 0.0 collective-permute-start.5
  10.6 198.0 %project.1 = (bf16[16384,1536]{1,0:T(8,128)(2,1)}, bf16[16384,768]{1,0:T(8,128)(2,1)}, bf16[16384,768]{1,0:T(8,128)(2,1)}, bf16[16384,768]{1,0:T(8,128)(2,1)}, b...) custom-call(bf16[16384,1536]{1,0:T(8,128)(2,1)} %x_ref.1, bf16[16384,1536]{1,0:T(8,128)(2,1)} %g_ref.1, ...), custom_call_target="tpu_custom_call" | custom-call | flops 170080698368 | bytes 251658240 | tf_op jit(solution)/shard_map/project/pallas_call | solution.py:117
  208.6 0.0 collective-permute-start
  208.6 2.0 collective-permute-start.1
  210.6 0.1 collective-permute-start.2
  210.7 0.0 copy-done.4
  210.7 0.1 broadcast_in_dim.10
  210.8 0.1 broadcast_in_dim.11
  210.9 0.1 broadcast_in_dim.12
  211.0 0.3 rev.6
  211.3 0.0 collective-permute-done
  211.3 6.4 collective-permute-done.1
  217.7 4.7 collective-permute-done.2
  222.4 1.0 add_add_fusion.near_ref
  223.4 0.0 collective-permute-done.3.refs_3_.refs_4_.refs_5_.w_ref.refs_8_
  223.4 1.6 collective-permute-start.4
  225.0 0.1 pad_add_fusion.refs_0_.off_ref
  225.1 5.3 hold.1
  230.4 1.0 collective-permute-done.4.far_ref
  231.4 2.7 head_state.1
  234.1 0.0 copy-start.1
  234.2 0.0 collective-permute-done.5.refs_20_.refs_7_
  234.2 0.0 copy-done
  234.2 0.0 copy-done.2
  234.2 43.2 %rows.4 = (bf16[2,8192,1536]{2,1,0:T(8,128)(2,1)}, bf16[2,8192,1536]{2,1,0:T(8,128)(2,1)}, bf16[2,8192,768]{2,1,0:T(8,128)(2,1)}, bf16[2,2,8192,768]{3,2,1,0:T(8...) custom-call(s32[2]{0:T(128)S(1)} %pad_add_fusion.refs_0_.off_ref, ...), custom_call_target="tpu_custom_call" | custom-call | flops 31406948352 | bytes 44040192 | tf_op jit(solution)/shard_map/rows/pallas_call | solution.py:326
  277.4 62.3 %rows.5 = (bf16[2,8192,1536]{2,1,0:T(8,128)(2,1)}, bf16[2,8192,1536]{2,1,0:T(8,128)(2,1)}, bf16[2,8192,768]{2,1,0:T(8,128)(2,1)}, bf16[2,2,8192,768]{3,2,1,0:T(8...) custom-call(s32[2]{0:T(128)S(1)} %pad_add_fusion.refs_0_.off_ref, ...), custom_call_target="tpu_custom_call", output_to_operand_aliasing={{0}: (21, {}), {1}: (22, {}), {2}: (23, {}), {3}: (24, {}),... | custom-call | flops 47110422528 | bytes 66060288 | tf_op jit(solution)/shard_map/rows/pallas_call | solution.py:326
  339.7 99.4 %rows.6 = (bf16[2,8192,1536]{2,1,0:T(8,128)(2,1)}, bf16[2,8192,1536]{2,1,0:T(8,128)(2,1)}, bf16[2,8192,768]{2,1,0:T(8,128)(2,1)}, bf16[2,2,8192,768]{3,2,1,0:T(8...) custom-call(s32[2]{0:T(128)S(1)} %pad_add_fusion.refs_0_.off_ref, ...), custom_call_target="tpu_custom_call", output_to_operand_aliasing={{0}: (21, {}), {1}: (22, {}), {2}: (23, {}), {3}: (24, {}),... | custom-call | flops 78517370880 | bytes 110100480 | tf_op jit(solution)/shard_map/rows/pallas_call | solution.py:326
  439.0 0.0 copy-done.3
  439.1 119.0 %rows.7 = (bf16[2,8192,1536]{2,1,0:T(8,128)(2,1)}, bf16[2,8192,1536]{2,1,0:T(8,128)(2,1)}, bf16[2,8192,768]{2,1,0:T(8,128)(2,1)}, bf16[2,2,8192,768]{3,2,1,0:T(8...) custom-call(s32[2]{0:T(128)S(1)} %pad_add_fusion.refs_0_.off_ref, ...), custom_call_target="tpu_custom_call", output_to_operand_aliasing={{0}: (21, {}), {1}: (22, {}), {2}: (23, {}), {3}: (24, {}),... | custom-call | flops 94220845056 | bytes 132120576 | tf_op jit(solution)/shard_map/rows/pallas_call | solution.py:326
  558.1 88.0 %token_sum.2 = (f32[1,768,1536]{2,1,0:T(8,128)}, f32[1,1536,768]{2,1,0:T(8,128)}) custom-call(bf16[16384,768]{1,0:T(8,128)(2,1)} %bitcast.60, bf16[16384,1536]{1,0:T(8,128)(2,1)} %get-tuple-element.68.refs_1_.refs_0_, bf16[1,16384,1536]{2,1,0:T(8,128)(2,1)} %bitcast.42, bf16[1,16384,768]{2,1,0:T(8,128)(2,1)} %bitcast.61), custom_call_target="tpu_custom_call" | custom-call | flops 77309411328 | bytes 150994944 | tf_op jit(solution)/shard_map/token_sum/pallas_call | solution.py:435
  646.1 0.0 reduce-scatter.4.cloned.1.call-update
  646.1 0.0 reduce-scatter.6.cloned.1.call-start
  646.1 89.1 %token_sum.3 = f32[2,1536,768]{2,1,0:T(8,128)} custom-call(bf16[16384,1536]{1,0:T(8,128)(2,1)} %get-tuple-element.68.refs_1_.refs_0_, bf16[2,16384,768]{2,1,0:T(8,128)(2,1)} %bitcast.43), custom_call_target="tpu_custom_call" | custom-call | flops 77309411328 | bytes 100663296 | tf_op jit(solution)/shard_map/token_sum/pallas_call | solution.py:435
  735.3 0.0 reduce-scatter.6.cloned.1.call-update
  735.3 0.0 reduce-scatter.8.cloned.1.call-start
  735.3 1.8 collective-permute-start.8
  737.1 0.3 collective-permute-start.9
  737.4 1.7 collective-permute-start.7
  739.1 0.0 reduce-scatter.8.cloned.1.call-update
  739.2 0.3 collective-permute-start.6
  739.5 0.1 add_reduce_fusion
  739.5 1.8 collective-permute-start.11
  741.3 468.5 %collective-permute-done.11 = f32[2,1536]{1,0:T(2,128)S(1)} collective-permute-done((f32[2,1536]{1,0:T(2,128)S(1)}, f32[2,1536]{1,0:T(2,128)S(1)}, u32[]{:S(2)}, u32[]{:S(2)}) %collective-permute-start.11) | collective-permute-done | bytes 12320 | tf_op jit(solution)/shard_map/ppermute | solution.py:507
  1209.8 0.0 collective-permute-start.12
  1209.8 8.2 far_v.1.refs_4_
  1218.0 0.1 reshape.78
  1218.1 0.1 reduce_sum.19
  1218.2 0.0 collective-permute-done.12
  1218.3 1.7 collective-permute-start.13
  1220.0 0.6 reshape.79
  1220.6 1.4 collective-permute-done.13
  1222.0 1.7 collective-permute-start.10
  1223.7 0.6 slice_reduce_fusion
  1224.4 0.0 collective-permute-done.6.refs_10_
  1224.4 0.0 collective-permute-done.7.refs_11_
  1224.4 0.0 collective-permute-done.9.refs_13_
  1224.4 0.0 collective-permute-done.8.refs_12_
  1224.4 0.0 reduce-scatter.4.cloned.1.call-done.refs_9_
  1224.4 74.0 %far_y.1 = (bf16[2,8192,1536]{2,1,0:T(8,128)(2,1)}, bf16[2,8192,1536]{2,1,0:T(8,128)(2,1)}, f32[3,384,768]{2,1,0:T(8,128)}) custom-call(s32[2]{0:T(128)} %copy-done.3, bf16[2,8192,1536]{2,1,0:T(8,128)(2,1)} %bitcast.35, bf16[2,8192,768]{2,1,0:T(8,128)(2,1)} %get-tuple-element.102.refs_2_, ...), custom_call_target="tpu_custom_call", output_to_operand_aliasing={{0}: (14, {}), {1}: (15, {})} | custom-call | flops 54116589568 | bytes 138412032 | tf_op jit(solution)/shard_map/far_y/pallas_call | solution.py:402
  1298.4 0.0 collective-permute-done.10
  1298.5 3.8 constant_dynamic-update-slice_fusion
  1302.2 3.2 constant_dynamic-update-slice_fusion.1
  (16 shorter events, 0.1 us)
Async XLA Ops:
  7.2 1217.2 %reduce-scatter.4.cloned.1.call-start = ((), (), s32[]{:S(2)}) async-start(), calls=%async_computation.3 | async-start | bytes 5898240 | tf_op jit(solution)/shard_map/reduce_scatter | solution.py:498
  7.2 216.2 %collective-permute-start.3 = (bf16[3,1536,768]{2,1,0:T(8,128)(2,1)}, bf16[3,1536,768]{2,1,0:T(8,128)(2,1)}, u32[]{:S(2)}, u32[]{:S(2)}) collective-permute-start(bf16[3,1536,768]{2,1,0:T(8,128)(2,1)} %bitcast.66), channel_id=1, source_target_pairs={{0,4},{4,0},{1,5},{5,1},{2,6},{6,2},{3,7},{7,3}} | collective-permute-start | bytes 21233672 | tf_op jit(solution)/shard_map/ppermute | solution.py:455
  10.6 223.6 %collective-permute-start.5 = (bf16[768,1536]{1,0:T(8,128)(2,1)}, bf16[768,1536]{1,0:T(8,128)(2,1)}, u32[]{:S(2)}, u32[]{:S(2)}) collective-permute-start(bf16[768,1536]{1,0:T(8,128)(2,1)} %refs_6_.1), channel_id=1, source_target_pairs={{0,4},{4,0},{1,5},{5,1},{2,6},{6,2},{3,7},{7,3}} | collective-permute-start | bytes 7077896 | tf_op jit(solution)/shard_map/ppermute | solution.py:455
  10.6 200.1 %copy-start.4 = (f32[48]{0:T(128)S(1)}, f32[48]{0:T(128)}, u32[]{:S(2)}) copy-start(f32[48]{0:T(128)} %param.13) | copy-start | bytes 580
  208.6 2.7 collective-permute-start
  208.6 9.1 collective-permute-start.1
  210.6 11.8 collective-permute-start.2
  223.4 8.0 collective-permute-start.4
  225.1 213.9 %copy-start.3 = (s32[2]{0:T(128)}, s32[2]{0:T(128)S(1)}, u32[]{:S(2)}) copy-start(s32[2]{0:T(128)S(1)} %pad_add_fusion.refs_0_.off_ref) | copy-start | bytes 28
  225.1 9.0 copy-start
  225.1 9.1 copy-start.2
  234.1 204.9 %copy-start.1 = (bf16[6,256,256]{2,1,0:T(8,128)(2,1)}, bf16[6,256,256]{2,1,0:T(8,128)(2,1)S(1)}, u32[]{:S(2)}) copy-start(bf16[6,256,256]{2,1,0:T(8,128)(2,1)S(1)} %get-tuple-element.76.refs_9_.refs_5_) | copy-start | bytes 2359300
  646.1 656.1 %reduce-scatter.6.cloned.1.call-start = ((), (), s32[]{:S(2)}) async-start(), calls=%async_computation.4 | async-start | bytes 11796480 | tf_op jit(solution)/shard_map/reduce_scatter | solution.py:501
  735.3 570.1 %reduce-scatter.8.cloned.1.call-start = ((), (), s32[]{:S(2)}) async-start(), calls=%async_computation.5 | async-start | bytes 5898240 | tf_op jit(solution)/shard_map/reduce_scatter | solution.py:497
  735.3 489.0 %collective-permute-start.8 = (bf16[1,2560,1536]{2,1,0:T(8,128)(2,1)}, bf16[1,2560,1536]{2,1,0:T(8,128)(2,1)}, u32[]{:S(2)}, u32[]{:S(2)}) collective-permute-start(bf16[1,2560,1536]{2,1,0:T(8,128)(2,1)} %get-tuple-element.112), channel_id=1, source_target_pairs={{0,4},{4,0},{1,5},{5,1},{2,6},{6,2},{3,7},{7,3}} | collective-permute-start | bytes 23592968 | tf_op jit(solution)/shard_map/ppermute | solution.py:455
  737.1 487.3 %collective-permute-start.9 = (bf16[1,2048,1536]{2,1,0:T(8,128)(2,1)}, bf16[1,2048,1536]{2,1,0:T(8,128)(2,1)}, u32[]{:S(2)}, u32[]{:S(2)}) collective-permute-start(bf16[1,2048,1536]{2,1,0:T(8,128)(2,1)} %get-tuple-element.113), channel_id=1, source_target_pairs={{0,4},{4,0},{1,5},{5,1},{2,6},{6,2},{3,7},{7,3}} | collective-permute-start | bytes 18874376 | tf_op jit(solution)/shard_map/ppermute | solution.py:455
  737.4 487.0 %collective-permute-start.7 = (bf16[1,1536,1536]{2,1,0:T(8,128)(2,1)}, bf16[1,1536,1536]{2,1,0:T(8,128)(2,1)}, u32[]{:S(2)}, u32[]{:S(2)}) collective-permute-start(bf16[1,1536,1536]{2,1,0:T(8,128)(2,1)} %get-tuple-element.111), channel_id=1, source_target_pairs={{0,4},{4,0},{1,5},{5,1},{2,6},{6,2},{3,7},{7,3}} | collective-permute-start | bytes 14155784 | tf_op jit(solution)/shard_map/ppermute | solution.py:455
  739.2 485.2 %collective-permute-start.6 = (bf16[1,1024,1536]{2,1,0:T(8,128)(2,1)}, bf16[1,1024,1536]{2,1,0:T(8,128)(2,1)}, u32[]{:S(2)}, u32[]{:S(2)}) collective-permute-start(bf16[1,1024,1536]{2,1,0:T(8,128)(2,1)} %get-tuple-element.110), channel_id=1, source_target_pairs={{0,4},{4,0},{1,5},{5,1},{2,6},{6,2},{3,7},{7,3}} | collective-permute-start | bytes 9437192 | tf_op jit(solution)/shard_map/ppermute | solution.py:455
  739.5 470.3 %collective-permute-start.11 = (f32[2,1536]{1,0:T(2,128)S(1)}, f32[2,1536]{1,0:T(2,128)S(1)}, u32[]{:S(2)}, u32[]{:S(2)}) collective-permute-start(f32[2,1536]{1,0:T(2,128)S(1)} %add_reduce_fusion), channel_id=1, source_target_pairs={{0,4},{4,0},{1,5},{5,1},{2,6},{6,2},{3,7},{7,3}} | collective-permute-start | bytes 36872 | tf_op jit(solution)/shard_map/ppermute | solution.py:507
  1209.8 8.4 collective-permute-start.12
  1218.3 3.7 collective-permute-start.13
  1222.0 76.5 %collective-permute-start.10 = (bf16[1,1024,1536]{2,1,0:T(8,128)(2,1)}, bf16[1,1024,1536]{2,1,0:T(8,128)(2,1)}, u32[]{:S(2)}, u32[]{:S(2)}) collective-permute-start(bf16[1,1024,1536]{2,1,0:T(8,128)(2,1)} %get-tuple-element.120), channel_id=1, source_target_pairs={{0,4},{4,0},{1,5},{5,1},{2,6},{6,2},{3,7},{7,3}} | collective-permute-start | bytes 9437192 | tf_op jit(solution)/shard_map/ppermute | solution.py:455
Sparse Core Ops, SparseCore 0:
  646.2 43.5 reduce-scatter.3
  735.4 73.5 reduce-scatter.5
  812.1 42.3 reduce-scatter.7

commit v9 on v8

--- a/solution.py
+++ b/solution.py
@@ -23,8 +23,8 @@
 ROWS_LIMIT = 38_000_000
 HOLD_LIMIT = 36_000_000
 SUM_ROWS = 1024
-OWN_CHUNKS = ((4,), (6,), (10,), (8, 4))
-EARLY_V = 6
+OWN_CHUNKS = ((4,), (6,), (10,), (6, 6))
+EARLY_V = 4
 
 
 def dot(a, b, dims=NN):
@@ -67,8 +67,9 @@
     return pl.CostEstimate(flops=int(flops), bytes_accessed=int(nbytes), transcendentals=0)
 
 
-def project_body(x_ref, g_ref, w_ref, wo_ref, gm_ref, bt_ref, u_ref, q_ref, k_ref, v_ref, do_ref, st_ref, part_ref, gr, da, qs, ks):
+def project_body(x_ref, g_ref, w_ref, wo_ref, gm_ref, bt_ref, u_ref, act_ref, st_ref, part_ref, gr, da, qs, ks):
     i = pl.program_id(0)
+    q_ref, k_ref, v_ref, do_ref = (act_ref.at[e] for e in range(4))
     rows, cols = q_ref.shape
     groups = cols // GROUP
     do_ref[...] = dot(g_ref[...], wo_ref[...], NT).astype(BF16)
@@ -101,25 +102,25 @@
                     tot += jnp.where(col_head == h, acc[s, h * HEAD:(h + 1) * HEAD, :], 0.0)
                 part_ref[(a * groups + s) * HEAD:(a * groups + s + 1) * HEAD, :] = tot
         base = 2 * groups * HEAD
+        part_ref[base:, :] = jnp.zeros((part_ref.shape[0] - base, GROUP), F32)
         for a, acc in enumerate((qs, ks)):
             tot = jnp.sum(acc[...], axis=0, keepdims=True)
             for s in range(groups):
-                part_ref[base + 8 * (a * groups + s):base + 8 * (a * groups + s + 1), :] = jnp.broadcast_to(
-                    tot[:, s * GROUP:(s + 1) * GROUP], (8, GROUP))
+                part_ref[base + a * groups + s:base + a * groups + s + 1, :] = tot[:, s * GROUP:(s + 1) * GROUP]
 
 
 def project(x, g, w3, wo, gamma, beta):
     tokens, width = x.shape
     cols = wo.shape[0]
     groups = cols // GROUP
-    part_rows = 2 * groups * (HEAD + 8)
+    part_rows = 2 * groups * HEAD + 8 * pl.cdiv(2 * groups, 8)
     row = lambda c: row_spec(PROJ_ROWS, c, lambda i: i)
     return pl.pallas_call(
         project_body,
         grid=(tokens // PROJ_ROWS,),
         in_specs=[row(width), row(width), whole(w3.shape), whole(wo.shape), whole(gamma.shape), whole(beta.shape)],
-        out_specs=[row(width)] + [row(cols)] * 4 + [row(LANES), pl.BlockSpec((part_rows, GROUP), lambda i: (0, 0))],
-        out_shape=[sds((tokens, width), BF16)] + [sds((tokens, cols), BF16)] * 4 + [sds((tokens, LANES), F32), sds((part_rows, GROUP), F32)],
+        out_specs=[row(width), pl.BlockSpec((4, PROJ_ROWS, cols), lambda i: (0, i, 0)), row(LANES), pl.BlockSpec((part_rows, GROUP), lambda i: (0, 0))],
+        out_shape=[sds((tokens, width), BF16), sds((4, tokens, cols), BF16), sds((tokens, LANES), F32), sds((part_rows, GROUP), F32)],
         scratch_shapes=[pltpu.VMEM((groups, GROUP, GROUP), F32)] * 2 + [pltpu.VMEM((8, cols), F32)] * 2,
         name="project",
         compiler_params=params(),
@@ -168,8 +169,8 @@
         for s in range(groups):
             gram_mat = spread(ref[s * HEAD:(s + 1) * HEAD, :])
             d_attn = spread(ref[(groups + s) * HEAD:(groups + s + 1) * HEAD, :])
-            b_row = ref[base + 8 * (groups + s):base + 8 * (groups + s) + 1, :]
-            a_col = to_col(ref[base + 8 * s:base + 8 * s + 1, :])
+            b_row = ref[base + groups + s:base + groups + s + 1, :]
+            a_col = to_col(ref[base + s:base + s + 1, :])
             g = side * groups + s
             tau = to_col(tau_ref[g:g + 1, :])
             norm_prod = jnp.sqrt(a_col) * jnp.sqrt(b_row)
@@ -239,12 +240,12 @@
 def rows_body(*refs, n_alias, send_blocks):
     it = iter(refs)
     nxt = lambda n: [next(it) for _ in range(n)]
-    off_ref, x_ref, g_ref, u_ref, st_ref, q_ref, k_ref, v_ref, do_ref = nxt(9)
+    off_ref, x_ref, g_ref, u_ref, st_ref, act_ref = nxt(6)
     attn_ref, dgram_ref, coef_ref, gm_ref = nxt(4)
     wn_ref, wf_ref = nxt(3), nxt(3)
     won_ref, wof_ref = nxt(2)
     nxt(n_alias)
-    y_ref, gx_ref, o_ref, rqk_ref, rv_ref = nxt(5)
+    y_ref, gx_ref, r_ref = nxt(3)
     send_refs = nxt(len(send_blocks))
     (dsum_ref,) = nxt(1)
     on_s, rn_s, of_s, rf_s, qf_s, kf_s, vf_s, dof_s, gh_s = nxt(9)
@@ -257,8 +258,8 @@
         for s in range(groups):
             c = slice(s * GROUP, (s + 1) * GROUP)
             for half in (own, other):
-                o, dq, dk, dv = mix_block(q_ref[half, :, c], k_ref[half, :, c], v_ref[half, :, c], do_ref[half, :, c], *state, 0, s)
-                o_ref[half, :, c], rqk_ref[0, half, :, c], rqk_ref[1, half, :, c], rv_ref[half, :, c] = o, dq, dk, dv
+                o, dq, dk, dv = mix_block(*(act_ref[e, half, :, c] for e in range(4)), *state, 0, s)
+                r_ref[0, half, :, c], r_ref[1, half, :, c], r_ref[2, half, :, c], r_ref[3, half, :, c] = dq, dk, dv, o
                 if half is own:
                     on_s[:, c], rn_s[0, :, c], rn_s[1, :, c], rn_s[2, :, c] = o, dq, dk, dv
         u = u_ref[0]
@@ -317,7 +318,7 @@
     blocks = sum(send_blocks)
     firsts = [sum(send_blocks[:n]) for n in range(len(send_blocks))]
     send_spec = lambda first, n: pl.BlockSpec((1, ROWS, width), lambda j, off: (0, jnp.clip(j - first, 0, n - 1), 0))
-    cols = acts[4].shape[2]
+    cols = acts[4].shape[-1]
     row = half_spec(ROWS, width, 0, start)
     both = lambda *lead: both_spec(lead, ROWS, cols, start)
     *loaded, gamma = weights
@@ -328,14 +329,14 @@
         grid_spec=pltpu.PrefetchScalarGridSpec(
             num_scalar_prefetch=1,
             grid=(blocks,),
-            in_specs=[row] * 3 + [half_spec(ROWS, LANES, 0, start)] + [both()] * 4 + [whole(t.shape) for t in consts] + [pl.BlockSpec(memory_space=pltpu.VMEM)] * len(loaded) + [pl.BlockSpec(memory_space=pl.ANY)] * len(prev),
-            out_specs=[row, row, both(), both(2), both(),
+            in_specs=[row] * 3 + [half_spec(ROWS, LANES, 0, start), both(4)] + [whole(t.shape) for t in consts] + [pl.BlockSpec(memory_space=pltpu.VMEM)] * len(loaded) + [pl.BlockSpec(memory_space=pl.ANY)] * len(prev),
+            out_specs=[row, row, both(4),
                        *[send_spec(first, n) for first, n in zip(firsts, send_blocks)],
                        pl.BlockSpec((2, 8, width), lambda j, off: (0, 0, 0))],
             scratch_shapes=[pltpu.VMEM((ROWS, cols), BF16), pltpu.VMEM((3, ROWS, cols), BF16)] * 2 + [pltpu.VMEM((ROWS, cols), BF16)] * 4
             + [pltpu.VMEM((ROWS, width), F32)],
         ),
-        out_shape=[sds((2, half, width), BF16)] * 2 + [sds((2, half, cols), BF16), sds((2, 2, half, cols), BF16), sds((2, half, cols), BF16),
+        out_shape=[sds((2, half, width), BF16)] * 2 + [sds((4, 2, half, cols), BF16),
                                                        *[sds((1, n * ROWS, width), BF16) for n in send_blocks], sds((2, 8, width), F32)],
         input_output_aliases={first + a: a for a in range(len(prev))},
         name="rows",
@@ -378,13 +379,13 @@
     for s in range(groups):
         c = slice(s * GROUP, (s + 1) * GROUP)
         of_s[:, c] = dot(vf_s[:, c], attn_ref[groups + s], NT).astype(BF16)
-    y_ref[0] = (x_ref[0].astype(F32) + (dot(o_ref[0], won_ref[...]) + dot(of_s[...], wof_ref[...]))).astype(BF16)
+    y_ref[0] = (x_ref[0].astype(F32) + (dot(o_ref[0, 0], won_ref[...]) + dot(of_s[...], wof_ref[...]))).astype(BF16)
     file_rows(lambda copy: copy.wait())
 
 
-def far_y(off, x2, o2, u2, vf, attn, wo_near, wo_far, w_far, dw_v, recv, y2, gx2):
+def far_y(off, x2, r, u2, vf, attn, wo_near, wo_far, w_far, dw_v, recv, y2, gx2):
     half, width = x2.shape[1:]
-    cols = o2.shape[2]
+    cols = r.shape[-1]
     rows = 2 * ROWS
     steps = half // rows
     early = vf.shape[0] // rows
@@ -392,13 +393,13 @@
     row = lambda c: half_spec(rows, c, 1, 0)
     part = (1, dw_v.shape[1] // steps, cols)
     any_ = pl.BlockSpec(memory_space=pl.ANY)
-    specs = [row(width), row(cols),
+    specs = [row(width), pl.BlockSpec((1, 1, rows, cols), lambda j, off: (3, off[1], j, 0)),
              pl.BlockSpec((1, rows, width), lambda j, off: (off[1], jnp.maximum(j, early), 0)),
              pl.BlockSpec((rows, cols), lambda j, off: (jnp.minimum(j, early - 1), 0)),
              whole(attn.shape), whole(wo_near.shape), whole(wo_far.shape),
              pl.BlockSpec((1, width, cols), lambda j, off: (2, 0, 0), pipeline_mode=pl.Buffered(1)),
              pl.BlockSpec(part, lambda j, off: (0, j, 0))]
-    args = [x2, o2, u2, vf, attn, wo_near, wo_far, w_far, dw_v, *recv]
+    args = [x2, r, u2, vf, attn, wo_near, wo_far, w_far, dw_v, *recv]
     return pl.pallas_call(
         functools.partial(far_y_body, early=early, copies=copies),
         grid_spec=pltpu.PrefetchScalarGridSpec(
@@ -423,26 +424,24 @@
     for l_ref, r_ref, count in zip(refs[:n], refs[n:out], planes):
         o_ref, out = refs[out], out + 1
         for e in range(count):
-            val = dot(l_ref[...], r_ref[e], TN)
+            val = dot(l_ref[0], r_ref[e], TN)
             o_ref[e] = jnp.where(first, val, o_ref[e] + val)
 
 
 def token_sum(*pairs):
-    tokens = pairs[0][0].shape[0]
-    flops = sum(2 * r.shape[0] * tokens * l.shape[1] * r.shape[2] for l, r in pairs)
-    nbytes = sum(2 * tokens * (l.shape[1] + r.shape[0] * r.shape[2]) for l, r in pairs)
-    shapes = [(r.shape[0], l.shape[1], r.shape[2]) for l, r in pairs]
-    return pl.pallas_call(
-        functools.partial(token_sum_body, planes=[r.shape[0] for _, r in pairs]),
+    tokens = pairs[0][0][0].shape[1]
+    spec = lambda t, e, count: pl.BlockSpec((count, SUM_ROWS, t.shape[2]), lambda i: (e // count, i, 0))
+    shapes = [(count, l.shape[2], r.shape[2]) for (l, _), (r, _, count) in pairs]
+    return pl.pallas_call(
+        functools.partial(token_sum_body, planes=[s[0] for s in shapes]),
         grid=(tokens // SUM_ROWS,),
-        in_specs=[row_spec(SUM_ROWS, l.shape[1], lambda i: i) for l, _ in pairs]
-        + [pl.BlockSpec((r.shape[0], SUM_ROWS, r.shape[2]), lambda i: (0, i, 0)) for _, r in pairs],
+        in_specs=[spec(l, e, 1) for (l, e), _ in pairs] + [spec(*rhs) for _, rhs in pairs],
         out_specs=[pl.BlockSpec(s, lambda i: (0, 0, 0)) for s in shapes],
         out_shape=[sds(s, F32) for s in shapes],
         name="token_sum",
         compiler_params=params(),
-        cost_estimate=cost(flops, nbytes),
-    )(*[l for l, _ in pairs], *[r for _, r in pairs])
+        cost_estimate=cost(sum(2 * tokens * a * b * c for a, b, c in shapes), sum(2 * tokens * (b + a * c) for a, b, c in shapes)),
+    )(*[l for (l, _), _ in pairs], *[rhs[0] for _, rhs in pairs])
 
 
 def solution(mesh):
@@ -466,9 +465,9 @@
         off = jnp.stack([me, 1 - me]).astype(jnp.int32)
         halves = lambda t: t.reshape(2, half, t.shape[-1])
 
-        u, q, k, v, do, stats, part = project(x, g, w_near, w_out, ln_gamma, ln_beta)
+        u, near, stats, part = project(x, g, w_near, w_out, ln_gamma, ln_beta)
         x2, g2, u2, stats2 = halves(x), halves(g), halves(u), halves(stats)
-        near = tuple(halves(t) for t in (q, k, v, do))
+        near = near.reshape(4, 2, half, cols)
         peers = [lax.ppermute(part, "sp", [(s, s ^ d) for s in range(sp_size)]) for d in (1, 2, 3)]
         part = (part + peers[0]) + (peers[1] + peers[2])
         part, wn_, wf_ = lax.optimization_barrier((part, w_near, w_far))
@@ -482,24 +481,25 @@
 
         prev, dsum, recv, start = (), None, [], 0
         for sizes in OWN_CHUNKS:
-            out = rows_call(off, start, sizes, (x2, g2, u2, stats2) + near, state, (*held, ln_gamma), prev)
-            prev, sent, ds = out[:5], out[5:-1], out[-1]
+            out = rows_call(off, start, sizes, (x2, g2, u2, stats2, near), state, (*held, ln_gamma), prev)
+            prev, sent, ds = out[:3], out[3:-1], out[-1]
             recv += [exchange(t) for t in sent]
             dsum = ds if dsum is None else dsum + ds
             start += sum(sizes)
-        y2, gx2, o2, rqk, rv = prev
-        dtau, rqk = lax.optimization_barrier((dtau, rqk))
+        y2, gx2, r = prev
+        dtau, r = lax.optimization_barrier((dtau, r))
         dtau = jnp.sum(dtau[:2 * groups].reshape(tp_size, cols // HEAD, HEAD), axis=2)
         grad_temp = jnp.where(me == 0, dtau, dtau[::-1]).reshape(-1)
 
-        dw_o, dw_v = token_sum((o2.reshape(tokens, cols), g[None]), (u, rv.reshape(1, tokens, cols)))
-        rqk, dw_o, dw_v = lax.optimization_barrier((rqk, dw_o, dw_v))
+        flat = r.reshape(4, tokens, cols)
+        dw_o, dw_v = token_sum(((flat, 3), (g[None], 0, 1)), ((u[None], 0), (flat, 2, 1)))
+        flat, dw_o, dw_v = lax.optimization_barrier((flat, dw_o, dw_v))
         grad_wout = lax.psum_scatter(dw_o[0], "sp", scatter_dimension=0, tiled=True)
         dw_v = lax.psum_scatter(dw_v, "sp", scatter_dimension=1, tiled=True)
-        (dw_qk,) = token_sum((u, rqk.reshape(2, tokens, cols)))
+        (dw_qk,) = token_sum(((u[None], 0), (flat, 0, 2)))
         y2, dw_qk = lax.optimization_barrier((y2, dw_qk))
         dw_qk = lax.psum_scatter(dw_qk, "sp", scatter_dimension=1, tiled=True)
-        y2, gx2, gw = far_y(off, x2, o2, u2, vf, attn, w_out, wo_far, w_far, dw_v, recv[:-1], y2, gx2)
+        y2, gx2, gw = far_y(off, x2, r, u2, vf, attn, w_out, wo_far, w_far, dw_v, recv[:-1], y2, gx2)
         grad_wqkv = jnp.transpose(lax.dynamic_update_slice(gw, dw_qk, (0, 0, 0)), (1, 0, 2))
 
         sums = jnp.sum(dsum, axis=1)

time: 1320 us -> 1310 us (level)
    ppermute x3, waiting for transfers between devices: 470 us -> 437 us  [step(): sums = sums + lax.ppermute(sums, axis, perm)]
    ppermute x8, waiting for transfers between devices: 1.03 us -> 26.8 us  [exchange(): return lax.ppermute(t, 'tp', swap)]
  transfers between devices with their start and end apart: 17 -> 17, of which waited for: 5 -> 6; matrix products, arithmetic and copies ran while one was open for 1% -> 1% of each run, Pallas kernels for 29% -> 29%
where the time goes in v9:
time: 1310 us; the launch traced here: 1300 us
  Pallas kernels  788 us (60%)
  waiting for transfers between devices  471 us (36%)
  starting transfers between devices  16.2 us (1%)
  between operations  14.4 us (1%)
    ppermute x3, waiting for transfers between devices, step(): sums = sums + lax.ppermute(sums, axis, perm)  437 us
    pallas_call x4, Pallas kernels, rows_call(): pl.pallas_call(functools.partial(rows_body, n_alias=len(prev), send_block...  324 us
    pallas_call x1, Pallas kernels, project(): pl.pallas_call(project_body, grid=(tokens // PROJ_ROWS,), in_specs=[row(w...  198 us
    pallas_call x2, Pallas kernels, token_sum(): pl.pallas_call(functools.partial(token_sum_body, planes=[s[0] for s in sh...  177 us
    pallas_call x1, Pallas kernels, far_y(): pl.pallas_call(functools.partial(far_y_body, early=early, copies=copies),...  74.8 us
    ppermute x8, waiting for transfers between devices, exchange(): return lax.ppermute(t, 'tp', swap)  26.8 us
  transfers between devices with their start and end apart: 17, of which 6 were waited for; matrix products, arithmetic and copies ran while one was open for 1% of the time, Pallas kernels for 29%

profile of v9, /device:TPU:0, one launch (start us, length us, event | category | flops | bytes accessed | tf_op | source)
XLA Modules:
  0.0 1301.8 jit_solution(13470092548728125200)
XLA Ops:
  7.2 0.0 reduce-scatter.4.cloned.1.call-start
  7.2 3.4 collective-permute-start.3
  10.6 0.0 collective-permute-start.5
  10.6 198.0 %project.1 = (bf16[16384,1536]{1,0:T(8,128)(2,1)}, bf16[4,16384,768]{2,1,0:T(8,128)(2,1)}, f32[16384,128]{1,0:T(8,128)}, f32[200,256]{1,0:T(8,128)}) custom-call(bf16[16384,1536]{1,0:T(8,128)(2,1)} %x_ref.1, bf16[16384,1536]{1,0:T(8,128)(2,1)} %g_ref.1, bf16[3,1536,768]{2,1,0:T(8,128)(2,1)} %bitcast.46, bf16[768,1536]{1,0:T(8,128)(2,1)} %refs_6_.1, ...), custom_call_target="tpu_custom_call" | custom-call | flops 170080698368 | bytes 251658240 | tf_op jit(solution)/shard_map/project/pallas_call | solution.py:118
  208.7 2.0 collective-permute-start.1
  210.6 0.0 collective-permute-start.2
  210.6 0.2 collective-permute-start
  210.8 0.1 broadcast_in_dim.14
  210.9 0.1 broadcast_in_dim.15
  211.0 0.1 broadcast_in_dim.16
  211.1 0.3 rev.6
  211.4 5.4 collective-permute-done.1
  216.8 2.3 collective-permute-done.2
  219.1 0.0 collective-permute-done
  219.1 1.0 add_add_fusion.near_ref
  220.1 0.0 collective-permute-done.3.refs_3_.refs_4_.refs_5_.w_ref.refs_8_
  220.1 1.5 collective-permute-start.4
  221.7 0.1 pad_add_fusion.refs_0_.off_ref
  221.8 5.2 hold.1
  226.9 0.0 copy-start
  227.0 0.7 collective-permute-done.4.far_ref
  227.7 2.7 head_state.1
  230.4 0.0 collective-permute-done.5.refs_17_.refs_7_
  230.4 0.0 copy-done.2
  230.4 43.1 %rows.4 = (bf16[2,8192,1536]{2,1,0:T(8,128)(2,1)}, bf16[2,8192,1536]{2,1,0:T(8,128)(2,1)}, bf16[4,2,8192,768]{3,2,1,0:T(8,128)(2,1)}, bf16[1,1024,1536]{2,1,0:T(8,128)(2,1)}, f32[2,8,1536]{2,1,0:T(8,128)S(1)}) custom-call(s32[2]{0:T(128)S(1)} %pad_add_fusion.refs_0_.off_ref, bf16[2,8192,1536]{2,1,0:T(8,128)(2,1)} %bitcast.34, ...), custom_call_target="tpu_custom_call" | custom-call | flops 31406948352 | bytes 44040192 | tf_op jit(solution)/shard_map/rows/pallas_call | solution.py:327
  273.5 62.2 %rows.5 = (bf16[2,8192,1536]{2,1,0:T(8,128)(2,1)}, bf16[2,8192,1536]{2,1,0:T(8,128)(2,1)}, bf16[4,2,8192,768]{3,2,1,0:T(8,128)(2,1)}, bf16[1,1536,1536]{2,1,0:T(8,128)(2,1)}, f32[2,8,1536]{2,1,0:T(8,128)S(1)}) custom-call(s32[2]{0:T(128)S(1)} %pad_add_fusion.refs_0_.off_ref, ...), custom_call_target="tpu_custom_call", output_to_operand_aliasing={{0}: (18, {}), {1}: (19, {}), {2}: (20, {})} | custom-call | flops 47110422528 | bytes 66060288 | tf_op jit(solution)/shard_map/rows/pallas_call | solution.py:327
  335.8 99.3 %rows.6 = (bf16[2,8192,1536]{2,1,0:T(8,128)(2,1)}, bf16[2,8192,1536]{2,1,0:T(8,128)(2,1)}, bf16[4,2,8192,768]{3,2,1,0:T(8,128)(2,1)}, bf16[1,2560,1536]{2,1,0:T(8,128)(2,1)}, f32[2,8,1536]{2,1,0:T(8,128)S(1)}) custom-call(s32[2]{0:T(128)S(1)} %pad_add_fusion.refs_0_.off_ref, ...), custom_call_target="tpu_custom_call", output_to_operand_aliasing={{0}: (18, {}), {1}: (19, {}), {2}: (20, {})} | custom-call | flops 78517370880 | bytes 110100480 | tf_op jit(solution)/shard_map/rows/pallas_call | solution.py:327
  435.0 119.0 %rows.7 = (bf16[2,8192,1536]{2,1,0:T(8,128)(2,1)}, bf16[2,8192,1536]{2,1,0:T(8,128)(2,1)}, bf16[4,2,8192,768]{3,2,1,0:T(8,128)(2,1)}, bf16[1,1536,1536]{2,1,0:T(...) custom-call(s32[2]{0:T(128)S(1)} %pad_add_fusion.refs_0_.off_ref, ...), custom_call_target="tpu_custom_call", output_to_operand_aliasing={{0}: (18, {}), {1}: (19, {}), {2}: (20, {})} | custom-call | flops 94220845056 | bytes 132120576 | tf_op jit(solution)/shard_map/rows/pallas_call | solution.py:327
  554.0 88.2 %token_sum.2 = (f32[1,768,1536]{2,1,0:T(8,128)}, f32[1,1536,768]{2,1,0:T(8,128)}) custom-call(bf16[4,16384,768]{2,1,0:T(8,128)(2,1)} %bitcast.8.refs_0_.refs_3_.refs_1_, bf16[1,16384,1536]{2,1,0:T(8,128)(2,1)} %bitcast.25, bf16[1,16384,1536]{2,1,0:T(8,128)(2,1)} %bitcast.33, bf16[4,16384,768]{2,1,0:T(8,128)(2,1)} %bitcast.8.refs_0_.refs_3_.refs_1_), custom_call_target="tpu_custom_call" | custom-call | flops 77309411328 | bytes 150994944 | tf_op jit(solution)/shard_map/token_sum/pallas_call | solution.py:435
  642.2 0.0 reduce-scatter.4.cloned.1.call-update
  642.2 0.0 reduce-scatter.6.cloned.1.call-start
  642.3 88.9 %token_sum.3 = f32[2,1536,768]{2,1,0:T(8,128)} custom-call(bf16[1,16384,1536]{2,1,0:T(8,128)(2,1)} %bitcast.26, bf16[4,16384,768]{2,1,0:T(8,128)(2,1)} %bitcast.8.refs_0_.refs_3_.refs_1_), custom_call_target="tpu_custom_call" | custom-call | flops 77309411328 | bytes 100663296 | tf_op jit(solution)/shard_map/token_sum/pallas_call | solution.py:435
  731.2 0.0 reduce-scatter.6.cloned.1.call-update
  731.2 0.0 reduce-scatter.8.cloned.1.call-start
  731.3 1.7 collective-permute-start.8
  733.0 0.4 collective-permute-start.7
  733.3 1.7 collective-permute-start.9
  735.0 0.0 reduce-scatter.8.cloned.1.call-update
  735.0 0.4 collective-permute-start.6
  735.4 0.1 add_reduce_fusion
  735.4 1.7 collective-permute-start.11
  737.1 435.2 %collective-permute-done.11 = f32[2,1536]{1,0:T(2,128)S(1)} collective-permute-done((f32[2,1536]{1,0:T(2,128)S(1)}, f32[2,1536]{1,0:T(2,128)S(1)}, u32[]{:S(2)}, u32[]{:S(2)}) %collective-permute-start.11) | collective-permute-done | bytes 12320 | tf_op jit(solution)/shard_map/ppermute | solution.py:507
  1172.3 0.0 collective-permute-start.12
  1172.4 6.5 far_v.1.refs_4_
  1178.9 0.1 reshape.58
  1179.0 0.1 reduce_sum.19
  1179.1 0.0 collective-permute-done.12
  1179.1 1.4 collective-permute-start.13
  1180.5 0.6 reshape.59
  1181.1 1.7 collective-permute-done.13
  1182.8 1.7 collective-permute-start.10
  1184.6 0.6 slice_reduce_fusion
  1185.2 0.0 collective-permute-done.6.refs_10_
  1185.2 0.0 collective-permute-done.7.refs_11_
  1185.2 0.0 collective-permute-done.9.refs_13_
  1185.2 0.0 collective-permute-done.8.refs_12_
  1185.2 0.0 reduce-scatter.4.cloned.1.call-done.refs_9_
  1185.3 74.8 %far_y.1 = (bf16[2,8192,1536]{2,1,0:T(8,128)(2,1)}, bf16[2,8192,1536]{2,1,0:T(8,128)(2,1)}, f32[3,384,768]{2,1,0:T(8,128)}) custom-call(s32[2]{0:T(128)} %copy-done.3, bf16[2,8192,1536]{2,1,0:T(8,128)(2,1)} %bitcast.38, bf16[4,2,8192,768]{3,2,1,0:T(8,128)(2,1)} %get-tuple-element.84.refs_2_, ...), custom_call_target="tpu_custom_call", output_to_operand_aliasing={{0}: (14, {}), {1}: (15, {})} | custom-call | flops 54116589568 | bytes 138412032 | tf_op jit(solution)/shard_map/far_y/pallas_call | solution.py:403
  1260.1 26.1 %collective-permute-done.10 = bf16[1,1536,1536]{2,1,0:T(8,128)(2,1)} collective-permute-done((bf16[1,1536,1536]{2,1,0:T(8,128)(2,1)}, bf16[1,1536,1536]{2,1,0:T(8,128)(2,1)}, u32[]{:S(2)}, u32[]{:S(2)}) %collective-permute-start.10) | collective-permute-done | bytes 4718624 | tf_op jit(solution)/shard_map/ppermute | solution.py:454
  1286.2 5.0 constant_dynamic-update-slice_fusion
  1291.2 1.8 constant_dynamic-update-slice_fusion.1
  1293.0 0.0 copy-start.6
  1293.0 0.0 reduce-scatter.8.cloned.1.call-done
  1293.0 1.8 copy-done.6
  (20 shorter events, 0.1 us)
Async XLA Ops:
  7.2 1178.1 %reduce-scatter.4.cloned.1.call-start = ((), (), s32[]{:S(2)}) async-start(), calls=%async_computation.3 | async-start | bytes 5898240 | tf_op jit(solution)/shard_map/reduce_scatter | solution.py:498
  7.2 212.9 %collective-permute-start.3 = (bf16[3,1536,768]{2,1,0:T(8,128)(2,1)}, bf16[3,1536,768]{2,1,0:T(8,128)(2,1)}, u32[]{:S(2)}, u32[]{:S(2)}) collective-permute-start(bf16[3,1536,768]{2,1,0:T(8,128)(2,1)} %bitcast.45), channel_id=1, source_target_pairs={{0,4},{4,0},{1,5},{5,1},{2,6},{6,2},{3,7},{7,3}} | collective-permute-start | bytes 21233672 | tf_op jit(solution)/shard_map/ppermute | solution.py:454
  10.6 219.8 %collective-permute-start.5 = (bf16[768,1536]{1,0:T(8,128)(2,1)}, bf16[768,1536]{1,0:T(8,128)(2,1)}, u32[]{:S(2)}, u32[]{:S(2)}) collective-permute-start(bf16[768,1536]{1,0:T(8,128)(2,1)} %refs_6_.1), channel_id=1, source_target_pairs={{0,4},{4,0},{1,5},{5,1},{2,6},{6,2},{3,7},{7,3}} | collective-permute-start | bytes 7077896 | tf_op jit(solution)/shard_map/ppermute | solution.py:454
  10.6 200.2 %copy-start.4 = (f32[48]{0:T(128)S(1)}, f32[48]{0:T(128)}, u32[]{:S(2)}) copy-start(f32[48]{0:T(128)} %param.13) | copy-start | bytes 580
  208.7 8.2 collective-permute-start.1
  210.6 8.5 collective-permute-start.2
  210.6 8.5 collective-permute-start
  220.1 7.5 collective-permute-start.4
  221.8 213.2 %copy-start.3 = (s32[2]{0:T(128)}, s32[2]{0:T(128)S(1)}, u32[]{:S(2)}) copy-start(s32[2]{0:T(128)S(1)} %pad_add_fusion.refs_0_.off_ref) | copy-start | bytes 28
  221.8 8.6 copy-start.2
  226.9 3.4 copy-start
  230.4 204.7 %copy-start.1 = (bf16[6,256,256]{2,1,0:T(8,128)(2,1)}, bf16[6,256,256]{2,1,0:T(8,128)(2,1)S(1)}, u32[]{:S(2)}) copy-start(bf16[6,256,256]{2,1,0:T(8,128)(2,1)S(1)} %get-tuple-element.63.refs_6_.refs_5_) | copy-start | bytes 2359300
  642.2 649.0 %reduce-scatter.6.cloned.1.call-start = ((), (), s32[]{:S(2)}) async-start(), calls=%async_computation.4 | async-start | bytes 11796480 | tf_op jit(solution)/shard_map/reduce_scatter | solution.py:501
  731.2 561.8 %reduce-scatter.8.cloned.1.call-start = ((), (), s32[]{:S(2)}) async-start(), calls=%async_computation.5 | async-start | bytes 5898240 | tf_op jit(solution)/shard_map/reduce_scatter | solution.py:497
  731.3 453.9 %collective-permute-start.8 = (bf16[1,2560,1536]{2,1,0:T(8,128)(2,1)}, bf16[1,2560,1536]{2,1,0:T(8,128)(2,1)}, u32[]{:S(2)}, u32[]{:S(2)}) collective-permute-start(bf16[1,2560,1536]{2,1,0:T(8,128)(2,1)} %get-tuple-element.90), channel_id=1, source_target_pairs={{0,4},{4,0},{1,5},{5,1},{2,6},{6,2},{3,7},{7,3}} | collective-permute-start | bytes 23592968 | tf_op jit(solution)/shard_map/ppermute | solution.py:454
  733.0 452.3 %collective-permute-start.7 = (bf16[1,1536,1536]{2,1,0:T(8,128)(2,1)}, bf16[1,1536,1536]{2,1,0:T(8,128)(2,1)}, u32[]{:S(2)}, u32[]{:S(2)}) collective-permute-start(bf16[1,1536,1536]{2,1,0:T(8,128)(2,1)} %get-tuple-element.89), channel_id=1, source_target_pairs={{0,4},{4,0},{1,5},{5,1},{2,6},{6,2},{3,7},{7,3}} | collective-permute-start | bytes 14155784 | tf_op jit(solution)/shard_map/ppermute | solution.py:454
  733.3 451.9 %collective-permute-start.9 = (bf16[1,1536,1536]{2,1,0:T(8,128)(2,1)}, bf16[1,1536,1536]{2,1,0:T(8,128)(2,1)}, u32[]{:S(2)}, u32[]{:S(2)}) collective-permute-start(bf16[1,1536,1536]{2,1,0:T(8,128)(2,1)} %get-tuple-element.91), channel_id=1, source_target_pairs={{0,4},{4,0},{1,5},{5,1},{2,6},{6,2},{3,7},{7,3}} | collective-permute-start | bytes 14155784 | tf_op jit(solution)/shard_map/ppermute | solution.py:454
  735.0 450.2 %collective-permute-start.6 = (bf16[1,1024,1536]{2,1,0:T(8,128)(2,1)}, bf16[1,1024,1536]{2,1,0:T(8,128)(2,1)}, u32[]{:S(2)}, u32[]{:S(2)}) collective-permute-start(bf16[1,1024,1536]{2,1,0:T(8,128)(2,1)} %get-tuple-element.88), channel_id=1, source_target_pairs={{0,4},{4,0},{1,5},{5,1},{2,6},{6,2},{3,7},{7,3}} | collective-permute-start | bytes 9437192 | tf_op jit(solution)/shard_map/ppermute | solution.py:454
  735.4 436.9 %collective-permute-start.11 = (f32[2,1536]{1,0:T(2,128)S(1)}, f32[2,1536]{1,0:T(2,128)S(1)}, u32[]{:S(2)}, u32[]{:S(2)}) collective-permute-start(f32[2,1536]{1,0:T(2,128)S(1)} %add_reduce_fusion), channel_id=1, source_target_pairs={{0,4},{4,0},{1,5},{5,1},{2,6},{6,2},{3,7},{7,3}} | collective-permute-start | bytes 36872 | tf_op jit(solution)/shard_map/ppermute | solution.py:507
  1172.3 6.8 collective-permute-start.12
  1179.1 3.7 collective-permute-start.13
  1182.8 103.4 %collective-permute-start.10 = (bf16[1,1536,1536]{2,1,0:T(8,128)(2,1)}, bf16[1,1536,1536]{2,1,0:T(8,128)(2,1)}, u32[]{:S(2)}, u32[]{:S(2)}) collective-permute-start(bf16[1,1536,1536]{2,1,0:T(8,128)(2,1)} %get-tuple-element.98), channel_id=1, source_target_pairs={{0,4},{4,0},{1,5},{5,1},{2,6},{6,2},{3,7},{7,3}} | collective-permute-start | bytes 14155784 | tf_op jit(solution)/shard_map/ppermute | solution.py:454
  1286.2 5.0 copy-start.5
  1293.0 1.8 copy-start.6
Sparse Core Ops, SparseCore 0:
  642.3 42.6 reduce-scatter.3
  731.3 72.5 reduce-scatter.5
  807.0 42.3 reduce-scatter.7

commit v10 on v8

--- a/solution.py
+++ b/solution.py
@@ -20,11 +20,11 @@
 PROJ_ROWS = 1024
 ROWS = 256
 STATE_LIMIT = 16_000_000
-ROWS_LIMIT = 38_000_000
+ROWS_LIMIT = 33_600_000
 HOLD_LIMIT = 36_000_000
 SUM_ROWS = 1024
-OWN_CHUNKS = ((4,), (6,), (10,), (8, 4))
-EARLY_V = 6
+OWN_CHUNKS = ((3,), (5,), (9,), (10, 5))
+EARLY_V = 2
 
 
 def dot(a, b, dims=NN):
@@ -55,6 +55,10 @@
     return pl.BlockSpec(shape, lambda *a: (0,) * len(shape), pipeline_mode=pl.Buffered(1))
 
 
+def plane_spec(shape, e):
+    return pl.BlockSpec((1, *shape[1:]), lambda *a: (e, 0, 0), pipeline_mode=pl.Buffered(1))
+
+
 def sds(shape, dtype):
     return jax.ShapeDtypeStruct(shape, dtype)
 
@@ -67,7 +71,7 @@
     return pl.CostEstimate(flops=int(flops), bytes_accessed=int(nbytes), transcendentals=0)
 
 
-def project_body(x_ref, g_ref, w_ref, wo_ref, gm_ref, bt_ref, u_ref, q_ref, k_ref, v_ref, do_ref, st_ref, part_ref, gr, da, qs, ks):
+def project_body(x_ref, g_ref, wq_ref, wk_ref, wv_ref, wo_ref, gm_ref, bt_ref, u_ref, q_ref, k_ref, v_ref, do_ref, st_ref, part_ref, gr, da, qs, ks):
     i = pl.program_id(0)
     rows, cols = q_ref.shape
     groups = cols // GROUP
@@ -76,8 +80,8 @@
     u_ref[...] = (xh * gm_ref[...].reshape(1, -1) + bt_ref[...].reshape(1, -1)).astype(BF16)
     st_ref[...] = jnp.where(lax.broadcasted_iota(jnp.int32, st_ref.shape, 1) < LANES // 2, mean, inv)
     u = u_ref[...]
-    for e, out in enumerate((q_ref, k_ref, v_ref)):
-        out[...] = dot(u, w_ref[e]).astype(BF16)
+    for w_ref, out in ((wq_ref, q_ref), (wk_ref, k_ref), (wv_ref, v_ref)):
+        out[...] = dot(u, w_ref[0]).astype(BF16)
 
     def add(acc, s, val):
         acc[s] = jnp.where(i == 0, val, acc[s] + val)
@@ -101,30 +105,30 @@
                     tot += jnp.where(col_head == h, acc[s, h * HEAD:(h + 1) * HEAD, :], 0.0)
                 part_ref[(a * groups + s) * HEAD:(a * groups + s + 1) * HEAD, :] = tot
         base = 2 * groups * HEAD
+        part_ref[base:, :] = jnp.zeros((part_ref.shape[0] - base, GROUP), F32)
         for a, acc in enumerate((qs, ks)):
             tot = jnp.sum(acc[...], axis=0, keepdims=True)
             for s in range(groups):
-                part_ref[base + 8 * (a * groups + s):base + 8 * (a * groups + s + 1), :] = jnp.broadcast_to(
-                    tot[:, s * GROUP:(s + 1) * GROUP], (8, GROUP))
+                part_ref[base + a * groups + s:base + a * groups + s + 1, :] = tot[:, s * GROUP:(s + 1) * GROUP]
 
 
 def project(x, g, w3, wo, gamma, beta):
     tokens, width = x.shape
     cols = wo.shape[0]
     groups = cols // GROUP
-    part_rows = 2 * groups * (HEAD + 8)
+    part_rows = 2 * groups * HEAD + 8 * pl.cdiv(2 * groups, 8)
     row = lambda c: row_spec(PROJ_ROWS, c, lambda i: i)
     return pl.pallas_call(
         project_body,
         grid=(tokens // PROJ_ROWS,),
-        in_specs=[row(width), row(width), whole(w3.shape), whole(wo.shape), whole(gamma.shape), whole(beta.shape)],
+        in_specs=[row(width), row(width), *[plane_spec(w3.shape, e) for e in range(3)], whole(wo.shape), whole(gamma.shape), whole(beta.shape)],
         out_specs=[row(width)] + [row(cols)] * 4 + [row(LANES), pl.BlockSpec((part_rows, GROUP), lambda i: (0, 0))],
         out_shape=[sds((tokens, width), BF16)] + [sds((tokens, cols), BF16)] * 4 + [sds((tokens, LANES), F32), sds((part_rows, GROUP), F32)],
         scratch_shapes=[pltpu.VMEM((groups, GROUP, GROUP), F32)] * 2 + [pltpu.VMEM((8, cols), F32)] * 2,
         name="project",
         compiler_params=params(),
         cost_estimate=cost(2 * tokens * width * cols * 4.4, 2 * tokens * (3 * width + 4 * cols)),
-    )(x, g, w3, wo, gamma, beta)
+    )(x, g, w3, w3, w3, wo, gamma, beta)
 
 
 def far_v_body(off_ref, u_ref, w_ref, *refs):
@@ -168,8 +172,8 @@
         for s in range(groups):
             gram_mat = spread(ref[s * HEAD:(s + 1) * HEAD, :])
             d_attn = spread(ref[(groups + s) * HEAD:(groups + s + 1) * HEAD, :])
-            b_row = ref[base + 8 * (groups + s):base + 8 * (groups + s) + 1, :]
-            a_col = to_col(ref[base + 8 * s:base + 8 * s + 1, :])
+            b_row = ref[base + groups + s:base + groups + s + 1, :]
+            a_col = to_col(ref[base + s:base + s + 1, :])
             g = side * groups + s
             tau = to_col(tau_ref[g:g + 1, :])
             norm_prod = jnp.sqrt(a_col) * jnp.sqrt(b_row)
@@ -351,17 +355,20 @@
     recv = nxt(len(copies))
     _, _, y_ref, gx_ref, gw_ref, vf_s, of_s, sem = nxt(8)
     j = pl.program_id(0)
-    rows = gx_ref.shape[1]
+    per = gx_ref.shape[1] // ROWS
 
     def file_rows(act):
-        start = 0
-        for ref, n in zip(recv, copies):
-
-            @pl.when((j >= start) & (j < start + n))
-            def _(ref=ref, start=start):
-                act(pltpu.make_async_copy(ref.at[0, pl.ds((j - start) * rows, rows)], gx_ref.at[0], sem))
-
-            start += n
+        for h in range(per):
+            b = j * per + h
+            start = 0
+            for ref, n in zip(recv, copies):
+
+                @pl.when((b >= start) & (b < start + n))
+                def _(ref=ref, start=start, h=h, b=b):
+                    src = ref.at[0, pl.ds((b - start) * ROWS, ROWS)]
+                    act(pltpu.make_async_copy(src, gx_ref.at[0, pl.ds(h * ROWS, ROWS)], sem.at[h]))
+
+                start += n
 
     file_rows(lambda copy: copy.start())
     gw_ref[...] = pv_ref[...]
@@ -388,7 +395,8 @@
     rows = 2 * ROWS
     steps = half // rows
     early = vf.shape[0] // rows
-    copies = [t.shape[1] // rows for t in recv]
+    copies = [t.shape[1] // ROWS for t in recv]
+    filed = pl.cdiv(sum(copies) * ROWS, rows)
     row = lambda c: half_spec(rows, c, 1, 0)
     part = (1, dw_v.shape[1] // steps, cols)
     any_ = pl.BlockSpec(memory_space=pl.ANY)
@@ -405,8 +413,8 @@
             num_scalar_prefetch=1,
             grid=(steps,),
             in_specs=specs + [any_] * (len(recv) + 2),
-            out_specs=[row(width), pl.BlockSpec((1, rows, width), lambda j, off: (off[1], jnp.minimum(j, sum(copies) - 1), 0)), pl.BlockSpec(part, lambda j, off: (2, j, 0))],
-            scratch_shapes=[pltpu.VMEM((rows, cols), BF16)] * 2 + [pltpu.SemaphoreType.DMA],
+            out_specs=[row(width), pl.BlockSpec((1, rows, width), lambda j, off: (off[1], jnp.minimum(j, filed - 1), 0)), pl.BlockSpec(part, lambda j, off: (2, j, 0))],
+            scratch_shapes=[pltpu.VMEM((rows, cols), BF16)] * 2 + [pltpu.SemaphoreType.DMA((rows // ROWS,))],
         ),
         out_shape=[sds(y2.shape, y2.dtype), sds(gx2.shape, gx2.dtype), sds((3, *dw_v.shape[1:]), F32)],
         input_output_aliases={len(args) + 1: 0, len(args) + 2: 1},
@@ -471,9 +479,10 @@
         near = tuple(halves(t) for t in (q, k, v, do))
         peers = [lax.ppermute(part, "sp", [(s, s ^ d) for s in range(sp_size)]) for d in (1, 2, 3)]
         part = (part + peers[0]) + (peers[1] + peers[2])
-        part, wn_, wf_ = lax.optimization_barrier((part, w_near, w_far))
+        part, wn_, wf_, wof_ = lax.optimization_barrier((part, w_near, w_far, wo_far))
         part_far = exchange(part)
-        held = (*hold(wn_, wf_), w_out, wo_far)
+        *held, wof_ = hold(wn_, wf_, wof_)
+        held = (*held, w_out, wof_)
         vf = far_v(off, u2, w_far, EARLY_V, 0, 1)
         tau = jnp.repeat(temps, HEAD).reshape(tp_size, groups, GROUP)
         tau = jnp.where(me == 0, tau, tau[::-1]).reshape(2 * groups, GROUP)

time: 1320 us -> 1310 us (level)
    ppermute x3, waiting for transfers between devices: 470 us -> 454 us  [step(): sums = sums + lax.ppermute(sums, axis, perm)]
where the time goes in v10:
time: 1310 us; the launch traced here: 1300 us
  Pallas kernels  788 us (60%)
  waiting for transfers between devices  473 us (36%)
  starting transfers between devices  14.7 us (1%)
  between operations  14.4 us (1%)
    ppermute x3, waiting for transfers between devices, step(): sums = sums + lax.ppermute(sums, axis, perm)  454 us
    pallas_call x4, Pallas kernels, rows_call(): pl.pallas_call(functools.partial(rows_body, n_alias=len(prev), send_block...  323 us
    pallas_call x1, Pallas kernels, project(): pl.pallas_call(project_body, grid=(tokens // PROJ_ROWS,), in_specs=[row(w...  198 us
    pallas_call x2, Pallas kernels, token_sum(): pl.pallas_call(functools.partial(token_sum_body, planes=[r.shape[0] for _...  177 us
    pallas_call x1, Pallas kernels, far_y(): pl.pallas_call(functools.partial(far_y_body, early=early, copies=copies),...  76.2 us
  transfers between devices with their start and end apart: 17, of which 5 were waited for; matrix products, arithmetic and copies ran while one was open for 1% of the time, Pallas kernels for 29%

profile of v10, /device:TPU:0, one launch (start us, length us, event | category | flops | bytes accessed | tf_op | source)
XLA Modules:
  0.0 1300.4 jit_solution(993556078310066981)
XLA Ops:
  7.2 0.0 reduce-scatter.4.cloned.1.call-start
  7.2 3.4 collective-permute-start.3
  10.6 0.0 collective-permute-start.4
  10.6 198.0 %project.1 = (bf16[16384,1536]{1,0:T(8,128)(2,1)}, bf16[16384,768]{1,0:T(8,128)(2,1)}, bf16[16384,768]{1,0:T(8,128)(2,1)}, bf16[16384,768]{1,0:T(8,128)(2,1)}, b...) custom-call(bf16[16384,1536]{1,0:T(8,128)(2,1)} %x_ref.1, bf16[16384,1536]{1,0:T(8,128)(2,1)} %g_ref.1, ...), custom_call_target="tpu_custom_call" | custom-call | flops 170080698368 | bytes 251658240 | tf_op jit(solution)/shard_map/project/pallas_call | solution.py:121
  208.7 0.0 collective-permute-start
  208.7 2.0 collective-permute-start.1
  210.7 0.1 collective-permute-start.2
  210.8 0.0 copy-done.4
  210.8 0.1 broadcast_in_dim.10
  210.9 0.1 broadcast_in_dim.11
  210.9 0.1 broadcast_in_dim.12
  211.0 0.3 rev.6
  211.4 0.0 collective-permute-done
  211.4 5.5 collective-permute-done.1
  216.9 3.8 collective-permute-done.2
  220.7 1.0 add_add_fusion.near_ref
  221.7 0.0 collective-permute-done.4.refs_6_.refs_7_
  221.7 0.0 collective-permute-done.3.refs_3_.refs_4_.refs_5_.w_ref.refs_8_
  221.7 1.6 collective-permute-start.5
  223.3 0.1 pad_add_fusion.refs_0_.off_ref
  223.4 6.0 hold.1
  229.4 0.0 collective-permute-done.5.far_ref
  229.4 2.7 head_state.1
  232.1 0.0 copy-start.1
  232.1 0.0 copy-done
  232.1 33.0 %rows.4 = (bf16[2,8192,1536]{2,1,0:T(8,128)(2,1)}, bf16[2,8192,1536]{2,1,0:T(8,128)(2,1)}, bf16[2,8192,768]{2,1,0:T(8,128)(2,1)}, bf16[2,2,8192,768]{3,2,1,0:T(8...) custom-call(s32[2]{0:T(128)S(1)} %pad_add_fusion.refs_0_.off_ref, ...), custom_call_target="tpu_custom_call" | custom-call | flops 23555211264 | bytes 33030144 | tf_op jit(solution)/shard_map/rows/pallas_call | solution.py:330
  265.1 52.6 %rows.5 = (bf16[2,8192,1536]{2,1,0:T(8,128)(2,1)}, bf16[2,8192,1536]{2,1,0:T(8,128)(2,1)}, bf16[2,8192,768]{2,1,0:T(8,128)(2,1)}, bf16[2,2,8192,768]{3,2,1,0:T(8...) custom-call(s32[2]{0:T(128)S(1)} %pad_add_fusion.refs_0_.off_ref, ...), custom_call_target="tpu_custom_call", output_to_operand_aliasing={{0}: (21, {}), {1}: (22, {}), {2}: (23, {}), {3}: (24, {}),... | custom-call | flops 39258685440 | bytes 55050240 | tf_op jit(solution)/shard_map/rows/pallas_call | solution.py:330
  317.6 89.9 %rows.6 = (bf16[2,8192,1536]{2,1,0:T(8,128)(2,1)}, bf16[2,8192,1536]{2,1,0:T(8,128)(2,1)}, bf16[2,8192,768]{2,1,0:T(8,128)(2,1)}, bf16[2,2,8192,768]{3,2,1,0:T(8...) custom-call(s32[2]{0:T(128)S(1)} %pad_add_fusion.refs_0_.off_ref, ...), custom_call_target="tpu_custom_call", output_to_operand_aliasing={{0}: (21, {}), {1}: (22, {}), {2}: (23, {}), {3}: (24, {}),... | custom-call | flops 70665633792 | bytes 99090432 | tf_op jit(solution)/shard_map/rows/pallas_call | solution.py:330
  407.5 0.0 copy-done.3
  407.6 0.0 copy-done.1
  407.6 147.4 %rows.7 = (bf16[2,8192,1536]{2,1,0:T(8,128)(2,1)}, bf16[2,8192,1536]{2,1,0:T(8,128)(2,1)}, bf16[2,8192,768]{2,1,0:T(8,128)(2,1)}, bf16[2,2,8192,768]{3,2,1,0:T(8...) custom-call(s32[2]{0:T(128)S(1)} %pad_add_fusion.refs_0_.off_ref, ...), custom_call_target="tpu_custom_call", output_to_operand_aliasing={{0}: (21, {}), {1}: (22, {}), {2}: (23, {}), {3}: (24, {}),... | custom-call | flops 117776056320 | bytes 165150720 | tf_op jit(solution)/shard_map/rows/pallas_call | solution.py:330
  555.0 88.0 %token_sum.2 = (f32[1,768,1536]{2,1,0:T(8,128)}, f32[1,1536,768]{2,1,0:T(8,128)}) custom-call(bf16[16384,768]{1,0:T(8,128)(2,1)} %bitcast.60, bf16[16384,1536]{1,0:T(8,128)(2,1)} %get-tuple-element.70.refs_1_.refs_0_, bf16[1,16384,1536]{2,1,0:T(8,128)(2,1)} %bitcast.42, bf16[1,16384,768]{2,1,0:T(8,128)(2,1)} %bitcast.61), custom_call_target="tpu_custom_call" | custom-call | flops 77309411328 | bytes 150994944 | tf_op jit(solution)/shard_map/token_sum/pallas_call | solution.py:443
  643.0 0.0 reduce-scatter.4.cloned.1.call-update
  643.0 0.0 reduce-scatter.6.cloned.1.call-start
  643.0 89.1 %token_sum.3 = f32[2,1536,768]{2,1,0:T(8,128)} custom-call(bf16[16384,1536]{1,0:T(8,128)(2,1)} %get-tuple-element.70.refs_1_.refs_0_, bf16[2,16384,768]{2,1,0:T(8,128)(2,1)} %bitcast.43), custom_call_target="tpu_custom_call" | custom-call | flops 77309411328 | bytes 100663296 | tf_op jit(solution)/shard_map/token_sum/pallas_call | solution.py:443
  732.2 0.0 reduce-scatter.6.cloned.1.call-update
  732.2 0.0 reduce-scatter.8.cloned.1.call-start
  732.2 1.2 collective-permute-start.9
  733.5 0.8 collective-permute-start.8
  734.3 1.2 collective-permute-start.7
  735.5 0.0 reduce-scatter.8.cloned.1.call-update
  735.5 0.8 collective-permute-start.6
  736.4 0.1 add_reduce_fusion
  736.4 1.2 collective-permute-start.11
  737.7 452.7 %collective-permute-done.11 = f32[2,1536]{1,0:T(2,128)S(1)} collective-permute-done((f32[2,1536]{1,0:T(2,128)S(1)}, f32[2,1536]{1,0:T(2,128)S(1)}, u32[]{:S(2)}, u32[]{:S(2)}) %collective-permute-start.11) | collective-permute-done | bytes 12320 | tf_op jit(solution)/shard_map/ppermute | solution.py:516
  1190.4 0.0 collective-permute-start.12
  1190.4 5.1 far_v.1.refs_4_
  1195.5 0.1 reshape.78
  1195.6 0.1 reduce_sum.19
  1195.7 0.0 collective-permute-done.12
  1195.7 1.5 collective-permute-start.13
  1197.2 0.6 reshape.79
  1197.8 1.6 collective-permute-done.13
  1199.4 0.6 collective-permute-start.10
  1200.1 0.6 slice_reduce_fusion
  1200.7 0.0 collective-permute-done.6.refs_10_
  1200.7 0.0 collective-permute-done.7.refs_11_
  1200.7 0.0 collective-permute-done.8.refs_12_
  1200.7 0.0 collective-permute-done.9.refs_13_
  1200.7 0.0 reduce-scatter.4.cloned.1.call-done.refs_9_
  1200.8 76.2 %far_y.1 = (bf16[2,8192,1536]{2,1,0:T(8,128)(2,1)}, bf16[2,8192,1536]{2,1,0:T(8,128)(2,1)}, f32[3,384,768]{2,1,0:T(8,128)}) custom-call(s32[2]{0:T(128)} %copy-done.3, bf16[2,8192,1536]{2,1,0:T(8,128)(2,1)} %bitcast.35, bf16[2,8192,768]{2,1,0:T(8,128)(2,1)} %get-tuple-element.106.refs_2_, ...), custom_call_target="tpu_custom_call", output_to_operand_aliasing={{0}: (14, {}), {1}: (15, {})} | custom-call | flops 54116589568 | bytes 138412032 | tf_op jit(solution)/shard_map/far_y/pallas_call | solution.py:410
  1276.9 9.0 collective-permute-done.10
  1286.0 4.3 constant_dynamic-update-slice_fusion
  1290.2 3.2 constant_dynamic-update-slice_fusion.1
  (16 shorter events, 0.1 us)
Async XLA Ops:
  7.2 1193.6 %reduce-scatter.4.cloned.1.call-start = ((), (), s32[]{:S(2)}) async-start(), calls=%async_computation.3 | async-start | bytes 5898240 | tf_op jit(solution)/shard_map/reduce_scatter | solution.py:507
  7.2 214.5 %collective-permute-start.3 = (bf16[3,1536,768]{2,1,0:T(8,128)(2,1)}, bf16[3,1536,768]{2,1,0:T(8,128)(2,1)}, u32[]{:S(2)}, u32[]{:S(2)}) collective-permute-start(bf16[3,1536,768]{2,1,0:T(8,128)(2,1)} %bitcast.66), channel_id=1, source_target_pairs={{0,4},{4,0},{1,5},{5,1},{2,6},{6,2},{3,7},{7,3}} | collective-permute-start | bytes 21233672 | tf_op jit(solution)/shard_map/ppermute | solution.py:463
  10.6 211.1 %collective-permute-start.4 = (bf16[768,1536]{1,0:T(8,128)(2,1)}, bf16[768,1536]{1,0:T(8,128)(2,1)}, u32[]{:S(2)}, u32[]{:S(2)}) collective-permute-start(bf16[768,1536]{1,0:T(8,128)(2,1)} %refs_6_.1), channel_id=1, source_target_pairs={{0,4},{4,0},{1,5},{5,1},{2,6},{6,2},{3,7},{7,3}} | collective-permute-start | bytes 7077896 | tf_op jit(solution)/shard_map/ppermute | solution.py:463
  10.6 200.2 %copy-start.4 = (f32[48]{0:T(128)S(1)}, f32[48]{0:T(128)}, u32[]{:S(2)}) copy-start(f32[48]{0:T(128)} %param.13) | copy-start | bytes 580
  208.7 2.7 collective-permute-start
  208.7 8.2 collective-permute-start.1
  210.7 10.0 collective-permute-start.2
  221.7 7.7 collective-permute-start.5
  223.4 184.2 %copy-start.3 = (s32[2]{0:T(128)}, s32[2]{0:T(128)S(1)}, u32[]{:S(2)}) copy-start(s32[2]{0:T(128)S(1)} %pad_add_fusion.refs_0_.off_ref) | copy-start | bytes 28
  223.4 8.7 copy-start
  223.4 8.7 copy-start.2
  232.1 175.5 %copy-start.1 = (bf16[6,256,256]{2,1,0:T(8,128)(2,1)}, bf16[6,256,256]{2,1,0:T(8,128)(2,1)S(1)}, u32[]{:S(2)}) copy-start(bf16[6,256,256]{2,1,0:T(8,128)(2,1)S(1)} %get-tuple-element.78.refs_9_.refs_5_) | copy-start | bytes 2359300
  643.0 647.3 %reduce-scatter.6.cloned.1.call-start = ((), (), s32[]{:S(2)}) async-start(), calls=%async_computation.4 | async-start | bytes 11796480 | tf_op jit(solution)/shard_map/reduce_scatter | solution.py:510
  732.2 561.3 %reduce-scatter.8.cloned.1.call-start = ((), (), s32[]{:S(2)}) async-start(), calls=%async_computation.5 | async-start | bytes 5898240 | tf_op jit(solution)/shard_map/reduce_scatter | solution.py:506
  732.2 468.5 %collective-permute-start.9 = (bf16[1,2560,1536]{2,1,0:T(8,128)(2,1)}, bf16[1,2560,1536]{2,1,0:T(8,128)(2,1)}, u32[]{:S(2)}, u32[]{:S(2)}) collective-permute-start(bf16[1,2560,1536]{2,1,0:T(8,128)(2,1)} %get-tuple-element.117), channel_id=1, source_target_pairs={{0,4},{4,0},{1,5},{5,1},{2,6},{6,2},{3,7},{7,3}} | collective-permute-start | bytes 23592968 | tf_op jit(solution)/shard_map/ppermute | solution.py:463
  733.5 467.2 %collective-permute-start.8 = (bf16[1,2304,1536]{2,1,0:T(8,128)(2,1)}, bf16[1,2304,1536]{2,1,0:T(8,128)(2,1)}, u32[]{:S(2)}, u32[]{:S(2)}) collective-permute-start(bf16[1,2304,1536]{2,1,0:T(8,128)(2,1)} %get-tuple-element.116), channel_id=1, source_target_pairs={{0,4},{4,0},{1,5},{5,1},{2,6},{6,2},{3,7},{7,3}} | collective-permute-start | bytes 21233672 | tf_op jit(solution)/shard_map/ppermute | solution.py:463
  734.3 466.4 %collective-permute-start.7 = (bf16[1,1280,1536]{2,1,0:T(8,128)(2,1)}, bf16[1,1280,1536]{2,1,0:T(8,128)(2,1)}, u32[]{:S(2)}, u32[]{:S(2)}) collective-permute-start(bf16[1,1280,1536]{2,1,0:T(8,128)(2,1)} %get-tuple-element.115), channel_id=1, source_target_pairs={{0,4},{4,0},{1,5},{5,1},{2,6},{6,2},{3,7},{7,3}} | collective-permute-start | bytes 11796488 | tf_op jit(solution)/shard_map/ppermute | solution.py:463
  735.5 465.2 %collective-permute-start.6 = (bf16[1,768,1536]{2,1,0:T(8,128)(2,1)S(1)}, bf16[1,768,1536]{2,1,0:T(8,128)(2,1)}, u32[]{:S(2)}, u32[]{:S(2)}) collective-permute-start(bf16[1,768,1536]{2,1,0:T(8,128)(2,1)S(1)} %get-tuple-element.114), channel_id=1, source_target_pairs={{0,4},{4,0},{1,5},{5,1},{2,6},{6,2},{3,7},{7,3}} | collective-permute-start | bytes 7077896 | tf_op jit(solution)/shard_map/ppermute | solution.py:463
  736.4 454.0 %collective-permute-start.11 = (f32[2,1536]{1,0:T(2,128)S(1)}, f32[2,1536]{1,0:T(2,128)S(1)}, u32[]{:S(2)}, u32[]{:S(2)}) collective-permute-start(f32[2,1536]{1,0:T(2,128)S(1)} %add_reduce_fusion), channel_id=1, source_target_pairs={{0,4},{4,0},{1,5},{5,1},{2,6},{6,2},{3,7},{7,3}} | collective-permute-start | bytes 36872 | tf_op jit(solution)/shard_map/ppermute | solution.py:516
  1190.4 5.3 collective-permute-start.12
  1195.7 3.7 collective-permute-start.13
  1199.4 86.5 %collective-permute-start.10 = (bf16[1,1280,1536]{2,1,0:T(8,128)(2,1)}, bf16[1,1280,1536]{2,1,0:T(8,128)(2,1)}, u32[]{:S(2)}, u32[]{:S(2)}) collective-permute-start(bf16[1,1280,1536]{2,1,0:T(8,128)(2,1)} %get-tuple-element.124), channel_id=1, source_target_pairs={{0,4},{4,0},{1,5},{5,1},{2,6},{6,2},{3,7},{7,3}} | collective-permute-start | bytes 11796488 | tf_op jit(solution)/shard_map/ppermute | solution.py:463
Sparse Core Ops, SparseCore 0:
  643.1 43.0 reduce-scatter.3
  732.3 73.0 reduce-scatter.5
  808.5 42.3 reduce-scatter.7
